TPU v7x, 32 devices: a whole 2x2x4 slice. The times are simulated.
32 devices in a mesh: dp: 8 (over z, y), neg: 4 (over x, core).
Axes of the slice: x: 2, y: 2, z: 4, core: 2. Of those that a mesh axis runs over, the one named last changes fastest.
Arguments:
- query_features: bfloat16 [8192, 512], P(('dp', 'neg')), may hold values from -8 to 8
- positive_features: bfloat16 [8192, 512], P(('dp', 'neg')), may hold values from -6 to 6
- negative_features: bfloat16 [16384, 512], P(('neg', 'dp')), may hold values from -6 to 6
- positive_ids: int32 [8192], P('dp'), may hold values from 0 to 8191, as said below
- positive_counts: int32 [8192], P(('dp', 'neg')), may hold values from 1 to 16
- negative_ids: int32 [16384], P('neg'), may hold values from 0 to 4095, as said below
- negative_counts: int32 [16384], P('neg'), may hold values from 64 to 4096
- query_first: bfloat16 [512, 1024], replicated, may hold values from -0.25 to 0.25
- query_second: bfloat16 [1024, 512], replicated, may hold values from -0.1875 to 0.1875
- query_third: bfloat16 [512, 256], replicated, may hold values from -0.25 to 0.25
- item_first: bfloat16 [512, 1024], replicated, may hold values from -0.25 to 0.25
- item_second: bfloat16 [1024, 512], replicated, may hold values from -0.1875 to 0.1875
- item_third: bfloat16 [512, 256], replicated, may hold values from -0.25 to 0.25
Outputs:
- mean_loss: float32 [], replicated
- clipped_query_first: float32 [512, 1024], P('dp')
- clipped_query_second: float32 [1024, 512], P('dp')
- clipped_query_third: float32 [512, 256], P('dp')
- clipped_item_first: float32 [512, 1024], P('dp')
- clipped_item_second: float32 [1024, 512], P('dp')
- clipped_item_third: float32 [512, 256], P('dp')
Inputs may be any that keep to these rules, and one draw needn't show every extreme that they name: `negative_ids`: ids of the sampled negatives; one id may stand for several negatives. `positive_ids`: A query's positive id may equal the ids of some negatives; those negatives are left out of that query's denominator.
All inputs are finite; a program needn't handle non-finite values.
Results may differ from a plain program's by a relative error of at most 0.0075.
Values may be sent and summed in bfloat16 or wider, within the bound.
A program may use at most 128 MiB of HBM per device.

v0:
```python
import functools

import jax
import jax.numpy as jnp
from jax import lax
from jax.experimental import pallas as pl
from jax.experimental.pallas import tpu as pltpu
from jax.sharding import PartitionSpec as P

inv_temp = 20.0
clip_norm = 256.0


def silu_slope(pre):
    sigma = jax.nn.sigmoid(pre)
    return sigma * (1.0 + pre * (1.0 - sigma))


def contract_rows(left, right):
    return lax.dot_general(
        left, right, (((0,), (0,)), ((), ())), preferred_element_type=jnp.float32
    )


def contract_cols(left, right):
    return lax.dot_general(
        left, right, (((1,), (1,)), ((), ())), preferred_element_type=jnp.float32
    )


def tower_forward(features, first, second, third):
    first_pre = jnp.dot(features, first, preferred_element_type=jnp.float32)
    first_act = jax.nn.silu(first_pre).astype(jnp.bfloat16)
    second_pre = jnp.dot(first_act, second, preferred_element_type=jnp.float32)
    second_act = jax.nn.silu(second_pre).astype(jnp.bfloat16)
    embedding = jnp.dot(second_act, third, preferred_element_type=jnp.float32)
    inv_norm = lax.rsqrt(jnp.sum(embedding * embedding, axis=1, keepdims=True) + 1.0)
    unit = (embedding * inv_norm).astype(jnp.bfloat16)
    return ((first_pre, first_act, second_pre, second_act, embedding, inv_norm), unit)


def tower_backward(features, second, third, saved, unit_grad):
    first_pre, first_act, second_pre, second_act, embedding, inv_norm = saved
    along = jnp.sum(embedding * unit_grad, axis=1, keepdims=True)
    embed_grad = (inv_norm * unit_grad - inv_norm * inv_norm * inv_norm * embedding * along).astype(
        jnp.bfloat16
    )
    third_grad = contract_rows(second_act, embed_grad)
    second_slope = (contract_cols(embed_grad, third) * silu_slope(second_pre)).astype(jnp.bfloat16)
    second_grad = contract_rows(first_act, second_slope)
    first_slope = (contract_cols(second_slope, second) * silu_slope(first_pre)).astype(jnp.bfloat16)
    first_grad = contract_rows(features, first_slope)
    return (first_grad, second_grad, third_grad)


pack_columns = 256
vmem = pl.BlockSpec(memory_space=pltpu.VMEM)


def greet(ndp, nneg, me_dp, me_neg):
    barrier = pltpu.get_barrier_semaphore()
    for k in range(1, nneg):
        pl.semaphore_signal(
            barrier, inc=1, device_id={"neg": lax.rem(me_neg + k, nneg)}, device_id_type=pl.DeviceIdType.MESH
        )
    for k in range(1, ndp):
        pl.semaphore_signal(
            barrier, inc=1, device_id={"dp": lax.rem(me_dp + k, ndp)}, device_id_type=pl.DeviceIdType.MESH
        )
    pl.semaphore_wait(barrier, (nneg - 1) + (ndp - 1))


def send(src, dst, send_sem, recv_sem, axis, target):
    copy = pltpu.make_async_remote_copy(
        src_ref=src,
        dst_ref=dst,
        send_sem=send_sem,
        recv_sem=recv_sem,
        device_id={axis: target},
        device_id_type=pl.DeviceIdType.MESH,
    )
    copy.start()
    return copy


def share(axis, n, me, src_of, dst, send_sem, recv_sem):
    return [
        send(src_of(lax.rem(me + k, n)), dst.at[me], send_sem.at[k], recv_sem.at[k], axis, lax.rem(me + k, n))
        for k in range(1, n)
    ]


def finish(copies):
    for copy in copies:
        copy.wait()


def link(src, dst, sems, index, axis, target):
    send_sems, recv_sems = sems
    return pltpu.make_async_remote_copy(
        src_ref=src,
        dst_ref=dst,
        send_sem=send_sems.at[index],
        recv_sem=recv_sems.at[index],
        device_id={axis: target},
        device_id_type=pl.DeviceIdType.MESH,
    )


def gather_kernel(
    ndp, nneg, query_ref, negative_ref, group_ref, shard_ref, qs, qr, rs, rr, ls, lr, ys, yr
):
    me_dp, me_neg = lax.axis_index("dp"), lax.axis_index("neg")
    line = ndp // 2
    place = me_dp // 2
    partner = me_dp + 1 - 2 * lax.rem(me_dp, 2)
    cuts = negative_ref.shape[0]
    greet(ndp, nneg, me_dp, me_neg)
    goes_right, goes_left = place < line - 1, place > 0

    def block(slot, j, distance):
        return negative_ref.at[j] if distance == 0 else shard_ref.at[slot, j]

    def right(distance, j):
        slot = me_dp - 2 * distance
        return link(block(slot, j, distance), shard_ref.at[slot, j], (rs, rr), (distance + 1) * cuts + j, "dp", lax.rem(me_dp + 2, ndp))

    def left(distance, j):
        slot = me_dp + 2 * distance
        return link(block(slot, j, distance), shard_ref.at[slot, j], (ls, lr), (distance + 1) * cuts + j, "dp", lax.rem(me_dp + ndp - 2, ndp))

    def across(offset, j):
        slot = me_dp + 2 * offset
        return link(block(slot, j, abs(offset)), shard_ref.at[slot, j], (ys, yr), (offset + line - 1) * cuts + j, "dp", partner)

    def arrival(slot, j, sems, index):
        return link(shard_ref.at[slot, j], shard_ref.at[slot, j], sems, index, "dp", partner)

    for j in range(cuts):
        pl.when(goes_right)(lambda j=j: right(0, j).start())
        pl.when(goes_left)(lambda j=j: left(0, j).start())
        across(0, j).start()
    copies = share("neg", nneg, me_neg, lambda t: query_ref, group_ref, qs, qr)
    group_ref[me_neg] = query_ref[...]
    shard_ref[me_dp] = negative_ref[...]
    for distance in range(1, line):
        for j in range(cuts):

            @pl.when(place >= distance)
            def _():
                arrival(me_dp - 2 * distance, j, (rs, rr), distance * cuts + j).wait_recv()
                across(-distance, j).start()
                pl.when(goes_right)(lambda: right(distance, j).start())

            @pl.when(place + distance < line)
            def _():
                arrival(me_dp + 2 * distance, j, (ls, lr), distance * cuts + j).wait_recv()
                across(distance, j).start()
                pl.when(goes_left)(lambda: left(distance, j).start())

    for distance in range(line):
        for j in range(cuts):

            @pl.when(place >= distance)
            def _():
                across(-distance, j).wait_send()
                arrival(partner - 2 * distance, j, (ys, yr), (line - 1 - distance) * cuts + j).wait_recv()
                pl.when(goes_right)(lambda: right(distance, j).wait_send())

            @pl.when(place + distance < line)
            def _():
                if distance:
                    across(distance, j).wait_send()
                    arrival(partner + 2 * distance, j, (ys, yr), (line - 1 + distance) * cuts + j).wait_recv()
                pl.when(goes_left)(lambda: left(distance, j).wait_send())

    finish(copies)


def query_kernel(ndp, nneg, part_ref, denom_ref, sum_ref, total_ref, land, denom_land, qs, qr, ds, dr):
    me_dp, me_neg = lax.axis_index("dp"), lax.axis_index("neg")
    greet(1, nneg, me_dp, me_neg)
    small = share("neg", nneg, me_neg, lambda t: denom_ref, denom_land, ds, dr)
    copies = share("neg", nneg, me_neg, lambda t: part_ref.at[t], land, qs, qr)
    total = denom_ref[...]
    finish(small)
    for k in range(1, nneg):
        total = total + denom_land[lax.rem(me_neg + k, nneg)]
    total_ref[...] = total
    finish(copies)
    result = part_ref[me_neg].astype(jnp.float32)
    for k in range(1, nneg):
        result = result + land[lax.rem(me_neg + k, nneg)].astype(jnp.float32)
    sum_ref[...] = result


def negative_kernel(
    ndp, nneg, part_ref, sum_ref, pair_land, right_land, left_land, right_sum, left_sum, ys, yr, rs, rr, ls, lr
):
    me_dp, me_neg = lax.axis_index("dp"), lax.axis_index("neg")
    line = ndp // 2
    place, side = me_dp // 2, lax.rem(me_dp, 2)
    partner = me_dp + 1 - 2 * side
    cuts = part_ref.shape[1]
    greet(ndp, 1, me_dp, me_neg)
    order = sorted(range(line), key=lambda z: -abs(2 * z - line + 1))
    steps = [(z, j) for z in order for j in range(cuts)]
    from_left, from_right = place > 0, place < line - 1

    def across(z, j):
        return link(part_ref.at[2 * z + 1 - side, j], pair_land.at[z, j], (ys, yr), z * cuts + j, "dp", partner)

    def right(z, j):
        return link(right_sum.at[z, j], right_land.at[z, j], (rs, rr), z * cuts + j, "dp", lax.rem(me_dp + 2, ndp))

    def left(z, j):
        return link(left_sum.at[z, j], left_land.at[z, j], (ls, lr), z * cuts + j, "dp", lax.rem(me_dp + ndp - 2, ndp))

    for z, j in steps:
        across(z, j).start()
    for z, j in steps:
        across(z, j).wait_recv()
        own = part_ref[2 * z + side, j].astype(jnp.float32) + pair_land[z, j].astype(jnp.float32)

        @pl.when(place == z)
        def _():
            sum_ref[j] = own

        @pl.when(place == 0 if z else False)
        def _():
            right_sum[z, j] = own.astype(jnp.bfloat16)

        @pl.when((place > 0) & (place < z))
        def _():
            right(z, j).wait_recv()
            right_sum[z, j] = (own + right_land[z, j].astype(jnp.float32)).astype(jnp.bfloat16)

        pl.when(place < z)(lambda: right(z, j).start())

        @pl.when(place == line - 1 if z < line - 1 else False)
        def _():
            left_sum[z, j] = own.astype(jnp.bfloat16)

        @pl.when((place < line - 1) & (place > z))
        def _():
            left(z, j).wait_recv()
            left_sum[z, j] = (own + left_land[z, j].astype(jnp.float32)).astype(jnp.bfloat16)

        pl.when(place > z)(lambda: left(z, j).start())

    for j in range(cuts):

        @pl.when(from_left)
        def _():
            right(place, j).wait_recv()
            sum_ref[j] = sum_ref[j] + right_land[place, j].astype(jnp.float32)

        @pl.when(from_right)
        def _():
            left(place, j).wait_recv()
            sum_ref[j] = sum_ref[j] + left_land[place, j].astype(jnp.float32)

    for z, j in steps:
        across(z, j).wait_send()
        pl.when(place < z)(lambda: right(z, j).wait_send())
        pl.when(place > z)(lambda: left(z, j).wait_send())


def weight_kernel(
    ndp, nneg, packed_ref, loss_ref, gathered_ref, stats_ref,
    core_land, sum_a, sum_b, land_a, land_b, half_a, half_b, last_a, last_b, line_sum, line_land,
    stat_dp, stat_dp_land, stat_neg, stat_neg_land,
    cs, cr, xs, xr, ys, yr, ps, pr, ss, sr, ts, tr, gs, gr, hs, hr,
):
    me_dp, me_neg = lax.axis_index("dp"), lax.axis_index("neg")
    nx, line = nneg // 2, ndp // 2
    me_x, me_core = me_neg // 2, lax.rem(me_neg, 2)
    place, side = me_dp // 2, lax.rem(me_dp, 2)
    other, far = 1 - me_core, 1 - side
    mate, partner = 2 * me_x + other, 2 * place + far
    greet(ndp, nneg, me_dp, me_neg)
    turn = list(range(1, nx)) + [0]

    def x_of(k):
        return lax.rem(me_x + k, nx)

    core = {}
    for k in turn:
        x = x_of(k)
        core[k] = send(packed_ref.at[2 * x + other], core_land.at[x], cs.at[k], cr.at[k], "neg", mate)

    def add_core(x, y, half, target):
        def body(z, carry):
            target[z] = (
                packed_ref[2 * x + me_core, 2 * z + y, half].astype(jnp.float32)
                + core_land[x, 2 * z + y, half].astype(jnp.float32)
            ).astype(jnp.bfloat16)
            return carry

        lax.fori_loop(0, line, body, 0)

    def add(target, *terms):
        def body(z, carry):
            value = terms[0][z].astype(jnp.float32)
            for term in terms[1:]:
                value = value + term[z].astype(jnp.float32)
            target[z] = value.astype(jnp.bfloat16)
            return carry

        lax.fori_loop(0, line, body, 0)

    first_a = []
    for k in turn:
        x = x_of(k)
        core[k].wait_recv()
        if k:
            for y in range(2):
                add_core(x, y, 0, sum_a.at[x, y])
            first_a.append(send(sum_a.at[x], land_a.at[k], xs.at[k], xr.at[k], "neg", 2 * x + me_core))
        add_core(x, far, 1, sum_b.at[far, x])
    first_b = send(sum_b.at[far], land_b, ys.at[0], yr.at[0], "dp", partner)
    for y in range(2):
        add_core(me_x, y, 0, sum_a.at[me_x, y])
    for k in range(nx):
        add_core(x_of(k), side, 1, sum_b.at[side, x_of(k)])
    for copy in first_a:
        copy.wait_recv()
    add(half_a.at[far], sum_a.at[me_x, far], *[land_a.at[k, far] for k in range(1, nx)])
    second_a = send(half_a.at[far], last_a, ys.at[1], yr.at[1], "dp", partner)
    first_b.wait_recv()
    second_b = []
    for k in turn:
        x = x_of(k)
        add(half_b.at[x], sum_b.at[side, x], land_b.at[x])
        if k:
            second_b.append(
                send(half_b.at[x], last_b.at[k], xs.at[nx + k], xr.at[nx + k], "neg", 2 * x + me_core)
            )
    add(half_a.at[side], sum_a.at[me_x, side], *[land_a.at[k, side] for k in range(1, nx)])
    second_a.wait_recv()
    add(line_sum.at[0], half_a.at[side], last_a)
    third = []
    for half in range(2):
        if half:
            for copy in second_b:
                copy.wait_recv()
            add(line_sum.at[1], half_b.at[me_x], *[last_b.at[k] for k in range(1, nx)])
        for k in range(1, line):
            z = lax.rem(place + k, line)
            third.append(
                send(line_sum.at[half, z], line_land.at[half, k], ps.at[half * line + k], pr.at[half * line + k], "dp", 2 * z + side)
            )
    for copy in third:
        copy.wait_recv()
    squares = jnp.zeros((), jnp.float32)
    for half in range(2):
        piece = line_sum[half, place].astype(jnp.float32)
        for k in range(1, line):
            piece = piece + line_land[half, k].astype(jnp.float32)
        gathered_ref[me_neg, half] = piece.astype(jnp.bfloat16)
        squares = squares + jnp.sum(piece * piece)
    lane = lax.broadcasted_iota(jnp.int32, (8, 128), 1)
    stat_dp[...] = jnp.where(lane == 0, squares, loss_ref[0])
    stat_copies = share("dp", ndp, me_dp, lambda t: stat_dp, stat_dp_land, ss, sr)
    mine = gathered_ref.at[me_neg]
    spread = [send(mine, mine, gs.at[k], gr.at[k], "neg", 2 * x_of(k) + me_core) for k in range(1, nx)]
    spread.append(send(mine, mine, gs.at[0], gr.at[0], "neg", mate))
    finish(stat_copies)
    total = stat_dp[...]
    for k in range(1, ndp):
        total = total + stat_dp_land[lax.rem(me_dp + k, ndp)]
    stat_neg[...] = total
    stat_copies = share("neg", nneg, me_neg, lambda t: stat_neg, stat_neg_land, ts, tr)
    relay = []
    for k in range(1, nx):
        spread[k - 1].wait_recv()
        x = lax.rem(me_x + nx - k, nx)
        came = gathered_ref.at[2 * x + me_core]
        relay.append(send(came, came, hs.at[k], hr.at[k], "neg", mate))
    finish(stat_copies)
    total = stat_neg[...]
    for k in range(1, nneg):
        total = total + stat_neg_land[lax.rem(me_neg + k, nneg)]
    stats_ref[...] = total
    spread[-1].wait_recv()
    finish(relay)
    for copy in [*core.values(), *first_a, first_b, second_a, *second_b, *third, *spread]:
        copy.wait_send()


def call(kernel, collective, ndp, nneg, out_shape, scratch, in_specs):
    return pl.pallas_call(
        functools.partial(kernel, ndp, nneg),
        out_shape=out_shape,
        in_specs=in_specs,
        out_specs=tuple(vmem for _ in out_shape),
        scratch_shapes=scratch,
        compiler_params=pltpu.CompilerParams(
            collective_id=collective, has_side_effects=True, vmem_limit_bytes=48 * 1024 * 1024
        ),
    )


def sems(*counts):
    return [pltpu.SemaphoreType.DMA((count,)) for count in counts]


def to_packed(gradient, ndp):
    rows, columns = gradient.shape
    blocks = gradient.astype(jnp.bfloat16).reshape(ndp, rows // ndp, columns)
    return [blocks[:, :, c : c + pack_columns] for c in range(0, columns, pack_columns)]


def per_device(
    query_features,
    positive_features,
    negative_features,
    positive_ids,
    positive_counts,
    negative_ids,
    negative_counts,
    query_first,
    query_second,
    query_third,
    item_first,
    item_second,
    item_third,
):
    own_rows = query_features.shape[0]
    query_saved, query_unit = tower_forward(query_features, query_first, query_second, query_third)
    item_features = jnp.concatenate([positive_features, negative_features], axis=0)
    item_saved, item_unit = tower_forward(item_features, item_first, item_second, item_third)
    positive_unit = item_unit[:own_rows]
    negative_unit = item_unit[own_rows:]
    ndp, nneg = lax.axis_size("dp"), lax.axis_size("neg")
    width = query_unit.shape[1]
    cuts = 4
    cut_rows = negative_unit.shape[0] // cuts
    group_unit, shard_unit = call(
        gather_kernel,
        0,
        ndp,
        nneg,
        (
            jax.ShapeDtypeStruct((nneg,) + query_unit.shape, jnp.bfloat16),
            jax.ShapeDtypeStruct((ndp, cuts, cut_rows, width), jnp.bfloat16),
        ),
        sems(nneg, nneg, *([ndp // 2 * cuts + cuts] * 4), *([ndp * cuts] * 2)),
        [vmem, vmem],
    )(query_unit, negative_unit.reshape(cuts, cut_rows, width))
    group_unit = group_unit.reshape(-1, width)
    shard_unit = shard_unit.reshape(-1, width)
    scores = (
        contract_cols(group_unit, shard_unit) * inv_temp
        - jnp.log(negative_counts.astype(jnp.float32))[None, :]
    )
    weights = jnp.where(positive_ids[:, None] != negative_ids[None, :], jnp.exp(scores), 0.0)
    positive_logit = jnp.sum(
        query_unit.astype(jnp.float32) * positive_unit.astype(jnp.float32), axis=1
    ) * inv_temp - jnp.log(positive_counts.astype(jnp.float32))
    positive_exp = jnp.exp(positive_logit)
    offset = lax.axis_index("neg") * own_rows
    partial_value = jnp.sum(weights, axis=1)
    own_part = lax.dynamic_slice(partial_value, (offset,), (own_rows,)) + positive_exp
    partial_value = lax.dynamic_update_slice(partial_value, own_part, (offset,))
    block = weights.astype(jnp.bfloat16)
    query_part = jnp.dot(block, shard_unit, preferred_element_type=jnp.float32).astype(jnp.bfloat16)
    denom_shape = (nneg * own_rows // 128, 128)
    query_total, denom = call(
        query_kernel,
        1,
        ndp,
        nneg,
        (
            jax.ShapeDtypeStruct((own_rows, width), jnp.float32),
            jax.ShapeDtypeStruct(denom_shape, jnp.float32),
        ),
        [
            pltpu.VMEM((nneg, own_rows, width), jnp.bfloat16),
            pltpu.VMEM((nneg,) + denom_shape, jnp.float32),
        ]
        + sems(nneg, nneg, nneg, nneg),
        [vmem, vmem],
    )(query_part.reshape(nneg, own_rows, width), partial_value.reshape(denom_shape))
    denom = denom.reshape(-1)
    own_denom = lax.dynamic_slice(denom, (offset,), (own_rows,))
    loss_part = jnp.sum(jnp.log(own_denom) - positive_logit)
    positive_slope = positive_exp / own_denom - 1.0
    query_sum = query_total / own_denom[:, None]
    scaled_unit = (group_unit.astype(jnp.float32) / denom[:, None]).astype(jnp.bfloat16)
    negative_part = contract_rows(block, scaled_unit).astype(jnp.bfloat16)
    line = ndp // 2
    cut = (cuts, cut_rows, width)
    (negative_sum,) = call(
        negative_kernel,
        2,
        ndp,
        nneg,
        (jax.ShapeDtypeStruct(cut, jnp.float32),),
        [pltpu.VMEM((line,) + cut, jnp.bfloat16)] * 5 + sems(*([line * cuts] * 6)),
        [vmem],
    )(negative_part.reshape((ndp,) + cut))
    negative_sum = negative_sum.reshape(negative_unit.shape)
    query_grad = (
        query_sum + positive_slope[:, None] * positive_unit.astype(jnp.float32)
    ) * inv_temp
    positive_grad = positive_slope[:, None] * query_unit.astype(jnp.float32) * inv_temp
    item_grad = jnp.concatenate([positive_grad, negative_sum * inv_temp], axis=0)
    query_grads = tower_backward(query_features, query_second, query_third, query_saved, query_grad)
    item_grads = tower_backward(item_features, item_second, item_third, item_saved, item_grad)
    gradients = query_grads + item_grads
    parts = [part for gradient in gradients for part in to_packed(gradient, ndp)]
    packed = jnp.concatenate(parts, axis=1)
    rows = packed.shape[1] // nneg
    packed = packed.reshape(ndp, nneg, 2, rows // 2, pack_columns).transpose(1, 0, 2, 3, 4)
    nx = nneg // 2
    piece = (rows // 2, pack_columns)
    bf16, f32 = jnp.bfloat16, jnp.float32
    gathered, stats = call(
        weight_kernel,
        3,
        ndp,
        nneg,
        (jax.ShapeDtypeStruct((nneg, 2) + piece, bf16), jax.ShapeDtypeStruct((8, 128), f32)),
        [
            pltpu.VMEM((nx, ndp, 2) + piece, bf16),
            pltpu.VMEM((nx, 2, line) + piece, bf16),
            pltpu.VMEM((2, nx, line) + piece, bf16),
            pltpu.VMEM((nx, 2, line) + piece, bf16),
            pltpu.VMEM((nx, line) + piece, bf16),
            pltpu.VMEM((2, line) + piece, bf16),
            pltpu.VMEM((nx, line) + piece, bf16),
            pltpu.VMEM((line,) + piece, bf16),
            pltpu.VMEM((nx, line) + piece, bf16),
            pltpu.VMEM((2, line) + piece, bf16),
            pltpu.VMEM((2, line) + piece, bf16),
            pltpu.VMEM((8, 128), f32),
            pltpu.VMEM((ndp, 8, 128), f32),
            pltpu.VMEM((8, 128), f32),
            pltpu.VMEM((nneg, 8, 128), f32),
        ]
        + sems(nx, nx, 2 * nx, 2 * nx, 2, 2, ndp, ndp, ndp, ndp, nneg, nneg, nx, nx, nx, nx),
        [vmem, pl.BlockSpec(memory_space=pltpu.SMEM)],
    )(packed, loss_part.reshape(1))
    grad_norm = jnp.sqrt(stats[0, 0])
    mean_loss = stats[0, 1] / (own_rows * ndp * nneg)
    clip_factor = clip_norm / jnp.maximum(grad_norm, clip_norm)
    flat = gathered.reshape(nneg * rows, pack_columns)
    clipped = []
    start = 0
    for gradient in gradients:
        height, columns = gradient.shape[0] // ndp, gradient.shape[1]
        groups = columns // pack_columns
        blocks = [flat[start + g * height : start + (g + 1) * height] for g in range(groups)]
        start += groups * height
        clipped.append(jnp.concatenate(blocks, axis=1).astype(jnp.float32) * clip_factor)
    return (mean_loss, *clipped)


def solution(mesh):
    placed = (
        P(("dp", "neg"), None),
        P(("dp", "neg"), None),
        P(("neg", "dp"), None),
        P("dp"),
        P(("dp", "neg")),
        P("neg"),
        P("neg"),
        P(),
        P(),
        P(),
        P(),
        P(),
        P(),
    )
    return jax.shard_map(
        per_device,
        mesh=mesh,
        in_specs=placed,
        out_specs=(
            P(),
            P("dp", None),
            P("dp", None),
            P("dp", None),
            P("dp", None),
            P("dp", None),
            P("dp", None),
        ),
        check_vma=False,
    )
```

profile of v0, /device:TPU:0, one launch (start us, length us, event | category | flops | bytes accessed | tf_op | source)
XLA Modules:
  0.0 176.3 jit_solution(3404385544018689303)
XLA Ops:
  0.6 0.0 copy-start
  0.6 1.1 constant_dynamic-update-slice_fusion.1
  1.7 1.1 constant_dynamic-update-slice_fusion
  2.8 0.0 copy-start.28
  2.8 2.9 %multiply_convert_fusion.1 = (bf16[768,1024]{1,0:T(8,128)(2,1)S(1)}, f32[768,1024]{1,0:T(8,128)}) fusion(bf16[768,512]{1,0:T(8,128)(2,1)S(1)} %constant_dynamic-update-slice_fusion, bf16[512,1024]{1,0:T(8,128)(2,1)S(1)} %copy-done), kind=kOutput, calls=%fused_computation.6 | convolution fusion | flops 809238528 | bytes 6553600 | tf_op jit(solution)/shard_map/dot_general | solution.py:32
  5.7 0.0 copy-done.19
  5.7 2.3 %multiply_convert_fusion.3 = (bf16[768,512]{1,0:T(8,128)(2,1)S(1)}, f32[768,512]{1,0:T(8,128)}) fusion(bf16[768,1024]{1,0:T(8,128)(2,1)S(1)} %get-tuple-element.50, bf16[1024,512]{1,0:T(8,128)(2,1)S(1)} %copy-done.28), kind=kOutput, calls=%fused_computation.9 | convolution fusion | flops 807272448 | bytes 4980736 | tf_op jit(solution)/shard_map/dot_general | solution.py:34
  8.0 0.0 copy-start.29
  8.0 0.0 copy-done.13
  8.0 0.4 multiply_reduce_fusion.1
  8.5 0.4 copy-done.9
  8.9 0.2 multiply_convert_fusion.5
  9.1 0.4 copy-done.3
  9.5 0.0 copy-done.15
  9.5 0.4 fusion.19
  10.0 0.0 copy-start.17
  10.0 0.0 copy-start.21
  10.0 0.0 copy-start.30
  10.0 0.0 copy-start.31
  10.1 1.3 multiply_convert_fusion.6
  11.3 0.0 copy-done.4
  11.3 0.3 multiply_reduce_fusion.3
  11.6 0.4 copy-done.7
  12.0 0.1 copy.23
  12.2 0.6 broadcast_multiply_fusion.1
  12.8 0.2 fusion.11
  13.0 30.9 %shard_map.180 = (bf16[4,256,256]{2,1,0:T(8,128)(2,1)S(1)}, bf16[8,4,128,256]{3,2,1,0:T(8,128)(2,1)S(1)}) custom-call(bf16[256,256]{1,0:T(8,128)(2,1)S(1)} %get-tuple-element.22.query_ref, bf16[4,128,256]{2,1,0:T(8,128)(2,1)S(1)} %bitcast.59), custom_call_target="tpu_custom_call" | custom-call | tf_op jit(solution)/shard_map/pallas_call | solution.py:439
  43.9 5.1 %fusion = (f32[1024]{0:T(1024)S(1)}, bf16[1024,4096]{1,0:T(8,128)(2,1)S(1)}) fusion(f32[4096]{0:T(1024)S(1)} %convert_log_fusion, s32[4096]{0:T(1024)S(1)} %copy-done.30, s32[1024]{0:T(1024)S(1)} %copy-done.31, bf16[1024,256]{1,0:T(8,128)(2,1)S(1)} %bitcast.69, bf16[4096,256]{1,0:T(8,128)(2,1)S(1)} %bitcast.67), kind=kOutput, calls=%fused_computation.1 | convolution fusion | flops 2172648448 | bytes 11051008 | tf_op jit(solution)/shard_map/dot_general | solution.py:26
  49.0 0.0 copy-start.24
  49.0 2.3 %convolution_convert_fusion.5 = bf16[1024,256]{1,0:T(8,128)(2,1)S(1)} fusion(bf16[1024,4096]{1,0:T(8,128)(2,1)S(1)} %get-tuple-element.24, bf16[4096,256]{1,0:T(8,128)(2,1)S(1)} %bitcast.68), kind=kOutput, calls=%fused_computation.16 | convolution fusion | flops 2147745792 | bytes 11010048 | tf_op jit(solution)/shard_map/dot_general | solution.py:467
  51.4 0.9 copy-done.32
  52.3 0.2 add_dynamic-update-slice_fusion
  52.5 8.0 %shard_map.181 = (f32[256,256]{1,0:T(8,128)S(1)}, f32[8,128]{1,0:T(8,128)S(1)}) custom-call(bf16[4,256,256]{2,1,0:T(8,128)(2,1)S(1)} %bitcast.63, f32[8,128]{1,0:T(8,128)S(1)} %bitcast.64), custom_call_target="tpu_custom_call" | custom-call | tf_op jit(solution)/shard_map/pallas_call | solution.py:469
  60.6 5.9 %convolution_convert_fusion = bf16[4096,256]{1,0:T(8,128)(2,1)S(1)} fusion(bf16[1024,4096]{1,0:T(8,128)(2,1)} %copy-done.32, bf16[1024,256]{1,0:T(8,128)(2,1)S(1)} %bitcast.70, f32[1024]{0:T(1024)S(1)} %bitcast.65), kind=kOutput, calls=%fused_computation.3 | convolution fusion | flops 2149318656 | bytes 11014144 | tf_op jit(solution)/shard_map/dot_general | solution.py:20
  66.5 0.0 copy-start.25
  66.6 29.1 %shard_map.182 = f32[4,128,256]{2,1,0:T(8,128)S(1)} custom-call(bf16[8,4,128,256]{3,2,1,0:T(8,128)(2,1)S(1)} %bitcast.58), custom_call_target="tpu_custom_call" | custom-call | tf_op jit(solution)/shard_map/pallas_call | solution.py:494
  95.7 0.0 copy-start.14
  95.8 0.7 subtract_reduce_fusion
  96.5 0.2 fusion.10
  96.7 0.2 multiply_reduce_fusion
  96.9 0.4 subtract_convert_fusion
  97.3 1.6 multiply_convert_fusion.2
  98.9 0.0 copy-start.26
  99.0 0.0 copy-start.27
  99.0 0.0 copy-start.18
  99.0 5.5 %convolution_convert_fusion.2 = bf16[512,1024]{1,0:T(8,128)(2,1)} fusion(bf16[768,512]{1,0:T(8,128)(2,1)S(1)} %copy-done.20, f32[768,1024]{1,0:T(8,128)} %get-tuple-element.51, bf16[768,512]{1,0:T(8,128)(2,1)} %multiply_convert_fusion.2, bf16[1024,512]{1,0:T(8,128)(2,1)} %param.24), kind=kOutput, calls=%fused_computation.12 | convolution fusion | flops 1618214912 | bytes 6815744 | tf_op jit(solution)/shard_map/dot_general | solution.py:20
  104.5 0.2 subtract_convert_fusion.1
  104.8 2.1 %fusion.3 = bf16[256,512]{1,0:T(8,128)(2,1)} fusion(bf16[256,256]{1,0:T(8,128)(2,1)S(1)} %subtract_convert_fusion.1, bf16[512,256]{1,0:T(8,128)(2,1)S(1)} %copy-done.18, f32[256,512]{1,0:T(8,128)} %get-tuple-element.49), kind=kOutput, calls=%fused_computation.21 | convolution fusion | flops 68288512 | bytes 1179648 | tf_op jit(solution)/shard_map/dot_general | solution.py:26
  106.9 2.6 %convolution_convert_fusion.4 = bf16[1024,512]{0,1:T(8,128)(2,1)S(1)} fusion(bf16[256,512]{1,0:T(8,128)(2,1)S(1)} %copy-done.16, bf16[256,512]{1,0:T(8,128)(2,1)} %fusion.3, bf16[1024,512]{1,0:T(8,128)(2,1)} %param.21, f32[256,1024]{1,0:T(8,128)} %copy-done.4), kind=kOutput, calls=%fused_computation.14 | convolution fusion | flops 539754496 | bytes 3670016 | tf_op jit(solution)/shard_map/dot_general | solution.py:20
  109.7 0.0 copy-start.8
  109.7 1.6 convolution_convert_fusion.3
  111.4 0.3 convolution_convert_fusion.7
  111.9 0.8 copy-done.34
  112.7 0.2 copy-done.35
  112.9 1.0 convolution_convert_fusion.1
  114.0 0.0 copy-done.10
  114.0 0.1 copy-done.12
  114.1 0.4 convolution_convert_fusion.6
  114.5 0.3 copy.28
  114.8 55.8 %shard_map.183 = (bf16[4,2,144,256]{3,2,1,0:T(8,128)(2,1)S(1)}, f32[8,128]{1,0:T(8,128)S(1)}) custom-call(bf16[4,8,2,144,256]{4,3,2,1,0:T(8,128)(2,1)S(1)} %bitcast.57, f32[1]{0:T(128)} %bitcast.18.loss_ref), custom_call_target="tpu_custom_call" | custom-call | tf_op jit(solution)/shard_map/pallas_call | solution.py:519
  170.7 0.6 fusion.18
  172.1 0.7 convert_multiply_fusion.7
  172.7 0.9 convert_multiply_fusion.3
  173.6 0.8 convert_multiply_fusion.4
  (69 shorter events, 0.7 us)
Async XLA Ops:
  0.6 2.2 %copy-start = (bf16[512,1024]{1,0:T(8,128)(2,1)S(1)}, bf16[512,1024]{1,0:T(8,128)(2,1)}, u32[]{:S(2)}) copy-start(bf16[512,1024]{1,0:T(8,128)(2,1)} %param.23) | copy-start | bytes 3145732
  2.8 2.9 %copy-start.19 = (bf16[768,512]{1,0:T(8,128)(2,1)}, bf16[768,512]{1,0:T(8,128)(2,1)S(1)}, u32[]{:S(2)}) copy-start(bf16[768,512]{1,0:T(8,128)(2,1)S(1)} %constant_dynamic-update-slice_fusion) | copy-start | bytes 2359300
  2.8 2.9 %copy-start.28 = (bf16[1024,512]{1,0:T(8,128)(2,1)S(1)}, bf16[1024,512]{1,0:T(8,128)(2,1)}, u32[]{:S(2)}) copy-start(bf16[1024,512]{1,0:T(8,128)(2,1)} %param.24) | copy-start | bytes 3145732
  5.7 2.3 %copy-start.33 = (bf16[768,1024]{1,0:T(8,128)(2,1)}, bf16[768,1024]{1,0:T(8,128)(2,1)S(1)}, u32[]{:S(2)}) copy-start(bf16[768,1024]{1,0:T(8,128)(2,1)S(1)} %get-tuple-element.50) | copy-start | bytes 4718596
  5.7 2.3 %copy-start.13 = (bf16[512,256]{1,0:T(8,128)(2,1)S(1)}, bf16[512,256]{1,0:T(8,128)(2,1)}, u32[]{:S(2)}) copy-start(bf16[512,256]{1,0:T(8,128)(2,1)} %param.25) | copy-start | bytes 786436
  8.0 0.9 copy-start.9
  8.0 1.5 copy-start.3
  8.0 1.5 copy-start.15
  8.0 2.0 %copy-start.29 = (bf16[1024,512]{1,0:T(8,128)(2,1)S(1)}, bf16[1024,512]{1,0:T(8,128)(2,1)}, u32[]{:S(2)}) copy-start(bf16[1024,512]{1,0:T(8,128)(2,1)} %param.21) | copy-start | bytes 3145732
  9.5 3.4 %copy-start.1 = (bf16[768,256]{1,0:T(8,128)(2,1)}, bf16[768,256]{1,0:T(8,128)(2,1)S(1)}, u32[]{:S(2)}) copy-start(bf16[768,256]{1,0:T(8,128)(2,1)S(1)} %multiply_convert_fusion.5) | copy-start | bytes 1179652
  10.0 1.3 copy-start.4
  10.0 1.3 copy-start.17
  10.0 33.8 %copy-start.21 = (s32[4096]{0:T(1024)S(1)}, s32[4096]{0:T(1024)}, u32[]{:S(2)}) copy-start(s32[4096]{0:T(1024)} %param.19) | copy-start | bytes 49156
  10.0 33.9 %copy-start.30 = (s32[4096]{0:T(1024)S(1)}, s32[4096]{0:T(1024)}, u32[]{:S(2)}) copy-start(s32[4096]{0:T(1024)} %param.18) | copy-start | bytes 49156
  10.0 33.9 %copy-start.31 = (s32[1024]{0:T(1024)S(1)}, s32[1024]{0:T(1024)}, u32[]{:S(2)}) copy-start(s32[1024]{0:T(1024)} %param.16) | copy-start | bytes 12292
  11.3 0.7 copy-start.7
  49.0 3.3 %copy-start.32 = (bf16[1024,4096]{1,0:T(8,128)(2,1)}, bf16[1024,4096]{1,0:T(8,128)(2,1)S(1)}, u32[]{:S(2)}) copy-start(bf16[1024,4096]{1,0:T(8,128)(2,1)S(1)} %get-tuple-element.24) | copy-start | bytes 25165828
  49.0 3.3 %copy-start.24 = (s32[256]{0:T(256)S(1)}, s32[256]{0:T(256)}, u32[]{:S(2)}) copy-start(s32[256]{0:T(256)} %param.17) | copy-start | bytes 3076
  66.5 29.2 %copy-start.25 = (s32[256]{0:T(256)S(1)}, s32[256]{0:T(256)}, u32[]{:S(2)}) copy-start(s32[256]{0:T(256)} %param.17) | copy-start | bytes 3076
  66.5 29.9 %copy-start.2 = (bf16[768,256]{1,0:T(8,128)(2,1)S(1)}, bf16[768,256]{1,0:T(8,128)(2,1)}, u32[]{:S(2)}) copy-start(bf16[768,256]{1,0:T(8,128)(2,1)} %copy-done.1) | copy-start | bytes 1179652
  95.7 1.6 copy-start.14
  95.7 1.6 copy-start.36
  96.4 2.5 %copy-start.22 = (f32[256]{0:T(256)}, f32[256]{0:T(256)S(1)}, u32[]{:S(2)}) copy-start(f32[256]{0:T(256)S(1)} %divide_add_fusion) | copy-start | bytes 3076
  97.3 1.7 copy-start.11
  97.3 1.6 copy-start.20
  98.9 5.6 %copy-start.23 = (f32[256]{0:T(256)S(1)}, f32[256]{0:T(256)}, u32[]{:S(2)}) copy-start(f32[256]{0:T(256)} %copy-done.22) | copy-start | bytes 3076
  98.9 5.6 %copy-start.26 = (f32[256]{0:T(256)S(1)}, f32[256]{0:T(256)}, u32[]{:S(2)}) copy-start(f32[256]{0:T(256)} %get-tuple-element.45) | copy-start | bytes 3076
  99.0 5.6 %copy-start.27 = (f32[256]{0:T(256)S(1)}, f32[256]{0:T(256)}, u32[]{:S(2)}) copy-start(f32[256]{0:T(256)} %get-tuple-element.46) | copy-start | bytes 3076
  99.0 5.8 %copy-start.18 = (bf16[512,256]{1,0:T(8,128)(2,1)S(1)}, bf16[512,256]{1,0:T(8,128)(2,1)}, u32[]{:S(2)}) copy-start(bf16[512,256]{1,0:T(8,128)(2,1)} %param.22) | copy-start | bytes 786436
  104.5 2.3 %copy-start.16 = (bf16[256,512]{1,0:T(8,128)(2,1)S(1)}, bf16[256,512]{1,0:T(8,128)(2,1)}, u32[]{:S(2)}) copy-start(bf16[256,512]{1,0:T(8,128)(2,1)} %param.13) | copy-start | bytes 786436
  106.8 2.8 %copy-start.5 = (f32[256,1024]{1,0:T(8,128)S(1)}, f32[256,1024]{1,0:T(8,128)}, u32[]{:S(2)}) copy-start(f32[256,1024]{1,0:T(8,128)} %copy-done.4) | copy-start | bytes 3145732
  109.7 1.7 copy-start.8
  109.7 2.0 %copy-start.6 = (bf16[512,1024]{1,0:T(8,128)(2,1)S(1)}, bf16[512,1024]{1,0:T(8,128)(2,1)}, u32[]{:S(2)}) copy-start(bf16[512,1024]{1,0:T(8,128)(2,1)} %convolution_convert_fusion.2) | copy-start | bytes 3145732
  111.2 1.4 copy-start.34
  111.3 1.6 copy-start.35
  112.9 1.1 copy-start.10
  112.9 1.2 copy-start.12
where the time goes:
time: 177 us; the launch traced here: 176 us
  Pallas kernels  124 us (70%)
  matrix products  36 us (20%)
  local copies, waits for them, and re-layouts  7.26 us (4%)
  other arithmetic  5.3 us (3%)
  between operations  3.82 us (2%)
    pallas_call x1, Pallas kernels, per_device(): call(weight_kernel, 3, ndp, nneg, (jax.ShapeDtypeStruct((nneg, 2) + piece...  55.8 us
    pallas_call x1, Pallas kernels, per_device(): call(gather_kernel, 0, ndp, nneg, (jax.ShapeDtypeStruct((nneg,) + query_u...  30.9 us
    pallas_call x1, Pallas kernels, per_device(): call(negative_kernel, 2, ndp, nneg, (jax.ShapeDtypeStruct(cut, jnp.float3...  29.1 us
    dot_general x7, matrix products, contract_rows(): lax.dot_general(left, right, (((0,), (0,)), ((), ())), preferred_element_...  17.3 us
    dot_general x3, matrix products, contract_cols(): lax.dot_general(left, right, (((1,), (1,)), ((), ())), preferred_element_...  8.77 us
    pallas_call x1, Pallas kernels, per_device(): call(query_kernel, 1, ndp, nneg, (jax.ShapeDtypeStruct((own_rows, width),...  8.04 us
    unnamed x88, local copies, waits for them, and re-layouts  5.03 us
    dot_general x2, matrix products, tower_forward(): second_pre = jnp.dot(first_act, second, preferred_element_type=jnp.float32)  3.55 us

commit v1 on v0

--- a/solution.py
+++ b/solution.py
@@ -95,175 +95,343 @@
         copy.wait()
 
 
-def link(src, dst, sems, index, axis, target):
+def link(src, dst, sems, index, axis, target, send_index=None):
     send_sems, recv_sems = sems
     return pltpu.make_async_remote_copy(
         src_ref=src,
         dst_ref=dst,
-        send_sem=send_sems.at[index],
+        send_sem=send_sems.at[index if send_index is None else send_index],
         recv_sem=recv_sems.at[index],
         device_id={axis: target},
         device_id_type=pl.DeviceIdType.MESH,
     )
 
 
-def gather_kernel(
-    ndp, nneg, query_ref, negative_ref, group_ref, shard_ref, qs, qr, rs, rr, ls, lr, ys, yr
+def score_kernel(
+    ndp, nneg, query_ref, negative_ref, pid_ref, nid_ref, count_ref, pexp_ref, sum_ref, denom_ref, nsum_ref,
+    q_land, n_land, meta_out, meta, rows, pid_out, pid_land, pid_col, w, den, dpart, dland, scaled,
+    q_out, q_part, q_in, c_out, c_in, own, out, lx, ly, l2y, l2x,
+    sx, sy, rn, sm, rm, sr, sl, rq, s_meta, r_meta, s_pid, r_pid, sd, rd, sq, rqs,
+    sc, rc, s1x, r1x, s1y, r1y, s2y, r2y, s2x, r2x,
 ):
     me_dp, me_neg = lax.axis_index("dp"), lax.axis_index("neg")
-    line = ndp // 2
-    place = me_dp // 2
-    partner = me_dp + 1 - 2 * lax.rem(me_dp, 2)
-    cuts = negative_ref.shape[0]
-    greet(ndp, nneg, me_dp, me_neg)
+    line, nx = ndp // 2, nneg // 2
+    place, side = me_dp // 2, lax.rem(me_dp, 2)
+    me_x, me_core = me_neg // 2, lax.rem(me_neg, 2)
+    far, other = 1 - side, 1 - me_core
+    partner, mate = 2 * place + far, 2 * me_x + other
+    rows_q, width = query_ref.shape
+    block = 2 * negative_ref.shape[1]
+    lanes = den.shape[2]
+    cuts = q_land.shape[1]
+    half_w = width // 2
+    blocks = nneg * 2
+    here = (me_x * 2 + side) * 2 + me_core
+
+    def along(k):
+        return lax.rem(me_x + k, nx)
+
+    def at_place(z):
+        return 2 * z + side
+
+    barrier = pltpu.get_barrier_semaphore()
+    for k in range(1, line):
+        pl.semaphore_signal(
+            barrier, inc=1, device_id={"dp": at_place(lax.rem(place + k, line))}, device_id_type=pl.DeviceIdType.MESH
+        )
+
+    def quad(k):
+        b = lax.rem(here + k, blocks)
+        return {"dp": 2 * place + lax.rem(b // 2, 2), "neg": 2 * (b // 4) + lax.rem(b, 2)}
+
+    for k in range(1, blocks):
+        pl.semaphore_signal(barrier, inc=1, device_id=quad(k), device_id_type=pl.DeviceIdType.MESH)
+    meta_out[0:1, :] = nid_ref[pl.ds(me_dp, 1), :]
+    meta_out[1:2, :] = count_ref[pl.ds(me_dp, 1), :]
+    pid_out[...] = pid_ref[pl.ds(me_neg, 1), :]
+    pl.semaphore_wait(barrier, (line - 1) + (blocks - 1))
+
+    def slot(x, y, half):
+        return (x * 2 + y) * 2 + half
+
+    def piece(x, y, half):
+        return n_land.at[(x * 2 + y) * 2 + me_core, half]
+
+    def push(src, x, y, half, send_sems, index, axis, target):
+        return link(src, piece(x, y, half), (send_sems, rn), slot(x, y, half), axis, target, index)
+
+    def relay(src, x, y, half):
+        i = slot(x, y, half)
+        return link(src, piece(x, y, half), (sm, rm), i, "neg", mate)
+
+    def landed(x, y, half):
+        ref = piece(x, y, half)
+        link(ref, ref, (sy, rn), slot(x, y, half), "neg", mate, 0).wait_recv()
+
+    sends = []
+
+    def go(copy):
+        copy.start()
+        sends.append(copy)
+
+    def to_x(src, x, y, half, kind):
+        for k in range(1, nx):
+            go(push(src, x, y, half, sx, kind * nx + k, "neg", 2 * along(k) + me_core))
+
+    def to_y(src, x, y, half, index):
+        go(push(src, x, y, half, sy, index, "dp", partner))
+
+    first, second = negative_ref.at[0], negative_ref.at[1]
+    to_x(first, me_x, side, 0, 0)
+    to_y(second, me_x, side, 1, 0)
+    to_x(second, me_x, side, 1, 1)
+    to_y(first, me_x, side, 0, 1)
+    go(relay(first, me_x, side, 0))
+    go(relay(second, me_x, side, 1))
+
+    def chain(slot_z, j, distance, sems, target):
+        src = query_ref.at[pl.ds(j * (rows_q // cuts), rows_q // cuts)] if distance == 0 else q_land.at[slot_z, j]
+        return link(src, q_land.at[slot_z, j], (sems, rq), slot_z * cuts + j, "dp", target, distance * cuts + j)
+
+    def right(distance, j):
+        return chain(place - distance, j, distance, sr, at_place(lax.rem(place + 1, line)))
+
+    def left(distance, j):
+        return chain(place + distance, j, distance, sl, at_place(lax.rem(place + line - 1, line)))
+
     goes_right, goes_left = place < line - 1, place > 0
-
-    def block(slot, j, distance):
-        return negative_ref.at[j] if distance == 0 else shard_ref.at[slot, j]
-
-    def right(distance, j):
-        slot = me_dp - 2 * distance
-        return link(block(slot, j, distance), shard_ref.at[slot, j], (rs, rr), (distance + 1) * cuts + j, "dp", lax.rem(me_dp + 2, ndp))
-
-    def left(distance, j):
-        slot = me_dp + 2 * distance
-        return link(block(slot, j, distance), shard_ref.at[slot, j], (ls, lr), (distance + 1) * cuts + j, "dp", lax.rem(me_dp + ndp - 2, ndp))
-
-    def across(offset, j):
-        slot = me_dp + 2 * offset
-        return link(block(slot, j, abs(offset)), shard_ref.at[slot, j], (ys, yr), (offset + line - 1) * cuts + j, "dp", partner)
-
-    def arrival(slot, j, sems, index):
-        return link(shard_ref.at[slot, j], shard_ref.at[slot, j], sems, index, "dp", partner)
-
     for j in range(cuts):
         pl.when(goes_right)(lambda j=j: right(0, j).start())
         pl.when(goes_left)(lambda j=j: left(0, j).start())
-        across(0, j).start()
-    copies = share("neg", nneg, me_neg, lambda t: query_ref, group_ref, qs, qr)
-    group_ref[me_neg] = query_ref[...]
-    shard_ref[me_dp] = negative_ref[...]
-    for distance in range(1, line):
+    for k in range(1, blocks):
+        b = lax.rem(here + k, blocks)
+        copy = pltpu.make_async_remote_copy(
+            src_ref=meta_out, dst_ref=meta.at[here], send_sem=s_meta.at[k], recv_sem=r_meta.at[here],
+            device_id=quad(k), device_id_type=pl.DeviceIdType.MESH,
+        )
+        go(copy)
+    for k in range(1, line):
+        z = lax.rem(place + k, line)
+        go(link(pid_out, pid_land.at[place], (s_pid, r_pid), place, "dp", at_place(z), k))
+    n_land[here] = negative_ref[...]
+    for j in range(cuts):
+        q_land[place, j] = query_ref[pl.ds(j * (rows_q // cuts), rows_q // cuts), :]
+    meta[here] = meta_out[...]
+    pid_land[place] = pid_out[...]
+
+    for k in range(1, nx):
+        x = along(k)
+        landed(x, side, 0)
+        to_y(piece(x, side, 0), x, side, 0, 1 + k)
+        go(relay(piece(x, side, 0), x, side, 0))
+    landed(me_x, far, 1)
+    to_x(piece(me_x, far, 1), me_x, far, 1, 2)
+    go(relay(piece(me_x, far, 1), me_x, far, 1))
+
+    def q_step(distance):
         for j in range(cuts):
 
             @pl.when(place >= distance)
             def _():
-                arrival(me_dp - 2 * distance, j, (rs, rr), distance * cuts + j).wait_recv()
-                across(-distance, j).start()
+                ref = q_land.at[place - distance, j]
+                link(ref, ref, (sr, rq), (place - distance) * cuts + j, "dp", partner, 0).wait_recv()
                 pl.when(goes_right)(lambda: right(distance, j).start())
 
             @pl.when(place + distance < line)
             def _():
-                arrival(me_dp + 2 * distance, j, (ls, lr), distance * cuts + j).wait_recv()
-                across(distance, j).start()
+                ref = q_land.at[place + distance, j]
+                link(ref, ref, (sl, rq), (place + distance) * cuts + j, "dp", partner, 0).wait_recv()
                 pl.when(goes_left)(lambda: left(distance, j).start())
 
+    q_step(1)
+    for k in range(1, nx):
+        x = along(k)
+        landed(x, side, 1)
+        go(relay(piece(x, side, 1), x, side, 1))
+    landed(me_x, far, 0)
+    go(relay(piece(me_x, far, 0), me_x, far, 0))
+    for distance in range(2, line):
+        q_step(distance)
+    for half in range(2):
+        for k in range(1, nx):
+            x = along(k)
+            landed(x, far, half)
+            go(relay(piece(x, far, half), x, far, half))
+    for x in range(nx):
+        for y in range(2):
+            for half in range(2):
+                i = slot(x, y, half)
+                ref = n_land.at[(x * 2 + y) * 2 + other, half]
+                link(ref, ref, (sm, rm), i, "neg", mate).wait_recv()
+    for k in range(1, blocks):
+        b = lax.rem(here + k, blocks)
+        link(meta.at[b], meta.at[b], (s_meta, r_meta), b, "neg", mate).wait_recv()
+    for k in range(1, line):
+        z = lax.rem(place + k, line)
+        link(pid_land.at[z], pid_land.at[z], (s_pid, r_pid), z, "dp", partner).wait_recv()
+
+    for b in range(blocks):
+        rows[b, 0:1, :] = meta[b, 0:1, :].astype(jnp.float32)
+        rows[b, 1:2, :] = jnp.log(meta[b, 1:2, :].astype(jnp.float32))
+    for z in range(line):
+        pid_col[z] = jnp.broadcast_to(pid_land[z].astype(jnp.float32), (lanes, rows_q)).T
+        den[z] = jnp.zeros((rows_q, lanes), jnp.float32)
+
+    def unit(i, carry):
+        b, z = i // line, lax.rem(i, line)
+        dots = contract_cols(q_land[z].reshape(rows_q, width), n_land[b].reshape(block, width))
+        value = jnp.exp(dots * inv_temp - rows[b, 1:2, :])
+        ids = jnp.concatenate([pid_col[z]] * (block // lanes), axis=1)
+        value = jnp.where(ids != rows[b, 0:1, :], value, 0.0)
+        w[b, z] = value.astype(jnp.bfloat16)
+        total = den[z]
+        for c in range(0, block, lanes):
+            total = total + value[:, c : c + lanes]
+        den[z] = total
+        return carry
+
+    lax.fori_loop(0, blocks * line, unit, 0)
+    for z in range(line):
+        dpart[z] = jnp.sum(den[z].T, axis=0, keepdims=True)
+    dpart[place] = dpart[place] + pexp_ref[...]
+    for k in range(1, line):
+        z = lax.rem(place + k, line)
+        go(link(dpart, dland.at[place], (sd, rd), place, "dp", at_place(z), k))
+
+    def q_block(z):
+        if block % 128 == 0:
+            left_side = jnp.concatenate([w[b, z] for b in range(blocks)], axis=1)
+            return jnp.dot(
+                left_side, n_land[...].reshape(blocks * block, width), preferred_element_type=jnp.float32
+            )
+        total = jnp.zeros((rows_q, width), jnp.float32)
+        for b in range(blocks):
+            total = total + jnp.dot(w[b, z], n_land[b].reshape(block, width), preferred_element_type=jnp.float32)
+        return total
+
+    def q_send(k, z):
+        return link(q_out.at[z], q_in.at[place], (sq, rqs), place, "dp", at_place(z), k)
+
+    def q_push(k, carry):
+        z = lax.rem(place + k, line)
+        q_out[z] = q_block(z).astype(jnp.bfloat16)
+        q_send(k, z).start()
+        return carry
+
+    lax.fori_loop(1, line, q_push, 0)
+    q_part[...] = q_block(place)
+    total = dpart[...]
+    for k in range(1, line):
+        z = lax.rem(place + k, line)
+        link(dland.at[z], dland.at[z], (sd, rd), z, "dp", partner).wait_recv()
+        total = total + dland[z]
+    dpart2 = 1.0 / total
+    for z in range(line):
+        q_t = q_land[z].reshape(rows_q, width).astype(jnp.float32).T
+        scaled[:, z * rows_q : (z + 1) * rows_q] = (q_t * dpart2[z]).astype(jnp.bfloat16)
+    denom_ref[...] = dpart[place]
+    for k in range(1, line):
+        denom_ref[...] = denom_ref[...] + dland[lax.rem(place + k, line), place]
+
+    def dest(i):
+        x = lax.rem(me_x + 1 + i // 2, nx)
+        y = lax.rem(side + 1 + lax.rem(i, 2), 2)
+        return x, y
+
+    def part(x, y, core):
+        return jnp.dot(
+            scaled[...], w[(x * 2 + y) * 2 + core].reshape(line * rows_q, block), preferred_element_type=jnp.float32
+        )
+
+    def c_send(i):
+        x, y = dest(i)
+        return link(c_out.at[x, y], c_in.at[x, y], (sc, rc), x * 2 + y, "neg", mate)
+
+    def far_step(i, carry):
+        x, y = dest(i)
+        c_out[x, y] = part(x, y, other).astype(jnp.bfloat16).reshape(2, half_w, block)
+        c_send(i).start()
+        return carry
+
+    def send_1x(i):
+        x, y = dest(i)
+        return link(out.at[x, y, 0], lx.at[me_x, y], (s1x, r1x), me_x * 2 + y, "neg", 2 * x + me_core, x * 2 + y)
+
+    def send_1y(i):
+        x, y = dest(i)
+        return link(out.at[x, y, 1], ly.at[x], (s1y, r1y), x, "dp", partner)
+
+    def own_step(i, carry):
+        x, y = dest(i)
+        value = part(x, y, me_core).reshape(2, half_w, block)
+        link(c_in.at[x, y], c_in.at[x, y], (sc, rc), x * 2 + y, "neg", mate).wait_recv()
+        value = value + c_in[x, y].astype(jnp.float32)
+        own[x, y] = value
+
+        @pl.when(i < 2 * (nx - 1))
+        def _():
+            out[x, y, 0] = value[0].astype(jnp.bfloat16)
+            send_1x(i).start()
+
+        @pl.when(lax.rem(i, 2) == 0)
+        def _():
+            out[x, y, 1] = value[1].astype(jnp.bfloat16)
+            send_1y(i).start()
+
+        return carry
+
+    lax.fori_loop(0, 2 * nx, far_step, 0)
+    lax.fori_loop(0, 2 * nx, own_step, 0)
+    value = own[me_x, far, 0]
+    for k in range(1, nx):
+        x = along(k)
+        ref = lx.at[x, far]
+        link(ref, ref, (s1x, r1x), x * 2 + far, "neg", mate).wait_recv()
+        value = value + lx[x, far].astype(jnp.float32)
+    out[me_x, far, 0] = value.astype(jnp.bfloat16)
+    go(link(out.at[me_x, far, 0], l2y, (s2y, r2y), 0, "dp", partner))
+    for k in range(1, nx):
+        x = along(k)
+        link(ly.at[x], ly.at[x], (s1y, r1y), x, "dp", partner).wait_recv()
+        out[x, side, 1] = (own[x, side, 1] + ly[x].astype(jnp.float32)).astype(jnp.bfloat16)
+        go(link(out.at[x, side, 1], l2x.at[me_x], (s2x, r2x), me_x, "neg", 2 * x + me_core, x))
+    result = q_part[...]
+    for k in range(1, line):
+        z = lax.rem(place + k, line)
+        link(q_in.at[z], q_in.at[z], (sq, rqs), z, "dp", partner).wait_recv()
+        result = result + q_in[z].astype(jnp.float32)
+    sum_ref[...] = result
+    low = own[me_x, side, 0]
+    for k in range(1, nx):
+        x = along(k)
+        ref = lx.at[x, side]
+        link(ref, ref, (s1x, r1x), x * 2 + side, "neg", mate).wait_recv()
+        low = low + lx[x, side].astype(jnp.float32)
+    link(ly.at[me_x], ly.at[me_x], (s1y, r1y), me_x, "dp", partner).wait_recv()
+    high = own[me_x, side, 1] + ly[me_x].astype(jnp.float32)
+    link(l2y, l2y, (s2y, r2y), 0, "dp", partner).wait_recv()
+    nsum_ref[0] = low + l2y[...].astype(jnp.float32)
+    for k in range(1, nx):
+        x = along(k)
+        link(l2x.at[x], l2x.at[x], (s2x, r2x), x, "neg", mate).wait_recv()
+        high = high + l2x[x].astype(jnp.float32)
+    nsum_ref[1] = high
+
+    for copy in sends:
+        copy.wait_send()
     for distance in range(line):
         for j in range(cuts):
-
-            @pl.when(place >= distance)
-            def _():
-                across(-distance, j).wait_send()
-                arrival(partner - 2 * distance, j, (ys, yr), (line - 1 - distance) * cuts + j).wait_recv()
-                pl.when(goes_right)(lambda: right(distance, j).wait_send())
-
-            @pl.when(place + distance < line)
-            def _():
-                if distance:
-                    across(distance, j).wait_send()
-                    arrival(partner + 2 * distance, j, (ys, yr), (line - 1 + distance) * cuts + j).wait_recv()
-                pl.when(goes_left)(lambda: left(distance, j).wait_send())
-
-    finish(copies)
-
-
-def query_kernel(ndp, nneg, part_ref, denom_ref, sum_ref, total_ref, land, denom_land, qs, qr, ds, dr):
-    me_dp, me_neg = lax.axis_index("dp"), lax.axis_index("neg")
-    greet(1, nneg, me_dp, me_neg)
-    small = share("neg", nneg, me_neg, lambda t: denom_ref, denom_land, ds, dr)
-    copies = share("neg", nneg, me_neg, lambda t: part_ref.at[t], land, qs, qr)
-    total = denom_ref[...]
-    finish(small)
-    for k in range(1, nneg):
-        total = total + denom_land[lax.rem(me_neg + k, nneg)]
-    total_ref[...] = total
-    finish(copies)
-    result = part_ref[me_neg].astype(jnp.float32)
-    for k in range(1, nneg):
-        result = result + land[lax.rem(me_neg + k, nneg)].astype(jnp.float32)
-    sum_ref[...] = result
-
-
-def negative_kernel(
-    ndp, nneg, part_ref, sum_ref, pair_land, right_land, left_land, right_sum, left_sum, ys, yr, rs, rr, ls, lr
-):
-    me_dp, me_neg = lax.axis_index("dp"), lax.axis_index("neg")
-    line = ndp // 2
-    place, side = me_dp // 2, lax.rem(me_dp, 2)
-    partner = me_dp + 1 - 2 * side
-    cuts = part_ref.shape[1]
-    greet(ndp, 1, me_dp, me_neg)
-    order = sorted(range(line), key=lambda z: -abs(2 * z - line + 1))
-    steps = [(z, j) for z in order for j in range(cuts)]
-    from_left, from_right = place > 0, place < line - 1
-
-    def across(z, j):
-        return link(part_ref.at[2 * z + 1 - side, j], pair_land.at[z, j], (ys, yr), z * cuts + j, "dp", partner)
-
-    def right(z, j):
-        return link(right_sum.at[z, j], right_land.at[z, j], (rs, rr), z * cuts + j, "dp", lax.rem(me_dp + 2, ndp))
-
-    def left(z, j):
-        return link(left_sum.at[z, j], left_land.at[z, j], (ls, lr), z * cuts + j, "dp", lax.rem(me_dp + ndp - 2, ndp))
-
-    for z, j in steps:
-        across(z, j).start()
-    for z, j in steps:
-        across(z, j).wait_recv()
-        own = part_ref[2 * z + side, j].astype(jnp.float32) + pair_land[z, j].astype(jnp.float32)
-
-        @pl.when(place == z)
-        def _():
-            sum_ref[j] = own
-
-        @pl.when(place == 0 if z else False)
-        def _():
-            right_sum[z, j] = own.astype(jnp.bfloat16)
-
-        @pl.when((place > 0) & (place < z))
-        def _():
-            right(z, j).wait_recv()
-            right_sum[z, j] = (own + right_land[z, j].astype(jnp.float32)).astype(jnp.bfloat16)
-
-        pl.when(place < z)(lambda: right(z, j).start())
-
-        @pl.when(place == line - 1 if z < line - 1 else False)
-        def _():
-            left_sum[z, j] = own.astype(jnp.bfloat16)
-
-        @pl.when((place < line - 1) & (place > z))
-        def _():
-            left(z, j).wait_recv()
-            left_sum[z, j] = (own + left_land[z, j].astype(jnp.float32)).astype(jnp.bfloat16)
-
-        pl.when(place > z)(lambda: left(z, j).start())
-
-    for j in range(cuts):
-
-        @pl.when(from_left)
-        def _():
-            right(place, j).wait_recv()
-            sum_ref[j] = sum_ref[j] + right_land[place, j].astype(jnp.float32)
-
-        @pl.when(from_right)
-        def _():
-            left(place, j).wait_recv()
-            sum_ref[j] = sum_ref[j] + left_land[place, j].astype(jnp.float32)
-
-    for z, j in steps:
-        across(z, j).wait_send()
-        pl.when(place < z)(lambda: right(z, j).wait_send())
-        pl.when(place > z)(lambda: left(z, j).wait_send())
+            if distance < line - 1:
+                pl.when((place >= distance) & goes_right)(lambda: right(distance, j).wait_send())
+                pl.when((place + distance < line) & goes_left)(lambda: left(distance, j).wait_send())
+    for k in range(1, line):
+        q_send(k, lax.rem(place + k, line)).wait_send()
+    for i in range(2 * nx):
+        c_send(i).wait_send()
+        if i < 2 * (nx - 1):
+            send_1x(i).wait_send()
+        if i % 2 == 0:
+            send_1y(i).wait_send()
 
 
 def weight_kernel(
@@ -434,73 +602,70 @@
     negative_unit = item_unit[own_rows:]
     ndp, nneg = lax.axis_size("dp"), lax.axis_size("neg")
     width = query_unit.shape[1]
-    cuts = 4
-    cut_rows = negative_unit.shape[0] // cuts
-    group_unit, shard_unit = call(
-        gather_kernel,
+    line, nx = ndp // 2, nneg // 2
+    block = negative_unit.shape[0]
+    blocks, cuts, lanes = 2 * nneg, 2, min(block, 128)
+    bf16, f32, i32 = jnp.bfloat16, jnp.float32, jnp.int32
+    positive_logit = jnp.sum(
+        query_unit.astype(f32) * positive_unit.astype(f32), axis=1
+    ) * inv_temp - jnp.log(positive_counts.astype(f32))
+    positive_exp = jnp.exp(positive_logit)
+    rows_half = (width // 2, block)
+    query_total, denom, negative_sum = call(
+        score_kernel,
         0,
         ndp,
         nneg,
         (
-            jax.ShapeDtypeStruct((nneg,) + query_unit.shape, jnp.bfloat16),
-            jax.ShapeDtypeStruct((ndp, cuts, cut_rows, width), jnp.bfloat16),
-        ),
-        sems(nneg, nneg, *([ndp // 2 * cuts + cuts] * 4), *([ndp * cuts] * 2)),
-        [vmem, vmem],
-    )(query_unit, negative_unit.reshape(cuts, cut_rows, width))
-    group_unit = group_unit.reshape(-1, width)
-    shard_unit = shard_unit.reshape(-1, width)
-    scores = (
-        contract_cols(group_unit, shard_unit) * inv_temp
-        - jnp.log(negative_counts.astype(jnp.float32))[None, :]
-    )
-    weights = jnp.where(positive_ids[:, None] != negative_ids[None, :], jnp.exp(scores), 0.0)
-    positive_logit = jnp.sum(
-        query_unit.astype(jnp.float32) * positive_unit.astype(jnp.float32), axis=1
-    ) * inv_temp - jnp.log(positive_counts.astype(jnp.float32))
-    positive_exp = jnp.exp(positive_logit)
-    offset = lax.axis_index("neg") * own_rows
-    partial_value = jnp.sum(weights, axis=1)
-    own_part = lax.dynamic_slice(partial_value, (offset,), (own_rows,)) + positive_exp
-    partial_value = lax.dynamic_update_slice(partial_value, own_part, (offset,))
-    block = weights.astype(jnp.bfloat16)
-    query_part = jnp.dot(block, shard_unit, preferred_element_type=jnp.float32).astype(jnp.bfloat16)
-    denom_shape = (nneg * own_rows // 128, 128)
-    query_total, denom = call(
-        query_kernel,
-        1,
-        ndp,
-        nneg,
-        (
-            jax.ShapeDtypeStruct((own_rows, width), jnp.float32),
-            jax.ShapeDtypeStruct(denom_shape, jnp.float32),
+            jax.ShapeDtypeStruct((own_rows, width), f32),
+            jax.ShapeDtypeStruct((1, own_rows), f32),
+            jax.ShapeDtypeStruct((2,) + rows_half, f32),
         ),
         [
-            pltpu.VMEM((nneg, own_rows, width), jnp.bfloat16),
-            pltpu.VMEM((nneg,) + denom_shape, jnp.float32),
+            pltpu.VMEM((line, cuts, own_rows // cuts, width), bf16),
+            pltpu.VMEM((blocks, 2, block // 2, width), bf16),
+            pltpu.VMEM((2, block), i32),
+            pltpu.VMEM((blocks, 2, block), i32),
+            pltpu.VMEM((blocks, 2, block), f32),
+            pltpu.VMEM((1, own_rows), i32),
+            pltpu.VMEM((line, 1, own_rows), i32),
+            pltpu.VMEM((line, own_rows, lanes), f32),
+            pltpu.VMEM((blocks, line, own_rows, block), bf16),
+            pltpu.VMEM((line, own_rows, lanes), f32),
+            pltpu.VMEM((line, 1, own_rows), f32),
+            pltpu.VMEM((line, line, 1, own_rows), f32),
+            pltpu.VMEM((width, line * own_rows), bf16),
+            pltpu.VMEM((line, own_rows, width), bf16),
+            pltpu.VMEM((own_rows, width), f32),
+            pltpu.VMEM((line, own_rows, width), bf16),
+            pltpu.VMEM((nx, 2, 2) + rows_half, bf16),
+            pltpu.VMEM((nx, 2, 2) + rows_half, bf16),
+            pltpu.VMEM((nx, 2, 2) + rows_half, f32),
+            pltpu.VMEM((nx, 2, 2) + rows_half, bf16),
+            pltpu.VMEM((nx, 2) + rows_half, bf16),
+            pltpu.VMEM((nx,) + rows_half, bf16),
+            pltpu.VMEM(rows_half, bf16),
+            pltpu.VMEM((nx,) + rows_half, bf16),
         ]
-        + sems(nneg, nneg, nneg, nneg),
-        [vmem, vmem],
-    )(query_part.reshape(nneg, own_rows, width), partial_value.reshape(denom_shape))
-    denom = denom.reshape(-1)
-    own_denom = lax.dynamic_slice(denom, (offset,), (own_rows,))
+        + sems(
+            3 * nx, 1 + nx, 4 * nx, 4 * nx, 4 * nx, line * cuts, line * cuts, line * cuts,
+            blocks, blocks, line, line, line, line, line, line,
+            2 * nx, 2 * nx, 2 * nx, 2 * nx, nx, nx, 1, 1, nx, nx,
+        ),
+        [vmem] * 6,
+    )(
+        query_unit,
+        negative_unit.reshape(2, block // 2, width),
+        positive_ids.reshape(nneg, own_rows),
+        negative_ids.reshape(ndp, block),
+        negative_counts.reshape(ndp, block),
+        positive_exp.reshape(1, own_rows),
+    )
+    own_denom = denom.reshape(-1)
     loss_part = jnp.sum(jnp.log(own_denom) - positive_logit)
     positive_slope = positive_exp / own_denom - 1.0
     query_sum = query_total / own_denom[:, None]
-    scaled_unit = (group_unit.astype(jnp.float32) / denom[:, None]).astype(jnp.bfloat16)
-    negative_part = contract_rows(block, scaled_unit).astype(jnp.bfloat16)
-    line = ndp // 2
-    cut = (cuts, cut_rows, width)
-    (negative_sum,) = call(
-        negative_kernel,
-        2,
-        ndp,
-        nneg,
-        (jax.ShapeDtypeStruct(cut, jnp.float32),),
-        [pltpu.VMEM((line,) + cut, jnp.bfloat16)] * 5 + sems(*([line * cuts] * 6)),
-        [vmem],
-    )(negative_part.reshape((ndp,) + cut))
-    negative_sum = negative_sum.reshape(negative_unit.shape)
+    negative_sum = negative_sum.reshape(width, block).T
     query_grad = (
         query_sum + positive_slope[:, None] * positive_unit.astype(jnp.float32)
     ) * inv_temp
@@ -513,9 +678,7 @@
     packed = jnp.concatenate(parts, axis=1)
     rows = packed.shape[1] // nneg
     packed = packed.reshape(ndp, nneg, 2, rows // 2, pack_columns).transpose(1, 0, 2, 3, 4)
-    nx = nneg // 2
     piece = (rows // 2, pack_columns)
-    bf16, f32 = jnp.bfloat16, jnp.float32
     gathered, stats = call(
         weight_kernel,
         3,

time: 177 us -> 146 us (0.82)
  Pallas kernels: 124 us -> 97.8 us
  matrix products: 36 us -> 26.9 us
  local copies, waits for them, and re-layouts: 7.26 us -> 12.6 us
    pallas_call x3 -> x1, Pallas kernels: 68 us -> 47.7 us  [per_device(): call(score_kernel, 0, ndp, nneg, (jax.ShapeDtypeStruct((own_rows, width),...]
    dot_general x3 -> x2, matrix products: 8.77 us -> 2.62 us  [contract_cols(): lax.dot_general(left, right, (((1,), (1,)), ((), ())), preferred_element_...]
    pallas_call x1, Pallas kernels: 55.8 us -> 50.1 us  [per_device(): call(weight_kernel, 3, ndp, nneg, (jax.ShapeDtypeStruct((nneg, 2) + piece...]
    unnamed x88 -> x58, local copies, waits for them, and re-layouts: 5.03 us -> 7.89 us
    dot_general x1 -> x0, matrix products: 2.33 us -> none  [per_device(): jnp.dot(block, shard_unit, preferred_element_type=jnp.float32)]
    reshape x0 -> x3, local copies, waits for them, and re-layouts: none -> 2.28 us  [the longest x1 0.84 us: per_device(): positive_ids.reshape(nneg, own_rows)]
    dot_general x7 -> x6, matrix products: 17.3 us -> 15.1 us  [contract_rows(): lax.dot_general(left, right, (((0,), (0,)), ((), ())), preferred_element_...]
where the time goes in v1:
time: 146 us; the launch traced here: 145 us
  Pallas kernels  97.8 us (67%)
  matrix products  26.9 us (18%)
  local copies, waits for them, and re-layouts  12.6 us (9%)
  other arithmetic  4.44 us (3%)
  between operations  3.53 us (2%)
    pallas_call x1, Pallas kernels, per_device(): call(weight_kernel, 3, ndp, nneg, (jax.ShapeDtypeStruct((nneg, 2) + piece...  50.1 us
    pallas_call x1, Pallas kernels, per_device(): call(score_kernel, 0, ndp, nneg, (jax.ShapeDtypeStruct((own_rows, width),...  47.7 us
    dot_general x6, matrix products, contract_rows(): lax.dot_general(left, right, (((0,), (0,)), ((), ())), preferred_element_...  15.1 us
    unnamed x58, local copies, waits for them, and re-layouts  7.89 us
    dot_general x2, matrix products, tower_forward(): first_pre = jnp.dot(features, first, preferred_element_type=jnp.float32)  4.93 us
    dot_general x2, matrix products, tower_forward(): second_pre = jnp.dot(first_act, second, preferred_element_type=jnp.float32)  3.59 us

profile of v1, /device:TPU:0, one launch (start us, length us, event | category | flops | bytes accessed | tf_op | source)
XLA Modules:
  0.0 145.3 jit_solution(14954915076860368843)
XLA Ops:
  0.6 0.0 copy-start
  0.6 0.0 copy-start.17
  0.7 0.8 reshape.96.pid_ref
  1.5 0.7 reshape.97.nid_ref
  2.2 0.7 reshape.98.count_ref
  2.9 1.0 constant_dynamic-update-slice_fusion.1
  3.9 1.1 constant_dynamic-update-slice_fusion
  5.0 0.0 copy-start.13
  5.0 2.0 %fusion.17 = f32[256,1024]{1,0:T(8,128)S(1)} fusion(bf16[256,512]{1,0:T(8,128)(2,1)} %param.13, bf16[512,1024]{1,0:T(8,128)(2,1)} %param.20), kind=kOutput, calls=%fused_computation.79 | convolution fusion | flops 268435456 | bytes 2359296 | tf_op jit(solution)/shard_map/dot_general | solution.py:32
  7.0 0.0 copy-done.17
  7.0 0.0 copy-start.1
  7.1 0.0 copy-start.11
  7.1 1.3 multiply_convert_fusion.6
  8.4 0.0 copy-done.1
  8.4 0.0 copy-done.11
  8.4 0.3 multiply_reduce_fusion.3
  8.7 0.1 copy.24
  8.8 0.0 copy-done.13
  8.8 0.0 copy-done
  8.8 0.0 copy-start.16
  8.8 2.9 %multiply_convert_fusion.1 = (bf16[768,1024]{1,0:T(8,128)(2,1)S(1)}, f32[768,1024]{1,0:T(8,128)}) fusion(bf16[768,512]{1,0:T(8,128)(2,1)S(1)} %constant_dynamic-update-slice_fusion, bf16[512,1024]{1,0:T(8,128)(2,1)S(1)} %copy-done), kind=kOutput, calls=%fused_computation.2 | convolution fusion | flops 809238528 | bytes 6553600 | tf_op jit(solution)/shard_map/dot_general | solution.py:32
  11.7 0.0 copy-done.16
  11.8 2.3 %multiply_convert_fusion.3 = (bf16[768,512]{1,0:T(8,128)(2,1)S(1)}, f32[768,512]{1,0:T(8,128)}) fusion(bf16[768,1024]{1,0:T(8,128)(2,1)S(1)} %get-tuple-element.46, bf16[1024,512]{1,0:T(8,128)(2,1)S(1)} %copy-done.16), kind=kOutput, calls=%fused_computation.5 | convolution fusion | flops 807272448 | bytes 4980736 | tf_op jit(solution)/shard_map/dot_general | solution.py:34
  14.1 0.0 copy-done.18
  14.1 0.0 copy-done.8
  14.1 0.0 copy-start.19
  14.1 0.4 multiply_reduce_fusion.1
  14.5 0.2 multiply_convert_fusion.5
  14.7 0.2 fusion.8
  14.9 0.0 copy-done.6
  15.0 47.7 %shard_map.180 = (f32[256,256]{1,0:T(8,128)S(1)}, f32[1,256]{1,0:T(1,128)S(1)}, f32[2,128,512]{2,1,0:T(8,128)S(1)}) custom-call(bf16[256,256]{1,0:T(8,128)(2,1)S(1)} %get-tuple-element.18.query_ref, bf16[2,256,256]{2,1,0:T(8,128)(2,1)S(1)} %bitcast.50, s32[4,256]{1,0:T(4,128)S(1)} %reshape.96.pid_ref, s32[8,512]{1,0:T(8,128)S(1)} %reshape.97.nid_ref, ...), custom_call_target="tpu_custom_call" | custom-call | tf_op jit(solution)/shard_map/pallas_call | solution.py:614
  62.7 0.6 subtract_reduce_fusion
  63.3 0.2 fusion.7
  63.6 0.2 subtract_convert_fusion.1
  63.8 0.0 copy-done.19
  63.8 1.0 fusion.1
  64.8 1.0 convolution_convert_fusion.5
  65.9 0.2 copy.29
  66.1 0.0 copy-start.21
  66.1 0.2 multiply_reduce_fusion
  66.3 0.4 subtract_convert_fusion
  66.7 0.8 copy-done.21
  67.5 1.6 %multiply_convert_fusion.2 = bf16[768,512]{1,0:T(8,128)(2,1)} fusion(f32[768,512]{1,0:T(8,128)S(1)} %copy-done.21, bf16[768,256]{1,0:T(8,128)(2,1)S(1)} %subtract_convert_fusion, bf16[512,256]{1,0:T(8,128)(2,1)S(1)} %copy-done.9), kind=kOutput, calls=%fused_computation.4 | convolution fusion | flops 204865536 | bytes 3014656 | tf_op jit(solution)/shard_map/dot_general | solution.py:26
  69.1 0.0 copy-done.14
  69.1 5.5 %convolution_convert_fusion.1 = bf16[512,1024]{1,0:T(8,128)(2,1)} fusion(bf16[768,512]{1,0:T(8,128)(2,1)S(1)} %copy-done.14, f32[768,1024]{1,0:T(8,128)} %get-tuple-element.47, bf16[768,512]{1,0:T(8,128)(2,1)} %multiply_convert_fusion.2, bf16[1024,512]{1,0:T(8,128)(2,1)} %param.24), kind=kOutput, calls=%fused_computation.8 | convolution fusion | flops 1618214912 | bytes 6815744 | tf_op jit(solution)/shard_map/dot_general | solution.py:20
  74.6 2.8 %convolution_convert_fusion = bf16[1024,512]{1,0:T(8,128)(2,1)S(1)} fusion(bf16[768,1024]{1,0:T(8,128)(2,1)} %copy-done.18, bf16[768,512]{1,0:T(8,128)(2,1)} %multiply_convert_fusion.2), kind=kOutput, calls=%fused_computation.7 | convolution fusion | flops 805830656 | bytes 3407872 | tf_op jit(solution)/shard_map/dot_general | solution.py:20
  77.4 1.1 convolution_convert_fusion.4
  78.5 1.5 %convolution_convert_fusion.2 = bf16[1024,512]{1,0:T(8,128)(2,1)} fusion(bf16[256,512]{1,0:T(8,128)(2,1)S(1)} %copy-done.20, f32[256,1024]{1,0:T(8,128)S(1)} %copy-done.2), kind=kOutput, calls=%fused_computation.9 | convolution fusion | flops 270270464 | bytes 2359296 | tf_op jit(solution)/shard_map/dot_general | solution.py:20
  80.0 0.0 copy-done.10
  80.0 3.2 %convolution_convert_fusion.3 = bf16[1024,512]{0,1:T(8,128)(2,1)} fusion(bf16[256,512]{1,0:T(8,128)(2,1)S(1)} %copy-done.10, bf16[256,512]{1,0:T(8,128)(2,1)} %fusion.1, bf16[1024,512]{1,0:T(8,128)(2,1)} %param.21, f32[256,1024]{1,0:T(8,128)S(1)} %copy-done.2), kind=kOutput, calls=%fused_computation.10 | convolution fusion | flops 539754496 | bytes 3670016 | tf_op jit(solution)/shard_map/dot_general | solution.py:20
  83.2 1.1 slice_dynamic-update-slice_fusion.11
  84.3 1.0 slice_dynamic-update-slice_fusion.10
  85.3 1.0 slice_dynamic-update-slice_fusion.9
  86.3 1.0 slice_dynamic-update-slice_fusion.8
  87.3 1.1 slice_dynamic-update-slice_fusion.3
  88.3 0.0 copy-done.4
  88.3 0.0 copy-start.12
  88.7 0.6 copy-done.12
  89.3 0.3 copy.31
  89.7 50.1 %shard_map.181 = (bf16[4,2,144,256]{3,2,1,0:T(8,128)(2,1)S(1)}, f32[8,128]{1,0:T(8,128)S(1)}) custom-call(bf16[4,8,2,144,256]{4,3,2,1,0:T(8,128)(2,1)S(1)} %bitcast.49, f32[1]{0:T(128)} %bitcast.15.loss_ref), custom_call_target="tpu_custom_call" | custom-call | tf_op jit(solution)/shard_map/pallas_call | solution.py:682
  139.7 0.6 fusion.16
  141.7 0.7 convert_multiply_fusion.7
  142.4 0.8 convert_multiply_fusion.4
  143.3 0.9 convert_multiply_fusion.3
  (36 shorter events, 0.4 us)
Async XLA Ops:
  0.6 8.2 %copy-start = (bf16[512,1024]{1,0:T(8,128)(2,1)S(1)}, bf16[512,1024]{1,0:T(8,128)(2,1)}, u32[]{:S(2)}) copy-start(bf16[512,1024]{1,0:T(8,128)(2,1)} %param.23) | copy-start | bytes 3145732
  0.6 6.4 %copy-start.17 = (bf16[1024,512]{1,0:T(8,128)(2,1)S(1)}, bf16[1024,512]{1,0:T(8,128)(2,1)}, u32[]{:S(2)}) copy-start(bf16[1024,512]{1,0:T(8,128)(2,1)} %param.21) | copy-start | bytes 3145732
  5.0 3.8 %copy-start.13 = (bf16[768,512]{1,0:T(8,128)(2,1)}, bf16[768,512]{1,0:T(8,128)(2,1)S(1)}, u32[]{:S(2)}) copy-start(bf16[768,512]{1,0:T(8,128)(2,1)S(1)} %constant_dynamic-update-slice_fusion) | copy-start | bytes 2359300
  7.0 1.3 copy-start.1
  7.1 1.3 copy-start.11
  8.8 2.9 %copy-start.16 = (bf16[1024,512]{1,0:T(8,128)(2,1)S(1)}, bf16[1024,512]{1,0:T(8,128)(2,1)}, u32[]{:S(2)}) copy-start(bf16[1024,512]{1,0:T(8,128)(2,1)} %param.24) | copy-start | bytes 3145732
  11.7 2.3 %copy-start.18 = (bf16[768,1024]{1,0:T(8,128)(2,1)}, bf16[768,1024]{1,0:T(8,128)(2,1)S(1)}, u32[]{:S(2)}) copy-start(bf16[768,1024]{1,0:T(8,128)(2,1)S(1)} %get-tuple-element.46) | copy-start | bytes 4718596
  11.7 2.3 %copy-start.8 = (bf16[512,256]{1,0:T(8,128)(2,1)S(1)}, bf16[512,256]{1,0:T(8,128)(2,1)}, u32[]{:S(2)}) copy-start(bf16[512,256]{1,0:T(8,128)(2,1)} %param.25) | copy-start | bytes 786436
  14.1 0.9 copy-start.6
  14.1 0.8 copy-start.15
  14.1 49.7 %copy-start.19 = (f32[256,512]{1,0:T(8,128)S(1)}, f32[256,512]{1,0:T(8,128)}, u32[]{:S(2)}) copy-start(f32[256,512]{1,0:T(8,128)} %get-tuple-element.45) | copy-start | bytes 1572868
  64.8 1.8 %copy-start.9 = (bf16[512,256]{1,0:T(8,128)(2,1)S(1)}, bf16[512,256]{1,0:T(8,128)(2,1)}, u32[]{:S(2)}) copy-start(bf16[512,256]{1,0:T(8,128)(2,1)} %param.25) | copy-start | bytes 786436
  66.1 1.4 copy-start.21
  67.5 1.6 %copy-start.14 = (bf16[768,512]{1,0:T(8,128)(2,1)S(1)}, bf16[768,512]{1,0:T(8,128)(2,1)}, u32[]{:S(2)}) copy-start(bf16[768,512]{1,0:T(8,128)(2,1)} %copy-done.13) | copy-start | bytes 2359300
  74.6 2.8 %copy-start.7 = (bf16[768,512]{1,0:T(8,128)(2,1)S(1)}, bf16[768,512]{1,0:T(8,128)(2,1)}, u32[]{:S(2)}) copy-start(bf16[768,512]{1,0:T(8,128)(2,1)} %copy-done.6) | copy-start | bytes 2359300
  74.6 3.9 %copy-start.2 = (f32[256,1024]{1,0:T(8,128)S(1)}, f32[256,1024]{1,0:T(8,128)}, u32[]{:S(2)}) copy-start(f32[256,1024]{1,0:T(8,128)} %copy-done.1) | copy-start | bytes 3145732
  74.6 3.9 %copy-start.20 = (bf16[256,512]{1,0:T(8,128)(2,1)S(1)}, bf16[256,512]{1,0:T(8,128)(2,1)}, u32[]{:S(2)}) copy-start(bf16[256,512]{1,0:T(8,128)(2,1)} %fusion.1) | copy-start | bytes 786436
  78.5 1.5 %copy-start.10 = (bf16[256,512]{1,0:T(8,128)(2,1)S(1)}, bf16[256,512]{1,0:T(8,128)(2,1)}, u32[]{:S(2)}) copy-start(bf16[256,512]{1,0:T(8,128)(2,1)} %param.13) | copy-start | bytes 786436
  83.2 5.1 %copy-start.4 = (bf16[1024,512]{1,0:T(8,128)(2,1)S(1)}, bf16[1024,512]{1,0:T(8,128)(2,1)}, u32[]{:S(2)}) copy-start(bf16[1024,512]{1,0:T(8,128)(2,1)} %convolution_convert_fusion.2) | copy-start | bytes 3145732
  83.2 5.2 %copy-start.5 = (bf16[512,256]{1,0:T(8,128)(2,1)S(1)}, bf16[512,256]{1,0:T(8,128)(2,1)}, u32[]{:S(2)}) copy-start(bf16[512,256]{1,0:T(8,128)(2,1)} %convolution_convert_fusion.5) | copy-start | bytes 786436
  83.2 5.2 %copy-start.3 = (bf16[512,1024]{1,0:T(8,128)(2,1)S(1)}, bf16[512,1024]{1,0:T(8,128)(2,1)}, u32[]{:S(2)}) copy-start(bf16[512,1024]{1,0:T(8,128)(2,1)} %convolution_convert_fusion.1) | copy-start | bytes 3145732
  88.3 1.0 copy-start.12

commit v2 on v1

--- a/solution.py
+++ b/solution.py
@@ -36,20 +36,21 @@
     embedding = jnp.dot(second_act, third, preferred_element_type=jnp.float32)
     inv_norm = lax.rsqrt(jnp.sum(embedding * embedding, axis=1, keepdims=True) + 1.0)
     unit = (embedding * inv_norm).astype(jnp.bfloat16)
-    return ((first_pre, first_act, second_pre, second_act, embedding, inv_norm), unit)
+    saved = (silu_slope(first_pre), first_act, silu_slope(second_pre), second_act, embedding, inv_norm)
+    return saved, unit
 
 
 def tower_backward(features, second, third, saved, unit_grad):
-    first_pre, first_act, second_pre, second_act, embedding, inv_norm = saved
+    first_slope, first_act, second_slope, second_act, embedding, inv_norm = saved
     along = jnp.sum(embedding * unit_grad, axis=1, keepdims=True)
     embed_grad = (inv_norm * unit_grad - inv_norm * inv_norm * inv_norm * embedding * along).astype(
         jnp.bfloat16
     )
     third_grad = contract_rows(second_act, embed_grad)
-    second_slope = (contract_cols(embed_grad, third) * silu_slope(second_pre)).astype(jnp.bfloat16)
-    second_grad = contract_rows(first_act, second_slope)
-    first_slope = (contract_cols(second_slope, second) * silu_slope(first_pre)).astype(jnp.bfloat16)
-    first_grad = contract_rows(features, first_slope)
+    second_step = (contract_cols(embed_grad, third) * second_slope).astype(jnp.bfloat16)
+    second_grad = contract_rows(first_act, second_step)
+    first_step = (contract_cols(second_step, second) * first_slope).astype(jnp.bfloat16)
+    first_grad = contract_rows(features, first_step)
     return (first_grad, second_grad, third_grad)
 
 
@@ -577,6 +578,330 @@
     rows, columns = gradient.shape
     blocks = gradient.astype(jnp.bfloat16).reshape(ndp, rows // ndp, columns)
     return [blocks[:, :, c : c + pack_columns] for c in range(0, columns, pack_columns)]
+
+
+def backward_kernel(ndp, nneg, groups, *refs):
+    refs = list(refs)
+    take = iter(refs)
+    towers = [[next(take) for _ in range(9)] for _ in range(2)]
+    loss_ref = next(take)
+    stats_ref = next(take)
+    outs = [next(take) for _ in range(6)]
+    scratch = [[next(take) for _ in range(3)] for _ in range(2)]
+    names = ["packed", "c_in", "o1x", "l1x", "o1y", "l1y", "o2y", "l2y", "o2x", "l2x", "zs", "l3", "ag"]
+    bufs = [{name: next(take) for name in names} for _ in groups]
+    stat_dp, stat_dp_land, stat_neg, stat_neg_land = [next(take) for _ in range(4)]
+    sem_names = ["cs", "cr", "s1x", "r1x", "s1y", "r1y", "s2y", "r2y", "s2x", "r2x", "s3", "r3", "sg", "rg", "sh", "rh"]
+    for buf in bufs:
+        for name in sem_names:
+            buf[name] = next(take)
+    ss, sr, ts, tr = [next(take) for _ in range(4)]
+
+    me_dp, me_neg = lax.axis_index("dp"), lax.axis_index("neg")
+    line, nx = ndp // 2, nneg // 2
+    place, side = me_dp // 2, lax.rem(me_dp, 2)
+    me_x, me_core = me_neg // 2, lax.rem(me_neg, 2)
+    far, other = 1 - side, 1 - me_core
+    partner, mate = 2 * place + far, 2 * me_x + other
+    f32, bf16 = jnp.float32, jnp.bfloat16
+    greet(ndp, nneg, me_dp, me_neg)
+    pending = []
+
+    def go(copy):
+        copy.start()
+        pending.append(copy)
+
+    def x_of(k):
+        return lax.rem(me_x + k, nx)
+
+    def same_core(x):
+        return 2 * x + me_core
+
+    def z_of(k):
+        return lax.rem(place + k, line)
+
+    def arrived(ref, sem_array, index):
+        link(ref, ref, (sem_array, sem_array), index, "neg", mate).wait_recv()
+
+    def store(group, offset, value, dp, hg):
+        packed = bufs[group]["packed"]
+        pieces = hg // nneg
+        for p in range(value.shape[1] // pack_columns):
+            part = value[:, p * pack_columns : (p + 1) * pack_columns].astype(bf16)
+            part = part.reshape(value.shape[0] // hg, nx, 2, pieces, pack_columns)
+            lo = offset + p * pieces
+            for core in range(2):
+                packed[core, pl.ds(dp, value.shape[0] // hg), :, lo : lo + pieces, :] = part[:, :, core]
+
+    def weight_grad(group, offset, left_ref, right_ref):
+        rows, columns = left_ref.shape[1], right_ref.shape[1]
+        hg = rows // ndp
+        step = 2 * hg
+
+        def body(m, carry):
+            left = left_ref[:, pl.ds(pl.multiple_of(m * step, step), step)]
+            store(group, offset, contract_rows(left, right_ref[...]), 2 * m, hg)
+            return carry
+
+        lax.fori_loop(0, rows // step, body, 0)
+        return offset + hg // nneg * (columns // pack_columns)
+
+    def row_loop(count, body):
+        step = 256 if count % 256 == 0 else count
+
+        def wrapped(i, carry):
+            body(pl.ds(pl.multiple_of(i * step, step), step))
+            return carry
+
+        lax.fori_loop(0, count // step, wrapped, 0)
+
+    def embed_stage(t):
+        feat, act1, slope1, act2, slope2, emb_ref, grad_ref, second, third = towers[t]
+        eg, s2, s1 = scratch[t]
+
+        def body(rows):
+            emb, grad = emb_ref[rows, :], grad_ref[rows, :]
+            inv_norm = lax.rsqrt(jnp.sum(emb * emb, axis=1, keepdims=True) + 1.0)
+            along = jnp.sum(emb * grad, axis=1, keepdims=True)
+            value = (inv_norm * grad - inv_norm * inv_norm * inv_norm * emb * along).astype(bf16)
+            eg[rows, :] = value
+            s2[rows, :] = (contract_cols(value, third[...]) * slope2[rows, :]).astype(bf16)
+
+        row_loop(feat.shape[0], body)
+
+    def second_stage(t, group):
+        feat, act1, slope1, act2, slope2, emb_ref, grad_ref, second, third = towers[t]
+        eg, s2, s1 = scratch[t]
+        offset = weight_grad(group, 0, act2, eg)
+        weight_grad(group, offset, act1, s2)
+
+    def slope_stage(t):
+        feat, act1, slope1, act2, slope2, emb_ref, grad_ref, second, third = towers[t]
+        eg, s2, s1 = scratch[t]
+        columns = second.shape[0]
+
+        def body(rows):
+            for c in range(0, columns, 512):
+                value = contract_cols(s2[rows, :], second[c : c + 512, :]) * slope1[rows, c : c + 512]
+                s1[rows, c : c + 512] = value.astype(bf16)
+
+        row_loop(feat.shape[0], body)
+
+    def first_stage(t, group):
+        weight_grad(group, 0, towers[t][0], scratch[t][2])
+
+    def stage0(g):
+        b = bufs[g]
+        go(link(b["packed"].at[other], b["c_in"], (b["cs"], b["cr"]), 0, "neg", mate))
+
+    def base(b, dp, x, lo, hi):
+        return b["packed"][me_core, dp, x, lo:hi, :].astype(f32) + b["c_in"][dp, x, lo:hi, :].astype(f32)
+
+    def loop(count, body):
+        def wrapped(i, carry):
+            body(i)
+            return carry
+
+        lax.fori_loop(0, count, wrapped, 0)
+
+    def stage1(g):
+        b, (r1, r) = bufs[g], groups[g]
+        arrived(b["c_in"], b["cr"], 0)
+        for k in range(1, nx):
+            x = x_of(k)
+
+            def body(dp):
+                b["o1x"][x, dp] = base(b, dp, x, 0, r1).astype(bf16)
+
+            loop(ndp, body)
+            go(link(b["o1x"].at[x], b["l1x"].at[me_x], (b["s1x"], b["r1x"]), me_x, "neg", same_core(x), x))
+
+        def body_y(z):
+            for x in range(nx):
+                b["o1y"][z, x] = base(b, 2 * z + far, x, r1, r).astype(bf16)
+
+        loop(line, body_y)
+        go(link(b["o1y"], b["l1y"], (b["s1y"], b["r1y"]), 0, "dp", partner))
+
+    def low(b, dp, r1):
+        value = base(b, dp, me_x, 0, r1)
+        for k in range(1, nx):
+            value = value + b["l1x"][x_of(k), dp].astype(f32)
+        return value
+
+    def stage2(g):
+        b, (r1, r) = bufs[g], groups[g]
+        for k in range(1, nx):
+            x = x_of(k)
+            arrived(b["l1x"].at[x], b["r1x"], x)
+
+        def body(z):
+            b["o2y"][z] = low(b, 2 * z + far, r1).astype(bf16)
+
+        loop(line, body)
+        go(link(b["o2y"], b["l2y"], (b["s2y"], b["r2y"]), 0, "dp", partner))
+        arrived(b["l1y"], b["r1y"], 0)
+        for k in range(1, nx):
+            x = x_of(k)
+
+            def body_x(z):
+                value = base(b, 2 * z + side, x, r1, r) + b["l1y"][z, x].astype(f32)
+                b["o2x"][x, z] = value.astype(bf16)
+
+            loop(line, body_x)
+            go(link(b["o2x"].at[x], b["l2x"].at[me_x], (b["s2x"], b["r2x"]), me_x, "neg", same_core(x), x))
+
+    def stage3(g):
+        b, (r1, r) = bufs[g], groups[g]
+        arrived(b["l2y"], b["r2y"], 0)
+        for k in range(1, nx):
+            x = x_of(k)
+            arrived(b["l2x"].at[x], b["r2x"], x)
+
+        def body(z):
+            dp = 2 * z + side
+            b["zs"][z, 0:r1, :] = (low(b, dp, r1) + b["l2y"][z].astype(f32)).astype(bf16)
+            value = base(b, dp, me_x, r1, r) + b["l1y"][z, me_x].astype(f32)
+            for k in range(1, nx):
+                value = value + b["l2x"][x_of(k), z].astype(f32)
+            b["zs"][z, r1:r, :] = value.astype(bf16)
+
+        loop(line, body)
+        for k in range(1, line):
+            z = z_of(k)
+            go(link(b["zs"].at[z], b["l3"].at[place], (b["s3"], b["r3"]), place, "dp", 2 * z + side, z))
+
+    squares = []
+
+    def stage4(g):
+        b = bufs[g]
+        for k in range(1, line):
+            z = z_of(k)
+            arrived(b["l3"].at[z], b["r3"], z)
+        value = b["zs"][place].astype(f32)
+        for k in range(1, line):
+            value = value + b["l3"][z_of(k)].astype(f32)
+        squares.append(jnp.sum(value * value))
+        b["ag"][me_neg] = value.astype(bf16)
+        mine = b["ag"].at[me_neg]
+        for k in range(1, nx):
+            x = x_of(k)
+            go(link(mine, mine, (b["sg"], b["rg"]), me_x, "neg", same_core(x), x))
+        go(link(mine, mine, (b["sh"], b["rh"]), me_x, "neg", mate))
+
+    def stage5(g):
+        b = bufs[g]
+        for k in range(1, nx):
+            x = x_of(k)
+            ref = b["ag"].at[same_core(x)]
+            arrived(ref, b["rg"], x)
+            go(link(ref, ref, (b["sh"], b["rh"]), x, "neg", mate))
+
+    def stage6(g):
+        b = bufs[g]
+        for x in range(nx):
+            arrived(b["ag"].at[2 * x + other], b["rh"], x)
+
+    embed_stage(0)
+    second_stage(0, 0)
+    stage0(0)
+    slope_stage(0)
+    first_stage(0, 1)
+    stage0(1)
+    stage1(0)
+    embed_stage(1)
+    stage1(1)
+    second_stage(1, 2)
+    stage0(2)
+    stage2(0)
+    slope_stage(1)
+    stage1(2)
+    stage2(1)
+    first_stage(1, 3)
+    stage0(3)
+    stage3(0)
+    stage1(3)
+    stage3(1)
+    stage2(2)
+    stage4(0)
+    stage2(3)
+    stage4(1)
+    stage3(2)
+    stage3(3)
+    stage4(2)
+    stage4(3)
+    total_squares = squares[0] + squares[1] + squares[2] + squares[3]
+    lane = lax.broadcasted_iota(jnp.int32, (8, 128), 1)
+    stat_dp[...] = jnp.where(lane == 0, total_squares, loss_ref[0])
+    stat_copies = share("dp", ndp, me_dp, lambda t: stat_dp, stat_dp_land, ss, sr)
+    for g in range(4):
+        stage5(g)
+    finish(stat_copies)
+    total = stat_dp[...]
+    for k in range(1, ndp):
+        total = total + stat_dp_land[lax.rem(me_dp + k, ndp)]
+    stat_neg[...] = total
+    stat_copies = share("neg", nneg, me_neg, lambda t: stat_neg, stat_neg_land, ts, tr)
+    for g in range(4):
+        stage6(g)
+    finish(stat_copies)
+    total = stat_neg[...]
+    for k in range(1, nneg):
+        total = total + stat_neg_land[lax.rem(me_neg + k, nneg)]
+    stats_ref[...] = total
+    clip = clip_norm / jnp.maximum(jnp.sqrt(total[0:1, 0:1]), clip_norm)
+    for t in range(2):
+        third_out, second_out, first_out = outs[3 * t + 2], outs[3 * t + 1], outs[3 * t]
+        for group, out_ref, offset in (
+            (2 * t, third_out, 0),
+            (2 * t, second_out, third_out.shape[0] // nneg),
+            (2 * t + 1, first_out, 0),
+        ):
+            pieces = out_ref.shape[0] // nneg
+            for p in range(out_ref.shape[1] // pack_columns):
+                lo = offset + p * pieces
+                for n in range(nneg):
+                    value = bufs[group]["ag"][n, lo : lo + pieces, :].astype(f32) * clip
+                    out_ref[n * pieces : (n + 1) * pieces, p * pack_columns : (p + 1) * pack_columns] = value
+    for copy in pending:
+        copy.wait_send()
+
+
+def fused_backward(ndp, nneg, towers, loss_part):
+    line, nx = ndp // 2, nneg // 2
+    bf16, f32 = jnp.bfloat16, jnp.float32
+    groups, outs, scratch, buffers, semaphores = [], [], [], [], []
+    for feat, act1, slope1, act2, slope2, emb, grad, second, third in towers:
+        rows, fin = feat.shape
+        h1, h2, width = act1.shape[1], act2.shape[1], emb.shape[1]
+        for height, columns in ((fin, h1), (h1, h2), (h2, width)):
+            outs.append(jax.ShapeDtypeStruct((height // ndp, columns), f32))
+        both = h2 // (ndp * nneg) * (width // pack_columns) + h1 // (ndp * nneg) * (h2 // pack_columns)
+        alone = fin // (ndp * nneg) * (h1 // pack_columns)
+        for r in (both, alone):
+            groups.append((r * 4 // 9 // 16 * 16, r))
+        scratch += [pltpu.VMEM((rows, width), bf16), pltpu.VMEM((rows, h2), bf16), pltpu.VMEM((rows, h1), bf16)]
+    for r1, r in groups:
+        r2, c = r - r1, pack_columns
+        for shape in (
+            (2, ndp, nx, r, c), (ndp, nx, r, c), (nx, ndp, r1, c), (nx, ndp, r1, c), (line, nx, r2, c),
+            (line, nx, r2, c), (line, r1, c), (line, r1, c), (nx, line, r2, c), (nx, line, r2, c),
+            (line, r, c), (line, r, c), (nneg, r, c),
+        ):
+            buffers.append(pltpu.VMEM(shape, bf16))
+        semaphores += sems(1, 1, nx, nx, 1, 1, 1, 1, nx, nx, line, line, nx, nx, nx, nx)
+    stat = [pltpu.VMEM((8, 128), f32), pltpu.VMEM((ndp, 8, 128), f32), pltpu.VMEM((8, 128), f32), pltpu.VMEM((nneg, 8, 128), f32)]
+    operands = [operand for tower in towers for operand in tower]
+    return pl.pallas_call(
+        lambda *refs: backward_kernel(ndp, nneg, tuple(groups), *refs),
+        out_shape=(jax.ShapeDtypeStruct((8, 128), f32), *outs),
+        in_specs=[vmem] * len(operands) + [pl.BlockSpec(memory_space=pltpu.SMEM)],
+        out_specs=(vmem,) * 7,
+        scratch_shapes=scratch + buffers + stat + semaphores + sems(ndp, ndp, nneg, nneg),
+        compiler_params=pltpu.CompilerParams(
+            collective_id=1, has_side_effects=True, vmem_limit_bytes=56 * 1024 * 1024
+        ),
+    )(*operands, loss_part.reshape(1))
 
 
 def per_device(
@@ -671,6 +996,17 @@
     ) * inv_temp
     positive_grad = positive_slope[:, None] * query_unit.astype(jnp.float32) * inv_temp
     item_grad = jnp.concatenate([positive_grad, negative_sum * inv_temp], axis=0)
+    heights = (query_first.shape[0], query_second.shape[0], query_third.shape[0])
+    if all(height % (16 * ndp * nneg) == 0 for height in heights):
+        towers = [
+            (features, saved[1], saved[0], saved[3], saved[2], saved[4], grad, second, third)
+            for features, saved, grad, second, third in (
+                (query_features, query_saved, query_grad, query_second, query_third),
+                (item_features, item_saved, item_grad, item_second, item_third),
+            )
+        ]
+        stats, *clipped = fused_backward(ndp, nneg, towers, loss_part)
+        return (stats[0, 1] / (own_rows * ndp * nneg), *clipped)
     query_grads = tower_backward(query_features, query_second, query_third, query_saved, query_grad)
     item_grads = tower_backward(item_features, item_second, item_third, item_saved, item_grad)
     gradients = query_grads + item_grads

time: 146 us -> 130 us (0.89)
  matrix products: 26.9 us -> 9.94 us
  Pallas kernels: 97.8 us -> 100 us
  other arithmetic: 4.44 us -> 2.84 us
    dot_general x8 -> x0, matrix products: 17.7 us -> none  [the longest x6 15.1 us: contract_rows(): lax.dot_general(left, right, (((0,), (0,)), ((), ())), preferred_element_...]
    pallas_call x1, Pallas kernels: 50.1 us -> 52.6 us  [fused_backward(): pl.pallas_call(lambda *refs: backward_kernel(ndp, nneg, tuple(groups), *r...]
    mul x5 -> x0, other arithmetic: 2.38 us -> none  [the longest x3 2.36 us: per_device(): jnp.concatenate(blocks, axis=1).astype(jnp.float32) * clip_factor]
    unnamed x58 -> x41, local copies, waits for them, and re-layouts: 7.89 us -> 9.04 us
where the time goes in v2:
time: 130 us
  Pallas kernels  100 us (77%)
  local copies, waits for them, and re-layouts  14 us (11%)
  matrix products  9.94 us (8%)
  other arithmetic  2.84 us (2%)
  between operations  2.64 us (2%)
    pallas_call x1, Pallas kernels, fused_backward(): pl.pallas_call(lambda *refs: backward_kernel(ndp, nneg, tuple(groups), *r...  52.6 us
    pallas_call x1, Pallas kernels, per_device(): call(score_kernel, 0, ndp, nneg, (jax.ShapeDtypeStruct((own_rows, width),...  47.8 us
    unnamed x41, local copies, waits for them, and re-layouts  9.04 us
    dot_general x2, matrix products, tower_forward(): first_pre = jnp.dot(features, first, preferred_element_type=jnp.float32)  5.19 us
    dot_general x2, matrix products, tower_forward(): second_pre = jnp.dot(first_act, second, preferred_element_type=jnp.float32)  4.02 us

profile of v2, /device:TPU:0, one launch (start us, length us, event | category | flops | bytes accessed | tf_op | source)
XLA Modules:
  0.0 129.7 jit_solution(7864918303097351699)
XLA Ops:
  0.6 0.0 copy-start
  0.6 0.0 copy-start.12
  0.7 0.8 reshape.53.pid_ref
  1.5 0.7 reshape.54.nid_ref
  2.2 0.7 reshape.55.count_ref
  2.9 0.0 copy-start.16
  2.9 1.1 constant_dynamic-update-slice_fusion.1
  4.0 1.1 constant_dynamic-update-slice_fusion.refs_9_
  5.0 0.0 copy-done.12
  5.0 0.0 copy-done.16
  5.1 0.0 copy-start.5
  5.1 0.0 copy-start.9
  5.1 1.7 %add_multiply_fusion.2 = (f32[256,1024]{1,0:T(8,128)}, bf16[256,1024]{1,0:T(8,128)(2,1)S(1)}) fusion(bf16[256,512]{1,0:T(8,128)(2,1)S(1)} %copy-done.12, bf16[512,1024]{1,0:T(8,128)(2,1)S(1)} %copy-done.16), kind=kOutput, calls=%fused_computation.6 | convolution fusion | flops 270794752 | bytes 2883584 | tf_op jit(solution)/shard_map/dot_general | solution.py:32
  6.8 0.0 copy-start.11
  6.8 0.0 copy-done.9
  6.8 0.0 copy-start.7
  6.8 1.4 %add_multiply_fusion.3 = (f32[256,512]{1,0:T(8,128)}, bf16[256,512]{1,0:T(8,128)(2,1)S(1)}) fusion(bf16[256,1024]{1,0:T(8,128)(2,1)S(1)} %get-tuple-element.34.refs_1_, bf16[1024,512]{1,0:T(8,128)(2,1)S(1)} %copy-done.9), kind=kOutput, calls=%fused_computation.12 | convolution fusion | flops 269615104 | bytes 2359296 | tf_op jit(solution)/shard_map/dot_general | solution.py:34
  8.2 0.0 copy-done.11
  8.2 0.0 copy-start.8
  8.2 0.0 copy-done.7
  8.2 0.3 multiply_reduce_fusion.1
  8.5 0.1 copy.22.refs_5_
  8.6 0.0 copy-done.5
  8.7 0.0 copy-done
  8.7 0.0 copy-start.3
  8.7 0.0 copy-start.10
  8.7 3.5 %add_multiply_fusion = (f32[768,1024]{1,0:T(8,128)}, bf16[768,1024]{1,0:T(8,128)(2,1)S(1)}) fusion(bf16[768,512]{1,0:T(8,128)(2,1)S(1)} %constant_dynamic-update-slice_fusion.refs_9_, bf16[512,1024]{1,0:T(8,128)(2,1)S(1)} %copy-done), kind=kOutput, calls=%fused_computation | convolution fusion | flops 812384256 | bytes 6553600 | tf_op jit(solution)/shard_map/dot_general | solution.py:32
  12.2 0.0 copy-done.8
  12.2 0.0 copy-start.4
  12.2 0.0 copy-done.10
  12.2 0.0 copy-start.6
  12.2 2.6 %add_multiply_fusion.1 = (f32[768,512]{1,0:T(8,128)}, bf16[768,512]{1,0:T(8,128)(2,1)S(1)}) fusion(bf16[768,1024]{1,0:T(8,128)(2,1)S(1)} %get-tuple-element.30.refs_10_, bf16[1024,512]{1,0:T(8,128)(2,1)S(1)} %copy-done.10), kind=kOutput, calls=%fused_computation.3 | convolution fusion | flops 808845312 | bytes 4980736 | tf_op jit(solution)/shard_map/dot_general | solution.py:34
  14.8 0.0 copy-done.4
  14.8 0.0 copy-start.2
  14.8 0.0 copy-done.6
  14.8 0.0 copy-start.15
  14.8 0.4 multiply_reduce_fusion
  15.3 0.0 copy-start.1
  15.3 0.2 multiply_convert_fusion.3
  15.5 0.0 copy-done.3
  15.5 0.2 fusion.1
  15.7 0.1 copy-done.2
  15.8 0.0 copy-done.15
  15.8 47.8 %shard_map.180 = (f32[256,256]{1,0:T(8,128)S(1)}, f32[1,256]{1,0:T(1,128)S(1)}, f32[2,128,512]{2,1,0:T(8,128)S(1)}) custom-call(bf16[256,256]{1,0:T(8,128)(2,1)S(1)} %get-tuple-element.28.query_ref, bf16[2,256,256]{2,1,0:T(8,128)(2,1)S(1)} %bitcast.19, s32[4,256]{1,0:T(4,128)S(1)} %reshape.53.pid_ref, s32[8,512]{1,0:T(8,128)S(1)} %reshape.54.nid_ref, ...), custom_call_target="tpu_custom_call" | custom-call | tf_op jit(solution)/shard_map/pallas_call | solution.py:939
  63.6 0.6 subtract_reduce_fusion
  64.2 0.9 fusion
  65.0 0.0 copy-done.1
  65.1 0.2 copy.23
  65.3 1.0 pad_maximum_fusion.refs_15_
  66.2 52.6 %shard_map.181 = (f32[8,128]{1,0:T(8,128)}, f32[64,1024]{1,0:T(8,128)}, f32[128,512]{1,0:T(8,128)}, f32[64,256]{1,0:T(8,128)}, f32[64,1024]{1,0:T(8,128)}, /*index=5*/f32[128,512]{1,0:T(8,128)}, f32[64,256]{1,0:T(8,128)}) custom-call(bf16[256,512]{1,0:T(8,128)(2,1)} %refs_0_.1, bf16[256,1024]{1,0:T(8,128)(2,1)} %copy-done.11, ...), custom_call_target="tpu_custom_call" | custom-call | tf_op jit(solution)/shard_map/pallas_call | solution.py:895
  118.8 0.0 copy-start.13
  118.8 0.0 copy-start.14
  118.8 1.3 %slice.11 = f32[1,1]{1,0:T(1,128)} slice(f32[8,128]{1,0:T(8,128)} %get-tuple-element.20), slice={[0:1], [1:2]} | slice | bytes 8 | tf_op jit(solution)/shard_map/slice | solution.py:1009
  120.8 1.7 %copy.31 = f32[64,1024]{1,0:T(8,128)} copy(f32[64,1024]{1,0:T(8,128)} %get-tuple-element.53) | data formatting | bytes 524288
  122.5 1.7 %copy.32 = f32[128,512]{1,0:T(8,128)} copy(f32[128,512]{1,0:T(8,128)} %get-tuple-element.54) | data formatting | bytes 524288
  124.1 1.5 %copy.33 = f32[64,256]{1,0:T(8,128)} copy(f32[64,256]{1,0:T(8,128)} %get-tuple-element.55) | data formatting | bytes 131072
  125.6 1.7 %copy.34 = f32[64,1024]{1,0:T(8,128)} copy(f32[64,1024]{1,0:T(8,128)} %get-tuple-element.56) | data formatting | bytes 524288
  127.3 0.0 copy-done.13
  127.3 0.7 copy.35
  128.0 0.0 copy-done.14
  128.0 0.6 copy.36
  (5 shorter events, 0.1 us)
Async XLA Ops:
  0.6 8.0 %copy-start = (bf16[512,1024]{1,0:T(8,128)(2,1)S(1)}, bf16[512,1024]{1,0:T(8,128)(2,1)}, u32[]{:S(2)}) copy-start(bf16[512,1024]{1,0:T(8,128)(2,1)} %param.23) | copy-start | bytes 3145732
  0.6 4.4 %copy-start.12 = (bf16[256,512]{1,0:T(8,128)(2,1)S(1)}, bf16[256,512]{1,0:T(8,128)(2,1)}, u32[]{:S(2)}) copy-start(bf16[256,512]{1,0:T(8,128)(2,1)} %refs_0_.1) | copy-start | bytes 786436
  2.9 2.2 %copy-start.16 = (bf16[512,1024]{1,0:T(8,128)(2,1)S(1)}, bf16[512,1024]{1,0:T(8,128)(2,1)}, u32[]{:S(2)}) copy-start(bf16[512,1024]{1,0:T(8,128)(2,1)} %param.20) | copy-start | bytes 3145732
  5.1 3.6 %copy-start.5 = (bf16[768,512]{1,0:T(8,128)(2,1)}, bf16[768,512]{1,0:T(8,128)(2,1)S(1)}, u32[]{:S(2)}) copy-start(bf16[768,512]{1,0:T(8,128)(2,1)S(1)} %constant_dynamic-update-slice_fusion.refs_9_) | copy-start | bytes 2359300
  5.1 1.7 %copy-start.9 = (bf16[1024,512]{1,0:T(8,128)(2,1)S(1)}, bf16[1024,512]{1,0:T(8,128)(2,1)}, u32[]{:S(2)}) copy-start(bf16[1024,512]{1,0:T(8,128)(2,1)} %refs_7_.1) | copy-start | bytes 3145732
  6.8 1.4 %copy-start.11 = (bf16[256,1024]{1,0:T(8,128)(2,1)}, bf16[256,1024]{1,0:T(8,128)(2,1)S(1)}, u32[]{:S(2)}) copy-start(bf16[256,1024]{1,0:T(8,128)(2,1)S(1)} %get-tuple-element.34.refs_1_) | copy-start | bytes 1572868
  6.8 1.4 %copy-start.7 = (bf16[512,256]{1,0:T(8,128)(2,1)S(1)}, bf16[512,256]{1,0:T(8,128)(2,1)}, u32[]{:S(2)}) copy-start(bf16[512,256]{1,0:T(8,128)(2,1)} %refs_8_.1) | copy-start | bytes 786436
  8.2 4.0 %copy-start.8 = (bf16[256,512]{1,0:T(8,128)(2,1)}, bf16[256,512]{1,0:T(8,128)(2,1)S(1)}, u32[]{:S(2)}) copy-start(bf16[256,512]{1,0:T(8,128)(2,1)S(1)} %get-tuple-element.36.refs_3_) | copy-start | bytes 786436
  8.7 6.8 %copy-start.3 = (f32[256,256]{1,0:T(8,128)}, f32[256,256]{1,0:T(8,128)S(1)}, u32[]{:S(2)}) copy-start(f32[256,256]{1,0:T(8,128)S(1)} %copy.22.refs_5_) | copy-start | bytes 786436
  8.7 3.5 %copy-start.10 = (bf16[1024,512]{1,0:T(8,128)(2,1)S(1)}, bf16[1024,512]{1,0:T(8,128)(2,1)}, u32[]{:S(2)}) copy-start(bf16[1024,512]{1,0:T(8,128)(2,1)} %refs_16_.1) | copy-start | bytes 3145732
  12.2 2.6 %copy-start.4 = (bf16[768,1024]{1,0:T(8,128)(2,1)}, bf16[768,1024]{1,0:T(8,128)(2,1)S(1)}, u32[]{:S(2)}) copy-start(bf16[768,1024]{1,0:T(8,128)(2,1)S(1)} %get-tuple-element.30.refs_10_) | copy-start | bytes 4718596
  12.2 2.6 %copy-start.6 = (bf16[512,256]{1,0:T(8,128)(2,1)S(1)}, bf16[512,256]{1,0:T(8,128)(2,1)}, u32[]{:S(2)}) copy-start(bf16[512,256]{1,0:T(8,128)(2,1)} %refs_17_.1) | copy-start | bytes 786436
  14.8 0.9 copy-start.2
  14.8 0.9 copy-start.15
  15.3 49.8 %copy-start.1 = (f32[768,256]{1,0:T(8,128)}, f32[768,256]{1,0:T(8,128)S(1)}, u32[]{:S(2)}) copy-start(f32[768,256]{1,0:T(8,128)S(1)} %get-tuple-element.42.refs_14_) | copy-start | bytes 2359300
  118.8 8.5 %copy-start.13 = (f32[128,512]{1,0:T(8,128)S(1)}, f32[128,512]{1,0:T(8,128)}, u32[]{:S(2)}) copy-start(f32[128,512]{1,0:T(8,128)} %get-tuple-element.57) | copy-start | bytes 786436
  118.8 9.2 %copy-start.14 = (f32[64,256]{1,0:T(8,128)S(1)}, f32[64,256]{1,0:T(8,128)}, u32[]{:S(2)}) copy-start(f32[64,256]{1,0:T(8,128)} %get-tuple-element.58) | copy-start | bytes 196612

commit v3 on v2

--- a/solution.py
+++ b/solution.py
@@ -8,6 +8,7 @@
 from jax.sharding import PartitionSpec as P
 
 inv_temp = 20.0
+log2_e = 1.4426950408889634
 clip_norm = 256.0
 
 
@@ -147,9 +148,14 @@
 
     for k in range(1, blocks):
         pl.semaphore_signal(barrier, inc=1, device_id=quad(k), device_id_type=pl.DeviceIdType.MESH)
-    meta_out[0:1, :] = nid_ref[pl.ds(me_dp, 1), :]
-    meta_out[1:2, :] = count_ref[pl.ds(me_dp, 1), :]
-    pid_out[...] = pid_ref[pl.ds(me_neg, 1), :]
+    def own_ids(ref, index, count):
+        if count % 128 == 0:
+            return ref[:, pl.ds(pl.multiple_of(index * count, count), count)]
+        return ref[pl.ds(index, 1), :]
+
+    meta_out[0:1, :] = own_ids(nid_ref, me_dp, block)
+    meta_out[1:2, :] = own_ids(count_ref, me_dp, block)
+    pid_out[...] = own_ids(pid_ref, me_neg, rows_q)
     pl.semaphore_wait(barrier, (line - 1) + (blocks - 1))
 
     def slot(x, y, half):
@@ -273,15 +279,14 @@
 
     for b in range(blocks):
         rows[b, 0:1, :] = meta[b, 0:1, :].astype(jnp.float32)
-        rows[b, 1:2, :] = jnp.log(meta[b, 1:2, :].astype(jnp.float32))
+        rows[b, 1:2, :] = jnp.log2(meta[b, 1:2, :].astype(jnp.float32))
     for z in range(line):
         pid_col[z] = jnp.broadcast_to(pid_land[z].astype(jnp.float32), (lanes, rows_q)).T
         den[z] = jnp.zeros((rows_q, lanes), jnp.float32)
 
-    def unit(i, carry):
-        b, z = i // line, lax.rem(i, line)
+    def unit(b, z):
         dots = contract_cols(q_land[z].reshape(rows_q, width), n_land[b].reshape(block, width))
-        value = jnp.exp(dots * inv_temp - rows[b, 1:2, :])
+        value = jnp.exp2(dots * (inv_temp * log2_e) - rows[b, 1:2, :])
         ids = jnp.concatenate([pid_col[z]] * (block // lanes), axis=1)
         value = jnp.where(ids != rows[b, 0:1, :], value, 0.0)
         w[b, z] = value.astype(jnp.bfloat16)
@@ -289,9 +294,13 @@
         for c in range(0, block, lanes):
             total = total + value[:, c : c + lanes]
         den[z] = total
+
+    def units(b, carry):
+        for z in range(line):
+            unit(b, z)
         return carry
 
-    lax.fori_loop(0, blocks * line, unit, 0)
+    lax.fori_loop(0, blocks, units, 0)
     for z in range(line):
         dpart[z] = jnp.sum(den[z].T, axis=0, keepdims=True)
     dpart[place] = dpart[place] + pexp_ref[...]
@@ -557,7 +566,7 @@
         copy.wait_send()
 
 
-def call(kernel, collective, ndp, nneg, out_shape, scratch, in_specs):
+def call(kernel, collective, ndp, nneg, out_shape, scratch, in_specs, megabytes=48):
     return pl.pallas_call(
         functools.partial(kernel, ndp, nneg),
         out_shape=out_shape,
@@ -565,7 +574,7 @@
         out_specs=tuple(vmem for _ in out_shape),
         scratch_shapes=scratch,
         compiler_params=pltpu.CompilerParams(
-            collective_id=collective, has_side_effects=True, vmem_limit_bytes=48 * 1024 * 1024
+            collective_id=collective, has_side_effects=True, vmem_limit_bytes=megabytes * 1024 * 1024
         ),
     )
 
@@ -586,10 +595,12 @@
     towers = [[next(take) for _ in range(9)] for _ in range(2)]
     loss_ref = next(take)
     stats_ref = next(take)
-    outs = [next(take) for _ in range(6)]
+    gathered = [next(take) for _ in groups]
     scratch = [[next(take) for _ in range(3)] for _ in range(2)]
-    names = ["packed", "c_in", "o1x", "l1x", "o1y", "l1y", "o2y", "l2y", "o2x", "l2x", "zs", "l3", "ag"]
+    names = ["packed", "c_in", "o1x", "l1x", "o1y", "l1y", "o2y", "l2y", "o2x", "l2x", "zs", "l3"]
     bufs = [{name: next(take) for name in names} for _ in groups]
+    for buf, ref in zip(bufs, gathered):
+        buf["ag"] = ref
     stat_dp, stat_dp_land, stat_neg, stat_neg_land = [next(take) for _ in range(4)]
     sem_names = ["cs", "cr", "s1x", "r1x", "s1y", "r1y", "s2y", "r2y", "s2x", "r2x", "s3", "r3", "sg", "rg", "sh", "rh"]
     for buf in bufs:
@@ -849,25 +860,11 @@
     for k in range(1, nneg):
         total = total + stat_neg_land[lax.rem(me_neg + k, nneg)]
     stats_ref[...] = total
-    clip = clip_norm / jnp.maximum(jnp.sqrt(total[0:1, 0:1]), clip_norm)
-    for t in range(2):
-        third_out, second_out, first_out = outs[3 * t + 2], outs[3 * t + 1], outs[3 * t]
-        for group, out_ref, offset in (
-            (2 * t, third_out, 0),
-            (2 * t, second_out, third_out.shape[0] // nneg),
-            (2 * t + 1, first_out, 0),
-        ):
-            pieces = out_ref.shape[0] // nneg
-            for p in range(out_ref.shape[1] // pack_columns):
-                lo = offset + p * pieces
-                for n in range(nneg):
-                    value = bufs[group]["ag"][n, lo : lo + pieces, :].astype(f32) * clip
-                    out_ref[n * pieces : (n + 1) * pieces, p * pack_columns : (p + 1) * pack_columns] = value
     for copy in pending:
         copy.wait_send()
 
 
-def fused_backward(ndp, nneg, towers, loss_part):
+def fused_backward(ndp, nneg, towers, loss_part, own_queries):
     line, nx = ndp // 2, nneg // 2
     bf16, f32 = jnp.bfloat16, jnp.float32
     groups, outs, scratch, buffers, semaphores = [], [], [], [], []
@@ -886,22 +883,59 @@
         for shape in (
             (2, ndp, nx, r, c), (ndp, nx, r, c), (nx, ndp, r1, c), (nx, ndp, r1, c), (line, nx, r2, c),
             (line, nx, r2, c), (line, r1, c), (line, r1, c), (nx, line, r2, c), (nx, line, r2, c),
-            (line, r, c), (line, r, c), (nneg, r, c),
+            (line, r, c), (line, r, c),
         ):
             buffers.append(pltpu.VMEM(shape, bf16))
         semaphores += sems(1, 1, nx, nx, 1, 1, 1, 1, nx, nx, line, line, nx, nx, nx, nx)
     stat = [pltpu.VMEM((8, 128), f32), pltpu.VMEM((ndp, 8, 128), f32), pltpu.VMEM((8, 128), f32), pltpu.VMEM((nneg, 8, 128), f32)]
     operands = [operand for tower in towers for operand in tower]
-    return pl.pallas_call(
+    stats, *gathered = pl.pallas_call(
         lambda *refs: backward_kernel(ndp, nneg, tuple(groups), *refs),
-        out_shape=(jax.ShapeDtypeStruct((8, 128), f32), *outs),
+        out_shape=(
+            jax.ShapeDtypeStruct((8, 128), f32),
+            *[jax.ShapeDtypeStruct((nneg, r, pack_columns), bf16) for _, r in groups],
+        ),
         in_specs=[vmem] * len(operands) + [pl.BlockSpec(memory_space=pltpu.SMEM)],
-        out_specs=(vmem,) * 7,
+        out_specs=(vmem,) * 5,
         scratch_shapes=scratch + buffers + stat + semaphores + sems(ndp, ndp, nneg, nneg),
         compiler_params=pltpu.CompilerParams(
-            collective_id=1, has_side_effects=True, vmem_limit_bytes=56 * 1024 * 1024
+            collective_id=1, has_side_effects=True, vmem_limit_bytes=40 * 1024 * 1024
         ),
     )(*operands, loss_part.reshape(1))
+    any_space = pl.BlockSpec(memory_space=pl.ANY)
+    mean_loss, *clipped = pl.pallas_call(
+        functools.partial(finish_kernel, nneg, own_queries * ndp * nneg),
+        out_shape=(jax.ShapeDtypeStruct((1,), f32), *outs),
+        in_specs=[vmem] * 5,
+        out_specs=(pl.BlockSpec(memory_space=pltpu.SMEM), *([any_space] * 6)),
+        scratch_shapes=[pltpu.VMEM(out.shape, f32) for out in outs] + sems(6),
+    )(stats, *gathered)
+    return (mean_loss.reshape(()), *clipped)
+
+
+def finish_kernel(nneg, count, stats_ref, *refs):
+    gathered, loss_ref, outs, staged, done = refs[:4], refs[4], refs[5:11], refs[11:17], refs[17]
+    clip = clip_norm / jnp.maximum(jnp.sqrt(stats_ref[0:1, 0:1]), clip_norm)
+    copies = []
+    for t in range(2):
+        third_ref, second_ref, first_ref = staged[3 * t + 2], staged[3 * t + 1], staged[3 * t]
+        for index, group, ref, offset in (
+            (3 * t + 1, 2 * t, second_ref, third_ref.shape[0] // nneg),
+            (3 * t, 2 * t + 1, first_ref, 0),
+            (3 * t + 2, 2 * t, third_ref, 0),
+        ):
+            pieces = ref.shape[0] // nneg
+            for p in range(ref.shape[1] // pack_columns):
+                lo = offset + p * pieces
+                for n in range(nneg):
+                    value = gathered[group][n, lo : lo + pieces, :].astype(jnp.float32) * clip
+                    ref[n * pieces : (n + 1) * pieces, p * pack_columns : (p + 1) * pack_columns] = value
+            copy = pltpu.make_async_copy(ref, outs[index], done.at[index])
+            copy.start()
+            copies.append(copy)
+    loss_ref[0] = jnp.sum(stats_ref[0:1, 1:2]) / count
+    for copy in copies:
+        copy.wait()
 
 
 def per_device(
@@ -978,12 +1012,13 @@
             2 * nx, 2 * nx, 2 * nx, 2 * nx, nx, nx, 1, 1, nx, nx,
         ),
         [vmem] * 6,
+        40,
     )(
         query_unit,
         negative_unit.reshape(2, block // 2, width),
-        positive_ids.reshape(nneg, own_rows),
-        negative_ids.reshape(ndp, block),
-        negative_counts.reshape(ndp, block),
+        positive_ids.reshape((1, -1) if own_rows % 128 == 0 else (nneg, own_rows)),
+        negative_ids.reshape((1, -1) if block % 128 == 0 else (ndp, block)),
+        negative_counts.reshape((1, -1) if block % 128 == 0 else (ndp, block)),
         positive_exp.reshape(1, own_rows),
     )
     own_denom = denom.reshape(-1)
@@ -1005,8 +1040,7 @@
                 (item_features, item_saved, item_grad, item_second, item_third),
             )
         ]
-        stats, *clipped = fused_backward(ndp, nneg, towers, loss_part)
-        return (stats[0, 1] / (own_rows * ndp * nneg), *clipped)
+        return fused_backward(ndp, nneg, towers, loss_part, own_rows)
     query_grads = tower_backward(query_features, query_second, query_third, query_saved, query_grad)
     item_grads = tower_backward(item_features, item_second, item_third, item_saved, item_grad)
     gradients = query_grads + item_grads

time: 130 us -> 128 us (0.985)
  Pallas kernels: 100 us -> 93.1 us
  local copies, waits for them, and re-layouts: 14 us -> 19.5 us
  between operations: 2.64 us -> 1.02 us
    unnamed x41 -> x63, local copies, waits for them, and re-layouts: 9.04 us -> 16.2 us
    pallas_call x1, Pallas kernels: 47.8 us -> 42.5 us  [per_device(): call(score_kernel, 0, ndp, nneg, (jax.ShapeDtypeStruct((own_rows, width),...]
    pallas_call x1, Pallas kernels: 52.6 us -> 47.9 us  [fused_backward(): pl.pallas_call(lambda *refs: backward_kernel(ndp, nneg, tuple(groups), *r...]
    pallas_call x0 -> x1, Pallas kernels: none -> 2.76 us  [fused_backward(): pl.pallas_call(functools.partial(finish_kernel, nneg, own_queries * ndp *...]
    reshape x3 -> x0, local copies, waits for them, and re-layouts: 2.24 us -> none  [the longest x1 0.8 us: per_device(): positive_ids.reshape(nneg, own_rows)]
    mul x1, local copies, waits for them, and re-layouts: 0.2 us -> 2.05 us  [per_device(): negative_sum * inv_temp]
    slice x1 -> x0, local copies, waits for them, and re-layouts: 1.3 us -> none  [per_device(): return (stats[0, 1] / (own_rows * ndp * nneg), *clipped)]
where the time goes in v3:
time: 128 us
  Pallas kernels  93.1 us (73%)
  local copies, waits for them, and re-layouts  19.5 us (15%)
  matrix products  9.89 us (8%)
  other arithmetic  4.05 us (3%)
    pallas_call x1, Pallas kernels, fused_backward(): pl.pallas_call(lambda *refs: backward_kernel(ndp, nneg, tuple(groups), *r...  47.9 us
    pallas_call x1, Pallas kernels, per_device(): call(score_kernel, 0, ndp, nneg, (jax.ShapeDtypeStruct((own_rows, width),...  42.5 us
    unnamed x63, local copies, waits for them, and re-layouts  16.2 us
    dot_general x2, matrix products, tower_forward(): first_pre = jnp.dot(features, first, preferred_element_type=jnp.float32)  5.11 us
    dot_general x2, matrix products, tower_forward(): second_pre = jnp.dot(first_act, second, preferred_element_type=jnp.float32)  4.05 us
    pallas_call x1, Pallas kernels, fused_backward(): pl.pallas_call(functools.partial(finish_kernel, nneg, own_queries * ndp *...  2.76 us

profile of v3, /device:TPU:0, one launch (start us, length us, event | category | flops | bytes accessed | tf_op | source)
XLA Modules:
  0.0 127.5 jit_solution(49794110296859462)
XLA Ops:
  0.6 0.0 copy-start
  0.6 0.0 copy-start.19
  0.7 0.0 copy-start.30
  0.7 1.1 constant_dynamic-update-slice_fusion.1
  1.8 1.1 constant_dynamic-update-slice_fusion.refs_9_
  2.9 0.0 copy-done.19
  2.9 0.0 copy-done.30
  2.9 0.0 copy-start.4
  2.9 0.0 copy-start.11
  2.9 1.6 %add_multiply_fusion.2 = (f32[256,1024]{1,0:T(8,128)}, bf16[256,1024]{1,0:T(8,128)(2,1)S(1)}) fusion(bf16[256,512]{1,0:T(8,128)(2,1)S(1)} %copy-done.19, bf16[512,1024]{1,0:T(8,128)(2,1)S(1)} %copy-done.30), kind=kOutput, calls=%fused_computation.6 | convolution fusion | flops 270794752 | bytes 2883584 | tf_op jit(solution)/shard_map/dot_general | solution.py:33
  4.6 0.0 copy-start.16
  4.6 0.0 copy-done.11
  4.6 0.0 copy-start.7
  4.6 1.4 %add_multiply_fusion.3 = (f32[256,512]{1,0:T(8,128)}, bf16[256,512]{1,0:T(8,128)(2,1)S(1)}) fusion(bf16[256,1024]{1,0:T(8,128)(2,1)S(1)} %get-tuple-element.44.refs_1_, bf16[1024,512]{1,0:T(8,128)(2,1)S(1)} %copy-done.11), kind=kOutput, calls=%fused_computation.12 | convolution fusion | flops 269615104 | bytes 2359296 | tf_op jit(solution)/shard_map/dot_general | solution.py:35
  6.0 0.0 copy-done.16
  6.0 0.0 copy-done.7
  6.0 0.3 multiply_reduce_fusion.1
  6.3 0.1 copy.22.refs_5_
  6.4 0.0 copy-done.4
  6.4 0.0 copy-done
  6.4 0.0 copy-start.13
  6.5 3.5 %add_multiply_fusion = (f32[768,1024]{1,0:T(8,128)}, bf16[768,1024]{1,0:T(8,128)(2,1)S(1)}) fusion(bf16[768,512]{1,0:T(8,128)(2,1)S(1)} %constant_dynamic-update-slice_fusion.refs_9_, bf16[512,1024]{1,0:T(8,128)(2,1)S(1)} %copy-done), kind=kOutput, calls=%fused_computation | convolution fusion | flops 812384256 | bytes 6553600 | tf_op jit(solution)/shard_map/dot_general | solution.py:33
  9.9 0.0 copy-done.8
  9.9 0.0 copy-start.1
  9.9 0.0 copy-done.13
  9.9 0.0 copy-start.6
  9.9 2.6 %add_multiply_fusion.1 = (f32[768,512]{1,0:T(8,128)}, bf16[768,512]{1,0:T(8,128)(2,1)S(1)}) fusion(bf16[768,1024]{1,0:T(8,128)(2,1)S(1)} %get-tuple-element.40.refs_10_, bf16[1024,512]{1,0:T(8,128)(2,1)S(1)} %copy-done.13), kind=kOutput, calls=%fused_computation.3 | convolution fusion | flops 808845312 | bytes 4980736 | tf_op jit(solution)/shard_map/dot_general | solution.py:35
  12.6 0.0 copy-done.1
  12.6 0.0 copy-done.6
  12.6 0.4 multiply_reduce_fusion
  13.0 0.0 copy-start.25
  13.0 0.0 copy-start.26
  13.1 0.0 copy-start.27
  13.1 0.2 multiply_convert_fusion.3
  13.3 0.2 fusion.1
  13.4 0.0 copy-done.29
  13.5 0.3 copy-done.25
  13.8 0.0 copy-done.26
  13.8 0.0 copy-done.27
  13.8 42.5 %shard_map.180 = (f32[256,256]{1,0:T(8,128)S(1)}, f32[1,256]{1,0:T(1,128)S(1)}, f32[2,128,512]{2,1,0:T(8,128)S(1)}) custom-call(bf16[256,256]{1,0:T(8,128)(2,1)S(1)} %get-tuple-element.38.query_ref, bf16[2,256,256]{2,1,0:T(8,128)(2,1)S(1)} %bitcast.22, s32[1,1024]{1,0:T(1,128)S(1)} %bitcast.26, s32[1,4096]{1,0:T(1,128)S(1)} %bitcast.23, ...), custom_call_target="tpu_custom_call" | custom-call | tf_op jit(solution)/shard_map/pallas_call | solution.py:973
  56.3 0.6 subtract_reduce_fusion
  56.9 0.9 fusion
  57.8 0.8 broadcast_multiply_fusion
  58.7 2.1 %copy.23 = f32[256,512]{0,1:T(8,128)} copy(f32[256,512]{1,0:T(8,128)} %bitcast.30) | data formatting | bytes 1048576 | tf_op jit(solution)/shard_map/mul | solution.py:1033
  60.7 1.3 %pad_maximum_fusion.refs_15_ = f32[768,256]{1,0:T(8,128)S(1)} fusion(f32[512,256]{1,0:T(8,128)} %bitcast.29, f32[256,256]{1,0:T(8,128)} %get-tuple-element.49), kind=kLoop, calls=%fused_computation.9 | loop fusion | flops 196608 | bytes 1572864 | tf_op jit(solution)/shard_map/concatenate | solution.py:1033
  62.0 0.4 copy-done.2
  62.4 1.4 %copy-done.3 = f32[768,512]{1,0:T(8,128)S(1)} copy-done((f32[768,512]{1,0:T(8,128)S(1)}, f32[768,512]{1,0:T(8,128)}, u32[]{:S(2)}) %copy-start.3) | copy-done | bytes 1572888
  63.8 1.1 copy-done.5
  64.9 0.9 copy-done.9
  65.8 0.9 copy-done.10
  66.8 1.2 copy-done.12
  68.0 1.2 copy-done.14
  69.2 1.2 copy-done.15
  70.5 1.0 copy-done.17
  71.5 1.0 copy-done.18
  72.6 0.9 copy-done.20
  73.5 47.9 %shard_map.181 = (f32[8,128]{1,0:T(8,128)S(1)}, bf16[4,80,256]{2,1,0:T(8,128)(2,1)S(1)}, bf16[4,64,256]{2,1,0:T(8,128)(2,1)S(1)}, bf16[4,80,256]{2,1,0:T(8,128)(2,1)S(1)}, bf16[4,64,256]{2,1,0:T(8,128)(2,1)S(1)}) custom-call(bf16[256,512]{1,0:T(8,128)(2,1)S(1)} %copy-done.20, bf16[256,1024]{1,0:T(8,128)(2,1)S(1)} %copy-done.17, f32[256,1024]{1,0:T(8,128)S(1)} %copy-done.15, ...), custom_call_target="tpu_custom_call" | custom-call | tf_op jit(solution)/shard_map/pallas_call | solution.py:892
  121.4 0.0 copy-start.21
  121.4 0.7 copy-done.21
  122.1 0.7 copy-done.22
  122.7 0.6 copy-done.23
  123.4 0.7 copy-done.24
  124.0 0.6 copy-done.28
  124.6 2.8 %shard_map.182 = (f32[1]{0:T(128)}, f32[64,1024]{1,0:T(8,128)}, f32[128,512]{1,0:T(8,128)}, f32[64,256]{1,0:T(8,128)}, f32[64,1024]{1,0:T(8,128)}, /*index=5*/f32[128,512]{1,0:T(8,128)}, f32[64,256]{1,0:T(8,128)}) custom-call(f32[8,128]{1,0:T(8,128)} %copy-done.28, bf16[4,80,256]{2,1,0:T(8,128)(2,1)} %copy-done.21, bf16[4,64,256]{2,1,0:T(8,128)(2,1)} %copy-done.23, ...), custom_call_target="tpu_custom_call" | custom-call | tf_op jit(solution)/shard_map/pallas_call | solution.py:906
  (21 shorter events, 0.1 us)
Async XLA Ops:
  0.6 5.8 %copy-start = (bf16[512,1024]{1,0:T(8,128)(2,1)S(1)}, bf16[512,1024]{1,0:T(8,128)(2,1)}, u32[]{:S(2)}) copy-start(bf16[512,1024]{1,0:T(8,128)(2,1)} %param.23) | copy-start | bytes 3145732
  0.6 2.2 %copy-start.19 = (bf16[256,512]{1,0:T(8,128)(2,1)S(1)}, bf16[256,512]{1,0:T(8,128)(2,1)}, u32[]{:S(2)}) copy-start(bf16[256,512]{1,0:T(8,128)(2,1)} %refs_0_.1) | copy-start | bytes 786436
  0.7 2.2 %copy-start.30 = (bf16[512,1024]{1,0:T(8,128)(2,1)S(1)}, bf16[512,1024]{1,0:T(8,128)(2,1)}, u32[]{:S(2)}) copy-start(bf16[512,1024]{1,0:T(8,128)(2,1)} %param.20) | copy-start | bytes 3145732
  2.9 3.5 %copy-start.4 = (bf16[768,512]{1,0:T(8,128)(2,1)}, bf16[768,512]{1,0:T(8,128)(2,1)S(1)}, u32[]{:S(2)}) copy-start(bf16[768,512]{1,0:T(8,128)(2,1)S(1)} %constant_dynamic-update-slice_fusion.refs_9_) | copy-start | bytes 2359300
  2.9 1.7 %copy-start.11 = (bf16[1024,512]{1,0:T(8,128)(2,1)S(1)}, bf16[1024,512]{1,0:T(8,128)(2,1)}, u32[]{:S(2)}) copy-start(bf16[1024,512]{1,0:T(8,128)(2,1)} %refs_7_.1) | copy-start | bytes 3145732
  4.6 1.4 %copy-start.16 = (bf16[256,1024]{1,0:T(8,128)(2,1)}, bf16[256,1024]{1,0:T(8,128)(2,1)S(1)}, u32[]{:S(2)}) copy-start(bf16[256,1024]{1,0:T(8,128)(2,1)S(1)} %get-tuple-element.44.refs_1_) | copy-start | bytes 1572868
  4.6 1.4 %copy-start.7 = (bf16[512,256]{1,0:T(8,128)(2,1)S(1)}, bf16[512,256]{1,0:T(8,128)(2,1)}, u32[]{:S(2)}) copy-start(bf16[512,256]{1,0:T(8,128)(2,1)} %refs_8_.1) | copy-start | bytes 786436
  6.0 3.9 %copy-start.8 = (bf16[256,512]{1,0:T(8,128)(2,1)}, bf16[256,512]{1,0:T(8,128)(2,1)S(1)}, u32[]{:S(2)}) copy-start(bf16[256,512]{1,0:T(8,128)(2,1)S(1)} %get-tuple-element.46.refs_3_) | copy-start | bytes 786436
  6.4 3.5 %copy-start.13 = (bf16[1024,512]{1,0:T(8,128)(2,1)S(1)}, bf16[1024,512]{1,0:T(8,128)(2,1)}, u32[]{:S(2)}) copy-start(bf16[1024,512]{1,0:T(8,128)(2,1)} %refs_16_.1) | copy-start | bytes 3145732
  9.9 2.6 %copy-start.1 = (bf16[768,1024]{1,0:T(8,128)(2,1)}, bf16[768,1024]{1,0:T(8,128)(2,1)S(1)}, u32[]{:S(2)}) copy-start(bf16[768,1024]{1,0:T(8,128)(2,1)S(1)} %get-tuple-element.40.refs_10_) | copy-start | bytes 4718596
  9.9 2.6 %copy-start.6 = (bf16[512,256]{1,0:T(8,128)(2,1)S(1)}, bf16[512,256]{1,0:T(8,128)(2,1)}, u32[]{:S(2)}) copy-start(bf16[512,256]{1,0:T(8,128)(2,1)} %refs_17_.1) | copy-start | bytes 786436
  12.6 0.9 copy-start.29
  13.0 0.7 copy-start.25
  13.0 0.7 copy-start.26
  13.1 0.7 copy-start.27
  60.7 1.6 %copy-start.2 = (bf16[768,1024]{1,0:T(8,128)(2,1)S(1)}, bf16[768,1024]{1,0:T(8,128)(2,1)}, u32[]{:S(2)}) copy-start(bf16[768,1024]{1,0:T(8,128)(2,1)} %copy-done.1) | copy-start | bytes 4718596
  62.4 1.4 %copy-start.3 = (f32[768,512]{1,0:T(8,128)S(1)}, f32[768,512]{1,0:T(8,128)}, u32[]{:S(2)}) copy-start(f32[768,512]{1,0:T(8,128)} %get-tuple-element.41.refs_13_) | copy-start | bytes 4718596
  63.8 1.1 copy-start.5
  64.9 0.9 copy-start.9
  65.8 0.9 copy-start.10
  66.8 1.2 copy-start.12
  68.0 1.2 copy-start.14
  69.2 1.2 copy-start.15
  70.5 1.0 copy-start.17
  71.5 1.0 copy-start.18
  72.6 0.9 copy-start.20
  121.4 0.7 copy-start.21
  122.1 0.7 copy-start.22
  122.7 0.6 copy-start.23
  123.4 0.7 copy-start.24
  124.0 0.6 copy-start.28

commit v4 on v3

--- a/solution.py
+++ b/solution.py
@@ -589,25 +589,26 @@
     return [blocks[:, :, c : c + pack_columns] for c in range(0, columns, pack_columns)]
 
 
-def backward_kernel(ndp, nneg, groups, *refs):
+step_inputs = (
+    "query_features", "positive_features", "negative_features", "positive_ids", "positive_counts", "negative_ids",
+    "negative_counts", "query_first", "query_second", "query_third", "item_first", "item_second", "item_third",
+)
+
+
+def step_kernel(ndp, nneg, names, groups, *refs):
     refs = list(refs)
-    take = iter(refs)
-    towers = [[next(take) for _ in range(9)] for _ in range(2)]
-    loss_ref = next(take)
-    stats_ref = next(take)
-    gathered = [next(take) for _ in groups]
-    scratch = [[next(take) for _ in range(3)] for _ in range(2)]
-    names = ["packed", "c_in", "o1x", "l1x", "o1y", "l1y", "o2y", "l2y", "o2x", "l2x", "zs", "l3"]
-    bufs = [{name: next(take) for name in names} for _ in groups]
+    inputs = dict(zip(step_inputs, refs))
+    stats_ref, gathered = refs[13], refs[14:18]
+    (
+        sources, q_unit, n_unit, p_unit, towers, grads, pexp, logit,
+        q_land, n_land, meta_out, meta, rows, pid_out, pid_land, pid_col, w, den, dpart, dland, scaled,
+        q_out, q_part, q_in, c_out, c_in, own, out, lx, ly, l2y, l2x,
+        sx, sy, rn, sm, rm, sr, sl, rq, s_meta, r_meta, s_pid, r_pid, sd, rd, sq, rqs,
+        sc, rc, s1x, r1x, s1y, r1y, s2y, r2y, s2x, r2x, loaded,
+        scratch, bufs, stat_dp, stat_dp_land, stat_neg, stat_neg_land, ss, sr2, ts, tr,
+    ) = jax.tree.unflatten(names, refs[18:])
     for buf, ref in zip(bufs, gathered):
         buf["ag"] = ref
-    stat_dp, stat_dp_land, stat_neg, stat_neg_land = [next(take) for _ in range(4)]
-    sem_names = ["cs", "cr", "s1x", "r1x", "s1y", "r1y", "s2y", "r2y", "s2x", "r2x", "s3", "r3", "sg", "rg", "sh", "rh"]
-    for buf in bufs:
-        for name in sem_names:
-            buf[name] = next(take)
-    ss, sr, ts, tr = [next(take) for _ in range(4)]
-
     me_dp, me_neg = lax.axis_index("dp"), lax.axis_index("neg")
     line, nx = ndp // 2, nneg // 2
     place, side = me_dp // 2, lax.rem(me_dp, 2)
@@ -615,11 +616,380 @@
     far, other = 1 - side, 1 - me_core
     partner, mate = 2 * place + far, 2 * me_x + other
     f32, bf16 = jnp.float32, jnp.bfloat16
-    greet(ndp, nneg, me_dp, me_neg)
-    pending = []
+    rows_q, width = q_unit.shape
+    block = 2 * n_unit.shape[1]
+    half_n = block // 2
+    lanes = den.shape[2]
+    cuts = q_land.shape[1]
+    half_w = width // 2
+    blocks = nneg * 2
+    here = (me_x * 2 + side) * 2 + me_core
+
+    order = (
+        "item_first", "negative_features", "item_second", "item_third", "query_features", "query_first", "query_second",
+        "query_third", "positive_features", "negative_ids", "negative_counts", "positive_ids", "positive_counts",
+    )
+    item_features = sources["item_features"]
+    places = dict(sources)
+    places["negative_features"] = item_features.at[0:block]
+    places["positive_features"] = item_features.at[block : block + rows_q]
+    loads = {}
+    for i, name in enumerate(order):
+        loads[name] = pltpu.make_async_copy(inputs[name], places[name], loaded.at[i])
+        loads[name].start()
+
+    def along(k):
+        return lax.rem(me_x + k, nx)
+
+    def at_place(z):
+        return 2 * z + side
+
+    barrier = pltpu.get_barrier_semaphore()
+
+    def quad(k):
+        b = lax.rem(here + k, blocks)
+        return {"dp": 2 * place + lax.rem(b // 2, 2), "neg": 2 * (b // 4) + lax.rem(b, 2)}
+
+    for k in range(1, line):
+        for y in range(2):
+            target = 2 * lax.rem(place + k, line) + y
+            pl.semaphore_signal(barrier, inc=1, device_id={"dp": target}, device_id_type=pl.DeviceIdType.MESH)
+    for k in range(1, blocks):
+        pl.semaphore_signal(barrier, inc=1, device_id=quad(k), device_id_type=pl.DeviceIdType.MESH)
+
+    def slot(x, y, half):
+        return (x * 2 + y) * 2 + half
+
+    def piece(x, y, half):
+        return n_land.at[(x * 2 + y) * 2 + me_core, half]
+
+    def push(src, x, y, half, send_sems, index, axis, target):
+        return link(src, piece(x, y, half), (send_sems, rn), slot(x, y, half), axis, target, index)
+
+    def relay(src, x, y, half):
+        i = slot(x, y, half)
+        return link(src, piece(x, y, half), (sm, rm), i, "neg", mate)
+
+    def landed(x, y, half):
+        ref = piece(x, y, half)
+        link(ref, ref, (sy, rn), slot(x, y, half), "neg", mate, 0).wait_recv()
+
+    sends = []
 
     def go(copy):
         copy.start()
+        sends.append(copy)
+
+    def to_x(src, x, y, half, kind):
+        for k in range(1, nx):
+            go(push(src, x, y, half, sx, kind * nx + k, "neg", 2 * along(k) + me_core))
+
+    def to_y(src, x, y, half, index):
+        go(push(src, x, y, half, sy, index, "dp", partner))
+
+    def chain(slot_z, j, distance, sems, target):
+        src = q_unit.at[pl.ds(j * (rows_q // cuts), rows_q // cuts)] if distance == 0 else q_land.at[slot_z, j]
+        return link(src, q_land.at[slot_z, j], (sems, rq), slot_z * cuts + j, "dp", target, distance * cuts + j)
+
+    def right(distance, j):
+        return chain(place - distance, j, distance, sr, at_place(lax.rem(place + 1, line)))
+
+    def left(distance, j):
+        return chain(place + distance, j, distance, sl, at_place(lax.rem(place + line - 1, line)))
+
+    goes_right, goes_left = place < line - 1, place > 0
+
+    def q_step(distance):
+        for j in range(cuts):
+
+            @pl.when(place >= distance)
+            def _():
+                ref = q_land.at[place - distance, j]
+                link(ref, ref, (sr, rq), (place - distance) * cuts + j, "dp", partner, 0).wait_recv()
+                pl.when(goes_right)(lambda: right(distance, j).start())
+
+            @pl.when(place + distance < line)
+            def _():
+                ref = q_land.at[place + distance, j]
+                link(ref, ref, (sl, rq), (place + distance) * cuts + j, "dp", partner, 0).wait_recv()
+                pl.when(goes_left)(lambda: left(distance, j).start())
+
+    def forward(lo, count, features, first, second, third, saved, unit_ref):
+        act1, slope1, act2, slope2, emb = saved
+        span = slice(lo, lo + count)
+
+        def layer(source, weight, act, slope):
+            columns = weight.shape[1]
+            step = 512 if columns % 512 == 0 else columns
+            for c in range(0, columns, step):
+                pre = jnp.dot(source[span, :], weight[:, c : c + step], preferred_element_type=f32)
+                sigma = jax.nn.sigmoid(pre)
+                act[span, c : c + step] = (pre * sigma).astype(bf16)
+                slope[span, c : c + step] = sigma * (1.0 + pre * (1.0 - sigma))
+
+        layer(features, first, act1, slope1)
+        layer(act1, second, act2, slope2)
+        value = jnp.dot(act2[span, :], third[...], preferred_element_type=f32)
+        emb[span, :] = value
+        inv_norm = lax.rsqrt(jnp.sum(value * value, axis=1, keepdims=True) + 1.0)
+        unit_ref[...] = (value * inv_norm).astype(bf16)
+
+    item_weights = tuple(sources[name] for name in ("item_first", "item_second", "item_third"))
+    query_weights = tuple(sources[name] for name in ("query_first", "query_second", "query_third"))
+    for name in ("negative_ids", "negative_counts", "positive_ids", "item_first", "negative_features", "item_second", "item_third"):
+        loads[name].wait()
+
+    def own_ids(ref, index, count):
+        return ref[:, pl.ds(pl.multiple_of(index * count, count), count)]
+
+    meta_out[0:1, :] = own_ids(sources["negative_ids"], me_dp, block)
+    meta_out[1:2, :] = own_ids(sources["negative_counts"], me_dp, block)
+    pid_out[...] = own_ids(sources["positive_ids"], me_neg, rows_q)
+    meta[here] = meta_out[...]
+    pid_land[place] = pid_out[...]
+    forward(0, half_n, item_features, *item_weights, towers[1], n_unit.at[0])
+    pl.semaphore_wait(barrier, 2 * (line - 1) + (blocks - 1))
+    for k in range(1, blocks):
+        copy = pltpu.make_async_remote_copy(
+            src_ref=meta_out, dst_ref=meta.at[here], send_sem=s_meta.at[k], recv_sem=r_meta.at[here],
+            device_id=quad(k), device_id_type=pl.DeviceIdType.MESH,
+        )
+        go(copy)
+    for k in range(1, line):
+        z = lax.rem(place + k, line)
+        go(link(pid_out, pid_land.at[place], (s_pid, r_pid), place, "dp", at_place(z), k))
+    n_first, n_second = n_unit.at[0], n_unit.at[1]
+    to_x(n_first, me_x, side, 0, 0)
+    to_y(n_first, me_x, side, 0, 1)
+    go(relay(n_first, me_x, side, 0))
+    n_land[here, 0] = n_unit[0]
+    for name in ("query_features", "query_first", "query_second", "query_third"):
+        loads[name].wait()
+    forward(0, rows_q, sources["query_features"], *query_weights, towers[0], q_unit)
+    for j in range(cuts):
+        pl.when(goes_right)(lambda j=j: right(0, j).start())
+        pl.when(goes_left)(lambda j=j: left(0, j).start())
+    for j in range(cuts):
+        q_land[place, j] = q_unit[pl.ds(j * (rows_q // cuts), rows_q // cuts), :]
+    forward(half_n, half_n, item_features, *item_weights, towers[1], n_unit.at[1])
+    to_y(n_second, me_x, side, 1, 0)
+    to_x(n_second, me_x, side, 1, 1)
+    go(relay(n_second, me_x, side, 1))
+    n_land[here, 1] = n_unit[1]
+    loads["positive_features"].wait()
+    loads["positive_counts"].wait()
+    forward(block, rows_q, item_features, *item_weights, towers[1], p_unit)
+    product = q_unit[...].astype(f32) * p_unit[...].astype(f32)
+    logit[...] = jnp.sum(product.T, axis=0, keepdims=True) * inv_temp - jnp.log(sources["positive_counts"][...].astype(f32))
+    pexp[...] = jnp.exp(logit[...])
+
+    for k in range(1, nx):
+        x = along(k)
+        landed(x, side, 0)
+        to_y(piece(x, side, 0), x, side, 0, 1 + k)
+        go(relay(piece(x, side, 0), x, side, 0))
+    for k in range(1, blocks):
+        b = lax.rem(here + k, blocks)
+        link(meta.at[b], meta.at[b], (s_meta, r_meta), b, "neg", mate).wait_recv()
+    for k in range(1, line):
+        z = lax.rem(place + k, line)
+        link(pid_land.at[z], pid_land.at[z], (s_pid, r_pid), z, "dp", partner).wait_recv()
+    for b in range(blocks):
+        rows[b, 0:1, :] = meta[b, 0:1, :].astype(f32)
+        rows[b, 1:2, :] = jnp.log2(meta[b, 1:2, :].astype(f32))
+    for z in range(line):
+        pid_col[z] = jnp.broadcast_to(pid_land[z].astype(f32), (lanes, rows_q)).T
+        den[z] = jnp.zeros((rows_q, lanes), f32)
+
+    def unit(b, z):
+        dots = contract_cols(q_land[z].reshape(rows_q, width), n_land[b].reshape(block, width))
+        value = jnp.exp2(dots * (inv_temp * log2_e) - rows[b, 1:2, :])
+        ids = jnp.concatenate([pid_col[z]] * (block // lanes), axis=1)
+        value = jnp.where(ids != rows[b, 0:1, :], value, 0.0)
+        w[b, z] = value.astype(jnp.bfloat16)
+        total = den[z]
+        for c in range(0, block, lanes):
+            total = total + value[:, c : c + lanes]
+        den[z] = total
+
+    def relayed(x, y):
+        for half in range(2):
+            ref = n_land.at[(x * 2 + y) * 2 + other, half]
+            link(ref, ref, (sm, rm), slot(x, y, half), "neg", mate).wait_recv()
+
+    def both_cores(x, y):
+        return [(x * 2 + y) * 2 + core for core in range(2)]
+
+    near_blocks = both_cores(me_x, side)
+    mid_blocks = both_cores(me_x, far)
+    far_blocks = []
+    for k in range(1, nx):
+        mid_blocks = mid_blocks + both_cores(along(k), side)
+        far_blocks = far_blocks + both_cores(along(k), far)
+
+    def units(lo, hi, chosen):
+        def body(z, carry):
+            for b in chosen:
+                unit(b, z)
+            return carry
+
+        lax.fori_loop(jnp.maximum(lo, 0), jnp.minimum(hi, line), body, 0)
+
+    relayed(me_x, side)
+    units(place, place + 1, near_blocks)
+    q_step(1)
+    units(place - 1, place, near_blocks)
+    units(place + 1, place + 2, near_blocks)
+    landed(me_x, far, 1)
+    to_x(piece(me_x, far, 1), me_x, far, 1, 2)
+    go(relay(piece(me_x, far, 1), me_x, far, 1))
+    landed(me_x, far, 0)
+    go(relay(piece(me_x, far, 0), me_x, far, 0))
+    for k in range(1, nx):
+        x = along(k)
+        landed(x, side, 1)
+        go(relay(piece(x, side, 1), x, side, 1))
+    q_step(2)
+    relayed(me_x, far)
+    for k in range(1, nx):
+        relayed(along(k), side)
+    units(place - 1, place + 2, mid_blocks)
+    units(place - 2, place - 1, near_blocks + mid_blocks)
+    units(place + 2, place + 3, near_blocks + mid_blocks)
+    for half in range(2):
+        for k in range(1, nx):
+            x = along(k)
+            landed(x, far, half)
+            go(relay(piece(x, far, half), x, far, half))
+    for distance in range(3, line):
+        q_step(distance)
+    for k in range(1, nx):
+        relayed(along(k), far)
+    units(place - 2, place + 3, far_blocks)
+    units(0, place - 2, near_blocks + mid_blocks + far_blocks)
+    units(place + 3, line, near_blocks + mid_blocks + far_blocks)
+    for z in range(line):
+        dpart[z] = jnp.sum(den[z].T, axis=0, keepdims=True)
+    dpart[place] = dpart[place] + pexp[...]
+    for k in range(1, line):
+        z = lax.rem(place + k, line)
+        go(link(dpart, dland.at[place], (sd, rd), place, "dp", at_place(z), k))
+
+    def q_block(z):
+        if block % 128 == 0:
+            left_side = jnp.concatenate([w[b, z] for b in range(blocks)], axis=1)
+            return jnp.dot(
+                left_side, n_land[...].reshape(blocks * block, width), preferred_element_type=jnp.float32
+            )
+        total = jnp.zeros((rows_q, width), jnp.float32)
+        for b in range(blocks):
+            total = total + jnp.dot(w[b, z], n_land[b].reshape(block, width), preferred_element_type=jnp.float32)
+        return total
+
+    def q_send(k, z):
+        return link(q_out.at[z], q_in.at[place], (sq, rqs), place, "dp", at_place(z), k)
+
+    def q_push(k, carry):
+        z = lax.rem(place + k, line)
+        q_out[z] = q_block(z).astype(jnp.bfloat16)
+        q_send(k, z).start()
+        return carry
+
+    lax.fori_loop(1, line, q_push, 0)
+    q_part[...] = q_block(place)
+    total = dpart[...]
+    for k in range(1, line):
+        z = lax.rem(place + k, line)
+        link(dland.at[z], dland.at[z], (sd, rd), z, "dp", partner).wait_recv()
+        total = total + dland[z]
+    dpart2 = 1.0 / total
+    for z in range(line):
+        q_t = q_land[z].reshape(rows_q, width).astype(jnp.float32).T
+        scaled[:, z * rows_q : (z + 1) * rows_q] = (q_t * dpart2[z]).astype(jnp.bfloat16)
+    def dest(i):
+        x = lax.rem(me_x + 1 + i // 2, nx)
+        y = lax.rem(side + 1 + lax.rem(i, 2), 2)
+        return x, y
+
+    def part(x, y, core):
+        return jnp.dot(
+            scaled[...], w[(x * 2 + y) * 2 + core].reshape(line * rows_q, block), preferred_element_type=jnp.float32
+        )
+
+    def c_send(i):
+        x, y = dest(i)
+        return link(c_out.at[x, y], c_in.at[x, y], (sc, rc), x * 2 + y, "neg", mate)
+
+    def far_step(i, carry):
+        x, y = dest(i)
+        c_out[x, y] = part(x, y, other).astype(jnp.bfloat16).reshape(2, half_w, block)
+        c_send(i).start()
+        return carry
+
+    def send_1x(i):
+        x, y = dest(i)
+        return link(out.at[x, y, 0], lx.at[me_x, y], (s1x, r1x), me_x * 2 + y, "neg", 2 * x + me_core, x * 2 + y)
+
+    def send_1y(i):
+        x, y = dest(i)
+        return link(out.at[x, y, 1], ly.at[x], (s1y, r1y), x, "dp", partner)
+
+    def own_step(i, carry):
+        x, y = dest(i)
+        value = part(x, y, me_core).reshape(2, half_w, block)
+        link(c_in.at[x, y], c_in.at[x, y], (sc, rc), x * 2 + y, "neg", mate).wait_recv()
+        value = value + c_in[x, y].astype(jnp.float32)
+        own[x, y] = value
+
+        @pl.when(i < 2 * (nx - 1))
+        def _():
+            out[x, y, 0] = value[0].astype(jnp.bfloat16)
+            send_1x(i).start()
+
+        @pl.when(lax.rem(i, 2) == 0)
+        def _():
+            out[x, y, 1] = value[1].astype(jnp.bfloat16)
+            send_1y(i).start()
+
+        return carry
+
+    lax.fori_loop(0, 2 * nx, far_step, 0)
+    lax.fori_loop(0, 2 * nx, own_step, 0)
+    value = own[me_x, far, 0]
+    for k in range(1, nx):
+        x = along(k)
+        ref = lx.at[x, far]
+        link(ref, ref, (s1x, r1x), x * 2 + far, "neg", mate).wait_recv()
+        value = value + lx[x, far].astype(jnp.float32)
+    out[me_x, far, 0] = value.astype(jnp.bfloat16)
+    go(link(out.at[me_x, far, 0], l2y, (s2y, r2y), 0, "dp", partner))
+    for k in range(1, nx):
+        x = along(k)
+        link(ly.at[x], ly.at[x], (s1y, r1y), x, "dp", partner).wait_recv()
+        out[x, side, 1] = (own[x, side, 1] + ly[x].astype(jnp.float32)).astype(jnp.bfloat16)
+        go(link(out.at[x, side, 1], l2x.at[me_x], (s2x, r2x), me_x, "neg", 2 * x + me_core, x))
+    denom = dpart[place]
+    for k in range(1, line):
+        denom = denom + dland[lax.rem(place + k, line), place]
+    loss_part = jnp.sum(jnp.log(denom) - logit[...])
+
+    def to_columns(row):
+        column = jnp.broadcast_to(row, (lanes, rows_q)).T
+        return jnp.concatenate([column] * (width // lanes), axis=1)
+
+    slope_columns = to_columns(pexp[...] / denom - 1.0) * inv_temp
+    grads[1][block : block + rows_q, :] = slope_columns * q_unit[...].astype(f32)
+    result = q_part[...]
+    for k in range(1, line):
+        z = lax.rem(place + k, line)
+        link(q_in.at[z], q_in.at[z], (sq, rqs), z, "dp", partner).wait_recv()
+        result = result + q_in[z].astype(jnp.float32)
+    grads[0][...] = result * (to_columns(1.0 / denom) * inv_temp) + slope_columns * p_unit[...].astype(f32)
+
+    pending = []
+
+    def queue(copy):
+        copy.start()
         pending.append(copy)
 
     def x_of(k):
@@ -633,6 +1003,11 @@
 
     def arrived(ref, sem_array, index):
         link(ref, ref, (sem_array, sem_array), index, "neg", mate).wait_recv()
+
+    steps = [
+        (sources["query_features"], *towers[0], grads[0], sources["query_second"], sources["query_third"]),
+        (item_features, *towers[1], grads[1], sources["item_second"], sources["item_third"]),
+    ]
 
     def store(group, offset, value, dp, hg):
         packed = bufs[group]["packed"]
@@ -667,7 +1042,7 @@
         lax.fori_loop(0, count // step, wrapped, 0)
 
     def embed_stage(t):
-        feat, act1, slope1, act2, slope2, emb_ref, grad_ref, second, third = towers[t]
+        feat, act1, slope1, act2, slope2, emb_ref, grad_ref, second, third = steps[t]
         eg, s2, s1 = scratch[t]
 
         def body(rows):
@@ -681,13 +1056,13 @@
         row_loop(feat.shape[0], body)
 
     def second_stage(t, group):
-        feat, act1, slope1, act2, slope2, emb_ref, grad_ref, second, third = towers[t]
+        feat, act1, slope1, act2, slope2, emb_ref, grad_ref, second, third = steps[t]
         eg, s2, s1 = scratch[t]
         offset = weight_grad(group, 0, act2, eg)
         weight_grad(group, offset, act1, s2)
 
     def slope_stage(t):
-        feat, act1, slope1, act2, slope2, emb_ref, grad_ref, second, third = towers[t]
+        feat, act1, slope1, act2, slope2, emb_ref, grad_ref, second, third = steps[t]
         eg, s2, s1 = scratch[t]
         columns = second.shape[0]
 
@@ -699,11 +1074,11 @@
         row_loop(feat.shape[0], body)
 
     def first_stage(t, group):
-        weight_grad(group, 0, towers[t][0], scratch[t][2])
+        weight_grad(group, 0, steps[t][0], scratch[t][2])
 
     def stage0(g):
         b = bufs[g]
-        go(link(b["packed"].at[other], b["c_in"], (b["cs"], b["cr"]), 0, "neg", mate))
+        queue(link(b["packed"].at[other], b["c_in"], (b["cs"], b["cr"]), 0, "neg", mate))
 
     def base(b, dp, x, lo, hi):
         return b["packed"][me_core, dp, x, lo:hi, :].astype(f32) + b["c_in"][dp, x, lo:hi, :].astype(f32)
@@ -725,14 +1100,14 @@
                 b["o1x"][x, dp] = base(b, dp, x, 0, r1).astype(bf16)
 
             loop(ndp, body)
-            go(link(b["o1x"].at[x], b["l1x"].at[me_x], (b["s1x"], b["r1x"]), me_x, "neg", same_core(x), x))
+            queue(link(b["o1x"].at[x], b["l1x"].at[me_x], (b["s1x"], b["r1x"]), me_x, "neg", same_core(x), x))
 
         def body_y(z):
             for x in range(nx):
                 b["o1y"][z, x] = base(b, 2 * z + far, x, r1, r).astype(bf16)
 
         loop(line, body_y)
-        go(link(b["o1y"], b["l1y"], (b["s1y"], b["r1y"]), 0, "dp", partner))
+        queue(link(b["o1y"], b["l1y"], (b["s1y"], b["r1y"]), 0, "dp", partner))
 
     def low(b, dp, r1):
         value = base(b, dp, me_x, 0, r1)
@@ -750,7 +1125,7 @@
             b["o2y"][z] = low(b, 2 * z + far, r1).astype(bf16)
 
         loop(line, body)
-        go(link(b["o2y"], b["l2y"], (b["s2y"], b["r2y"]), 0, "dp", partner))
+        queue(link(b["o2y"], b["l2y"], (b["s2y"], b["r2y"]), 0, "dp", partner))
         arrived(b["l1y"], b["r1y"], 0)
         for k in range(1, nx):
             x = x_of(k)
@@ -760,7 +1135,7 @@
                 b["o2x"][x, z] = value.astype(bf16)
 
             loop(line, body_x)
-            go(link(b["o2x"].at[x], b["l2x"].at[me_x], (b["s2x"], b["r2x"]), me_x, "neg", same_core(x), x))
+            queue(link(b["o2x"].at[x], b["l2x"].at[me_x], (b["s2x"], b["r2x"]), me_x, "neg", same_core(x), x))
 
     def stage3(g):
         b, (r1, r) = bufs[g], groups[g]
@@ -780,7 +1155,7 @@
         loop(line, body)
         for k in range(1, line):
             z = z_of(k)
-            go(link(b["zs"].at[z], b["l3"].at[place], (b["s3"], b["r3"]), place, "dp", 2 * z + side, z))
+            queue(link(b["zs"].at[z], b["l3"].at[place], (b["s3"], b["r3"]), place, "dp", 2 * z + side, z))
 
     squares = []
 
@@ -797,8 +1172,8 @@
         mine = b["ag"].at[me_neg]
         for k in range(1, nx):
             x = x_of(k)
-            go(link(mine, mine, (b["sg"], b["rg"]), me_x, "neg", same_core(x), x))
-        go(link(mine, mine, (b["sh"], b["rh"]), me_x, "neg", mate))
+            queue(link(mine, mine, (b["sg"], b["rg"]), me_x, "neg", same_core(x), x))
+        queue(link(mine, mine, (b["sh"], b["rh"]), me_x, "neg", mate))
 
     def stage5(g):
         b = bufs[g]
@@ -806,7 +1181,7 @@
             x = x_of(k)
             ref = b["ag"].at[same_core(x)]
             arrived(ref, b["rg"], x)
-            go(link(ref, ref, (b["sh"], b["rh"]), x, "neg", mate))
+            queue(link(ref, ref, (b["sh"], b["rh"]), x, "neg", mate))
 
     def stage6(g):
         b = bufs[g]
@@ -819,6 +1194,23 @@
     slope_stage(0)
     first_stage(0, 1)
     stage0(1)
+    n_low = own[me_x, side, 0]
+    for k in range(1, nx):
+        x = along(k)
+        ref = lx.at[x, side]
+        link(ref, ref, (s1x, r1x), x * 2 + side, "neg", mate).wait_recv()
+        n_low = n_low + lx[x, side].astype(jnp.float32)
+    link(ly.at[me_x], ly.at[me_x], (s1y, r1y), me_x, "dp", partner).wait_recv()
+    n_high = own[me_x, side, 1] + ly[me_x].astype(jnp.float32)
+    link(l2y, l2y, (s2y, r2y), 0, "dp", partner).wait_recv()
+    n_low = n_low + l2y[...].astype(jnp.float32)
+    for k in range(1, nx):
+        x = along(k)
+        link(l2x.at[x], l2x.at[x], (s2x, r2x), x, "neg", mate).wait_recv()
+        n_high = n_high + l2x[x].astype(jnp.float32)
+
+    grads[1][0:block, 0:half_w] = n_low.T * inv_temp
+    grads[1][0:block, half_w:width] = n_high.T * inv_temp
     stage1(0)
     embed_stage(1)
     stage1(1)
@@ -843,8 +1235,8 @@
     stage4(3)
     total_squares = squares[0] + squares[1] + squares[2] + squares[3]
     lane = lax.broadcasted_iota(jnp.int32, (8, 128), 1)
-    stat_dp[...] = jnp.where(lane == 0, total_squares, loss_ref[0])
-    stat_copies = share("dp", ndp, me_dp, lambda t: stat_dp, stat_dp_land, ss, sr)
+    stat_dp[...] = jnp.where(lane == 0, total_squares, loss_part)
+    stat_copies = share("dp", ndp, me_dp, lambda t: stat_dp, stat_dp_land, ss, sr2)
     for g in range(4):
         stage5(g)
     finish(stat_copies)
@@ -864,47 +1256,123 @@
         copy.wait_send()
 
 
-def fused_backward(ndp, nneg, towers, loss_part, own_queries):
+    for copy in sends:
+        copy.wait_send()
+    for distance in range(line):
+        for j in range(cuts):
+            if distance < line - 1:
+                pl.when((place >= distance) & goes_right)(lambda: right(distance, j).wait_send())
+                pl.when((place + distance < line) & goes_left)(lambda: left(distance, j).wait_send())
+    for k in range(1, line):
+        q_send(k, lax.rem(place + k, line)).wait_send()
+    for i in range(2 * nx):
+        c_send(i).wait_send()
+        if i < 2 * (nx - 1):
+            send_1x(i).wait_send()
+        if i % 2 == 0:
+            send_1y(i).wait_send()
+
+
+def fused_step(ndp, nneg, arguments):
     line, nx = ndp // 2, nneg // 2
-    bf16, f32 = jnp.bfloat16, jnp.float32
-    groups, outs, scratch, buffers, semaphores = [], [], [], [], []
-    for feat, act1, slope1, act2, slope2, emb, grad, second, third in towers:
-        rows, fin = feat.shape
-        h1, h2, width = act1.shape[1], act2.shape[1], emb.shape[1]
+    bf16, f32, i32 = jnp.bfloat16, jnp.float32, jnp.int32
+    named = dict(zip(step_inputs, arguments))
+    fin, h1 = named["item_first"].shape
+    h2, width = named["item_third"].shape
+    own_rows, block = named["query_features"].shape[0], named["negative_features"].shape[0]
+    blocks, cuts, lanes = 2 * nneg, 2, 128
+    rows_half = (width // 2, block)
+    sources = {"item_features": pltpu.VMEM((block + own_rows, fin), bf16)}
+    for name, value in named.items():
+        if name not in ("positive_features", "negative_features"):
+            sources[name] = pltpu.VMEM(value.shape, value.dtype)
+    counts = (own_rows, block + own_rows)
+    towers = [
+        [
+            pltpu.VMEM((count, h1), bf16), pltpu.VMEM((count, h1), f32), pltpu.VMEM((count, h2), bf16),
+            pltpu.VMEM((count, h2), f32), pltpu.VMEM((count, width), f32),
+        ]
+        for count in counts
+    ]
+    scratch = [
+        [pltpu.VMEM((count, width), bf16), pltpu.VMEM((count, h2), bf16), pltpu.VMEM((count, h1), bf16)]
+        for count in counts
+    ]
+    row = pltpu.VMEM((1, own_rows), f32)
+    score = [
+        pltpu.VMEM((line, cuts, own_rows // cuts, width), bf16),
+        pltpu.VMEM((blocks, 2, block // 2, width), bf16),
+        pltpu.VMEM((2, block), i32),
+        pltpu.VMEM((blocks, 2, block), i32),
+        pltpu.VMEM((blocks, 2, block), f32),
+        pltpu.VMEM((1, own_rows), i32),
+        pltpu.VMEM((line, 1, own_rows), i32),
+        pltpu.VMEM((line, own_rows, lanes), f32),
+        pltpu.VMEM((blocks, line, own_rows, block), bf16),
+        pltpu.VMEM((line, own_rows, lanes), f32),
+        pltpu.VMEM((line, 1, own_rows), f32),
+        pltpu.VMEM((line, line, 1, own_rows), f32),
+        pltpu.VMEM((width, line * own_rows), bf16),
+        pltpu.VMEM((line, own_rows, width), bf16),
+        pltpu.VMEM((own_rows, width), f32),
+        pltpu.VMEM((line, own_rows, width), bf16),
+        pltpu.VMEM((nx, 2, 2) + rows_half, bf16),
+        pltpu.VMEM((nx, 2, 2) + rows_half, bf16),
+        pltpu.VMEM((nx, 2, 2) + rows_half, f32),
+        pltpu.VMEM((nx, 2, 2) + rows_half, bf16),
+        pltpu.VMEM((nx, 2) + rows_half, bf16),
+        pltpu.VMEM((nx,) + rows_half, bf16),
+        pltpu.VMEM(rows_half, bf16),
+        pltpu.VMEM((nx,) + rows_half, bf16),
+    ] + sems(
+        3 * nx, 1 + nx, 4 * nx, 4 * nx, 4 * nx, line * cuts, line * cuts, line * cuts,
+        blocks, blocks, line, line, line, line, line, line,
+        2 * nx, 2 * nx, 2 * nx, 2 * nx, nx, nx, 1, 1, nx, nx, len(step_inputs),
+    )
+    groups, outs, bufs = [], [], []
+    for _ in counts:
         for height, columns in ((fin, h1), (h1, h2), (h2, width)):
             outs.append(jax.ShapeDtypeStruct((height // ndp, columns), f32))
         both = h2 // (ndp * nneg) * (width // pack_columns) + h1 // (ndp * nneg) * (h2 // pack_columns)
         alone = fin // (ndp * nneg) * (h1 // pack_columns)
         for r in (both, alone):
-            groups.append((r * 4 // 9 // 16 * 16, r))
-        scratch += [pltpu.VMEM((rows, width), bf16), pltpu.VMEM((rows, h2), bf16), pltpu.VMEM((rows, h1), bf16)]
+            groups.append((max((r * 4 + 72) // 144, 1) * 16, r))
+    c = pack_columns
+    sem_names = ["cs", "cr", "s1x", "r1x", "s1y", "r1y", "s2y", "r2y", "s2x", "r2x", "s3", "r3", "sg", "rg", "sh", "rh"]
     for r1, r in groups:
-        r2, c = r - r1, pack_columns
-        for shape in (
-            (2, ndp, nx, r, c), (ndp, nx, r, c), (nx, ndp, r1, c), (nx, ndp, r1, c), (line, nx, r2, c),
-            (line, nx, r2, c), (line, r1, c), (line, r1, c), (nx, line, r2, c), (nx, line, r2, c),
-            (line, r, c), (line, r, c),
-        ):
-            buffers.append(pltpu.VMEM(shape, bf16))
-        semaphores += sems(1, 1, nx, nx, 1, 1, 1, 1, nx, nx, line, line, nx, nx, nx, nx)
-    stat = [pltpu.VMEM((8, 128), f32), pltpu.VMEM((ndp, 8, 128), f32), pltpu.VMEM((8, 128), f32), pltpu.VMEM((nneg, 8, 128), f32)]
-    operands = [operand for tower in towers for operand in tower]
+        r2 = r - r1
+        shapes = dict(
+            packed=(2, ndp, nx, r, c), c_in=(ndp, nx, r, c), o1x=(nx, ndp, r1, c), l1x=(nx, ndp, r1, c),
+            o1y=(line, nx, r2, c), l1y=(line, nx, r2, c), o2y=(line, r1, c), l2y=(line, r1, c),
+            o2x=(nx, line, r2, c), l2x=(nx, line, r2, c), zs=(line, r, c), l3=(line, r, c),
+        )
+        buf = {name: pltpu.VMEM(shape, bf16) for name, shape in shapes.items()}
+        buf.update(zip(sem_names, sems(1, 1, nx, nx, 1, 1, 1, 1, nx, nx, line, line, nx, nx, nx, nx)))
+        bufs.append(buf)
+    tree = (
+        sources, pltpu.VMEM((own_rows, width), bf16), pltpu.VMEM((2, block // 2, width), bf16),
+        pltpu.VMEM((own_rows, width), bf16), towers, [pltpu.VMEM((count, width), f32) for count in counts], row, row,
+        *score, scratch, bufs,
+        pltpu.VMEM((8, 128), f32), pltpu.VMEM((ndp, 8, 128), f32), pltpu.VMEM((8, 128), f32), pltpu.VMEM((nneg, 8, 128), f32),
+        *sems(ndp, ndp, nneg, nneg),
+    )
+    leaves, names = jax.tree.flatten(tree)
+    any_space = pl.BlockSpec(memory_space=pl.ANY)
     stats, *gathered = pl.pallas_call(
-        lambda *refs: backward_kernel(ndp, nneg, tuple(groups), *refs),
+        functools.partial(step_kernel, ndp, nneg, names, tuple(groups)),
         out_shape=(
             jax.ShapeDtypeStruct((8, 128), f32),
             *[jax.ShapeDtypeStruct((nneg, r, pack_columns), bf16) for _, r in groups],
         ),
-        in_specs=[vmem] * len(operands) + [pl.BlockSpec(memory_space=pltpu.SMEM)],
+        in_specs=[any_space] * len(arguments),
         out_specs=(vmem,) * 5,
-        scratch_shapes=scratch + buffers + stat + semaphores + sems(ndp, ndp, nneg, nneg),
+        scratch_shapes=leaves,
         compiler_params=pltpu.CompilerParams(
-            collective_id=1, has_side_effects=True, vmem_limit_bytes=40 * 1024 * 1024
+            collective_id=1, has_side_effects=True, vmem_limit_bytes=67043328
         ),
-    )(*operands, loss_part.reshape(1))
-    any_space = pl.BlockSpec(memory_space=pl.ANY)
+    )(*arguments)
     mean_loss, *clipped = pl.pallas_call(
-        functools.partial(finish_kernel, nneg, own_queries * ndp * nneg),
+        functools.partial(finish_kernel, nneg, own_rows * ndp * nneg),
         out_shape=(jax.ShapeDtypeStruct((1,), f32), *outs),
         in_specs=[vmem] * 5,
         out_specs=(pl.BlockSpec(memory_space=pltpu.SMEM), *([any_space] * 6)),
@@ -954,6 +1422,19 @@
     item_third,
 ):
     own_rows = query_features.shape[0]
+    ndp, nneg = lax.axis_size("dp"), lax.axis_size("neg")
+    heights = (query_first.shape[0], query_second.shape[0], query_third.shape[0])
+    tiled = all(height % (16 * ndp * nneg) == 0 for height in heights)
+    if tiled and own_rows % 256 == 0 and negative_features.shape[0] % 256 == 0:
+        return fused_step(
+            ndp,
+            nneg,
+            (
+                query_features, positive_features, negative_features, positive_ids.reshape(1, -1),
+                positive_counts.reshape(1, -1), negative_ids.reshape(1, -1), negative_counts.reshape(1, -1),
+                query_first, query_second, query_third, item_first, item_second, item_third,
+            ),
+        )
     query_saved, query_unit = tower_forward(query_features, query_first, query_second, query_third)
     item_features = jnp.concatenate([positive_features, negative_features], axis=0)
     item_saved, item_unit = tower_forward(item_features, item_first, item_second, item_third)
@@ -1031,16 +1512,6 @@
     ) * inv_temp
     positive_grad = positive_slope[:, None] * query_unit.astype(jnp.float32) * inv_temp
     item_grad = jnp.concatenate([positive_grad, negative_sum * inv_temp], axis=0)
-    heights = (query_first.shape[0], query_second.shape[0], query_third.shape[0])
-    if all(height % (16 * ndp * nneg) == 0 for height in heights):
-        towers = [
-            (features, saved[1], saved[0], saved[3], saved[2], saved[4], grad, second, third)
-            for features, saved, grad, second, third in (
-                (query_features, query_saved, query_grad, query_second, query_third),
-                (item_features, item_saved, item_grad, item_second, item_third),
-            )
-        ]
-        return fused_backward(ndp, nneg, towers, loss_part, own_rows)
     query_grads = tower_backward(query_features, query_second, query_third, query_saved, query_grad)
     item_grads = tower_backward(item_features, item_second, item_third, item_saved, item_grad)
     gradients = query_grads + item_grads

time: 128 us -> 84.7 us (0.66)
  local copies, waits for them, and re-layouts: 19.5 us -> 0 us
  matrix products: 9.89 us -> 0 us
  Pallas kernels: 93.1 us -> 83.8 us
  other arithmetic: 4.05 us -> 0 us
    unnamed x63 -> x0, local copies, waits for them, and re-layouts: 16.2 us -> none
    dot_general x6 -> x0, matrix products: 9.89 us -> none  [the longest x2 5.11 us: tower_forward(): first_pre = jnp.dot(features, first, preferred_element_type=jnp.float32)]
    pallas_call x3 -> x2, Pallas kernels: 93.1 us -> 83.8 us  [the longest x1 81 us: fused_step(): pl.pallas_call(functools.partial(step_kernel, ndp, nneg, names, tuple(gro...]
    mul x1 -> x0, local copies, waits for them, and re-layouts: 2.05 us -> none  [per_device(): negative_sum * inv_temp]
    mul x2 -> x0, other arithmetic: 1.79 us -> none  [the longest x1 0.95 us: per_device(): positive_slope[:, None] * query_unit.astype(jnp.float32) * inv_temp]
where the time goes in v4:
time: 84.7 us; the launch traced here: 84.6 us
  Pallas kernels  83.8 us (99%)
    pallas_call x1, Pallas kernels, fused_step(): pl.pallas_call(functools.partial(step_kernel, ndp, nneg, names, tuple(gro...  81 us
    pallas_call x1, Pallas kernels, fused_step(): pl.pallas_call(functools.partial(finish_kernel, nneg, own_rows * ndp * nn...  2.76 us

profile of v4, /device:TPU:0, one launch (start us, length us, event | category | flops | bytes accessed | tf_op | source)
XLA Modules:
  0.0 84.6 jit_solution(3416862419428417727)
XLA Ops:
  0.6 81.0 %shard_map.180 = (f32[8,128]{1,0:T(8,128)}, bf16[4,80,256]{2,1,0:T(8,128)(2,1)}, bf16[4,64,256]{2,1,0:T(8,128)(2,1)}, bf16[4,80,256]{2,1,0:T(8,128)(2,1)}, bf16[4,64,256]{2,1,0:T(8,128)(2,1)}) custom-call(bf16[256,512]{1,0:T(8,128)(2,1)} %refs_0_.1, bf16[256,512]{1,0:T(8,128)(2,1)} %refs_1_.1, bf16[512,512]{1,0:T(8,128)(2,1)} %refs_2_.1, s32[1,1024]{1,0:T(1,128)} %bitcast.7, ...), custom_call_target="tpu_custom_call" | custom-call | tf_op jit(solution)/shard_map/pallas_call | solution.py:1361
  81.7 2.8 %shard_map.181 = (f32[1]{0:T(128)}, f32[64,1024]{1,0:T(8,128)}, f32[128,512]{1,0:T(8,128)}, f32[64,256]{1,0:T(8,128)}, f32[64,1024]{1,0:T(8,128)}, /*index=5*/f32[128,512]{1,0:T(8,128)}, f32[64,256]{1,0:T(8,128)}) custom-call(f32[8,128]{1,0:T(8,128)} %get-tuple-element.19.stats_ref, bf16[4,80,256]{2,1,0:T(8,128)(2,1)} %get-tuple-element.20.refs_0_, ...), custom_call_target="tpu_custom_call" | custom-call | tf_op jit(solution)/shard_map/pallas_call | solution.py:1374

commit v5 on v4

--- a/solution.py
+++ b/solution.py
@@ -605,10 +605,8 @@
         q_out, q_part, q_in, c_out, c_in, own, out, lx, ly, l2y, l2x,
         sx, sy, rn, sm, rm, sr, sl, rq, s_meta, r_meta, s_pid, r_pid, sd, rd, sq, rqs,
         sc, rc, s1x, r1x, s1y, r1y, s2y, r2y, s2x, r2x, loaded,
-        scratch, bufs, stat_dp, stat_dp_land, stat_neg, stat_neg_land, ss, sr2, ts, tr,
+        scratch, bufs, stat, stat_land, ss, sr2, left_sems,
     ) = jax.tree.unflatten(names, refs[18:])
-    for buf, ref in zip(bufs, gathered):
-        buf["ag"] = ref
     me_dp, me_neg = lax.axis_index("dp"), lax.axis_index("neg")
     line, nx = ndp // 2, nneg // 2
     place, side = me_dp // 2, lax.rem(me_dp, 2)
@@ -626,8 +624,8 @@
     here = (me_x * 2 + side) * 2 + me_core
 
     order = (
-        "item_first", "negative_features", "item_second", "item_third", "query_features", "query_first", "query_second",
-        "query_third", "positive_features", "negative_ids", "negative_counts", "positive_ids", "positive_counts",
+        "query_features", "query_first", "query_second", "query_third", "negative_features", "item_first", "item_second",
+        "item_third", "negative_ids", "negative_counts", "positive_ids", "positive_features", "positive_counts",
     )
     item_features = sources["item_features"]
     places = dict(sources)
@@ -650,12 +648,16 @@
         b = lax.rem(here + k, blocks)
         return {"dp": 2 * place + lax.rem(b // 2, 2), "neg": 2 * (b // 4) + lax.rem(b, 2)}
 
-    for k in range(1, line):
-        for y in range(2):
-            target = 2 * lax.rem(place + k, line) + y
-            pl.semaphore_signal(barrier, inc=1, device_id={"dp": target}, device_id_type=pl.DeviceIdType.MESH)
-    for k in range(1, blocks):
-        pl.semaphore_signal(barrier, inc=1, device_id=quad(k), device_id_type=pl.DeviceIdType.MESH)
+    devices = ndp * nneg
+    me = me_dp * nneg + me_neg
+
+    def everyone(n):
+        target = lax.rem(me + n, devices)
+        return target // nneg, lax.rem(target, nneg)
+
+    for n in range(1, devices):
+        dp, neg = everyone(n)
+        pl.semaphore_signal(barrier, inc=1, device_id={"dp": dp, "neg": neg}, device_id_type=pl.DeviceIdType.MESH)
 
     def slot(x, y, half):
         return (x * 2 + y) * 2 + half
@@ -714,7 +716,7 @@
                 link(ref, ref, (sl, rq), (place + distance) * cuts + j, "dp", partner, 0).wait_recv()
                 pl.when(goes_left)(lambda: left(distance, j).start())
 
-    def forward(lo, count, features, first, second, third, saved, unit_ref):
+    def forward(lo, count, features, first, second, third, saved, unit_ref, waits=((), (), ())):
         act1, slope1, act2, slope2, emb = saved
         span = slice(lo, lo + count)
 
@@ -727,28 +729,41 @@
                 act[span, c : c + step] = (pre * sigma).astype(bf16)
                 slope[span, c : c + step] = sigma * (1.0 + pre * (1.0 - sigma))
 
+        ready(waits[0])
         layer(features, first, act1, slope1)
+        ready(waits[1])
         layer(act1, second, act2, slope2)
+        ready(waits[2])
         value = jnp.dot(act2[span, :], third[...], preferred_element_type=f32)
         emb[span, :] = value
         inv_norm = lax.rsqrt(jnp.sum(value * value, axis=1, keepdims=True) + 1.0)
         unit_ref[...] = (value * inv_norm).astype(bf16)
 
+    def ready(chosen):
+        for name in chosen:
+            loads[name].wait()
+
     item_weights = tuple(sources[name] for name in ("item_first", "item_second", "item_third"))
     query_weights = tuple(sources[name] for name in ("query_first", "query_second", "query_third"))
-    for name in ("negative_ids", "negative_counts", "positive_ids", "item_first", "negative_features", "item_second", "item_third"):
-        loads[name].wait()
-
     def own_ids(ref, index, count):
         return ref[:, pl.ds(pl.multiple_of(index * count, count), count)]
 
+    forward(
+        0, rows_q, sources["query_features"], *query_weights, towers[0], q_unit,
+        (("query_features", "query_first"), ("query_second",), ("query_third",)),
+    )
+    pl.semaphore_wait(barrier, devices - 1)
+    for j in range(cuts):
+        pl.when(goes_right)(lambda j=j: right(0, j).start())
+        pl.when(goes_left)(lambda j=j: left(0, j).start())
+    for j in range(cuts):
+        q_land[place, j] = q_unit[pl.ds(j * (rows_q // cuts), rows_q // cuts), :]
+    ready(("negative_ids", "negative_counts", "positive_ids"))
     meta_out[0:1, :] = own_ids(sources["negative_ids"], me_dp, block)
     meta_out[1:2, :] = own_ids(sources["negative_counts"], me_dp, block)
     pid_out[...] = own_ids(sources["positive_ids"], me_neg, rows_q)
     meta[here] = meta_out[...]
     pid_land[place] = pid_out[...]
-    forward(0, half_n, item_features, *item_weights, towers[1], n_unit.at[0])
-    pl.semaphore_wait(barrier, 2 * (line - 1) + (blocks - 1))
     for k in range(1, blocks):
         copy = pltpu.make_async_remote_copy(
             src_ref=meta_out, dst_ref=meta.at[here], send_sem=s_meta.at[k], recv_sem=r_meta.at[here],
@@ -759,26 +774,22 @@
         z = lax.rem(place + k, line)
         go(link(pid_out, pid_land.at[place], (s_pid, r_pid), place, "dp", at_place(z), k))
     n_first, n_second = n_unit.at[0], n_unit.at[1]
+    forward(
+        0, half_n, item_features, *item_weights, towers[1], n_first,
+        (("negative_features", "item_first"), ("item_second",), ("item_third",)),
+    )
     to_x(n_first, me_x, side, 0, 0)
-    to_y(n_first, me_x, side, 0, 1)
     go(relay(n_first, me_x, side, 0))
     n_land[here, 0] = n_unit[0]
-    for name in ("query_features", "query_first", "query_second", "query_third"):
-        loads[name].wait()
-    forward(0, rows_q, sources["query_features"], *query_weights, towers[0], q_unit)
-    for j in range(cuts):
-        pl.when(goes_right)(lambda j=j: right(0, j).start())
-        pl.when(goes_left)(lambda j=j: left(0, j).start())
-    for j in range(cuts):
-        q_land[place, j] = q_unit[pl.ds(j * (rows_q // cuts), rows_q // cuts), :]
-    forward(half_n, half_n, item_features, *item_weights, towers[1], n_unit.at[1])
+    forward(half_n, half_n, item_features, *item_weights, towers[1], n_second)
     to_y(n_second, me_x, side, 1, 0)
     to_x(n_second, me_x, side, 1, 1)
+    to_y(n_first, me_x, side, 0, 1)
     go(relay(n_second, me_x, side, 1))
     n_land[here, 1] = n_unit[1]
-    loads["positive_features"].wait()
-    loads["positive_counts"].wait()
+    ready(("positive_features", "positive_counts"))
     forward(block, rows_q, item_features, *item_weights, towers[1], p_unit)
+    q_step(1)
     product = q_unit[...].astype(f32) * p_unit[...].astype(f32)
     logit[...] = jnp.sum(product.T, axis=0, keepdims=True) * inv_temp - jnp.log(sources["positive_counts"][...].astype(f32))
     pexp[...] = jnp.exp(logit[...])
@@ -836,38 +847,35 @@
         lax.fori_loop(jnp.maximum(lo, 0), jnp.minimum(hi, line), body, 0)
 
     relayed(me_x, side)
-    units(place, place + 1, near_blocks)
-    q_step(1)
-    units(place - 1, place, near_blocks)
-    units(place + 1, place + 2, near_blocks)
+    units(place - 1, place + 2, near_blocks)
     landed(me_x, far, 1)
     to_x(piece(me_x, far, 1), me_x, far, 1, 2)
     go(relay(piece(me_x, far, 1), me_x, far, 1))
-    landed(me_x, far, 0)
-    go(relay(piece(me_x, far, 0), me_x, far, 0))
+    q_step(2)
+    units(place - 2, place - 1, near_blocks)
+    units(place + 2, place + 3, near_blocks)
     for k in range(1, nx):
         x = along(k)
         landed(x, side, 1)
         go(relay(piece(x, side, 1), x, side, 1))
-    q_step(2)
-    relayed(me_x, far)
     for k in range(1, nx):
         relayed(along(k), side)
-    units(place - 1, place + 2, mid_blocks)
-    units(place - 2, place - 1, near_blocks + mid_blocks)
-    units(place + 2, place + 3, near_blocks + mid_blocks)
+    landed(me_x, far, 0)
+    go(relay(piece(me_x, far, 0), me_x, far, 0))
+    relayed(me_x, far)
+    units(place - 2, place + 3, mid_blocks)
+    for distance in range(3, line):
+        q_step(distance)
     for half in range(2):
         for k in range(1, nx):
             x = along(k)
             landed(x, far, half)
             go(relay(piece(x, far, half), x, far, half))
-    for distance in range(3, line):
-        q_step(distance)
+    units(0, place - 2, near_blocks + mid_blocks)
+    units(place + 3, line, near_blocks + mid_blocks)
     for k in range(1, nx):
         relayed(along(k), far)
-    units(place - 2, place + 3, far_blocks)
-    units(0, place - 2, near_blocks + mid_blocks + far_blocks)
-    units(place + 3, line, near_blocks + mid_blocks + far_blocks)
+    units(0, line, far_blocks)
     for z in range(line):
         dpart[z] = jnp.sum(den[z].T, axis=0, keepdims=True)
     dpart[place] = dpart[place] + pexp[...]
@@ -953,8 +961,16 @@
 
         return carry
 
-    lax.fori_loop(0, 2 * nx, far_step, 0)
-    lax.fori_loop(0, 2 * nx, own_step, 0)
+    ahead = 2
+
+    def both_steps(i, carry):
+        far_step(i + ahead, 0)
+        own_step(i, 0)
+        return carry
+
+    lax.fori_loop(0, ahead, far_step, 0)
+    lax.fori_loop(0, 2 * nx - ahead, both_steps, 0)
+    lax.fori_loop(2 * nx - ahead, 2 * nx, own_step, 0)
     value = own[me_x, far, 0]
     for k in range(1, nx):
         x = along(k)
@@ -1029,7 +1045,7 @@
             store(group, offset, contract_rows(left, right_ref[...]), 2 * m, hg)
             return carry
 
-        lax.fori_loop(0, rows // step, body, 0)
+        lax.fori_loop(0, rows // step, body, 0, unroll=True)
         return offset + hg // nneg * (columns // pack_columns)
 
     def row_loop(count, body):
@@ -1183,10 +1199,18 @@
             arrived(ref, b["rg"], x)
             queue(link(ref, ref, (b["sh"], b["rh"]), x, "neg", mate))
 
+    leaving = []
+
+    def leave(source, target, index):
+        copy = pltpu.make_async_copy(source, target, left_sems.at[index])
+        copy.start()
+        leaving.append(copy)
+
     def stage6(g):
         b = bufs[g]
         for x in range(nx):
             arrived(b["ag"].at[2 * x + other], b["rh"], x)
+        leave(b["ag"], gathered[g], g)
 
     embed_stage(0)
     second_stage(0, 0)
@@ -1194,6 +1218,7 @@
     slope_stage(0)
     first_stage(0, 1)
     stage0(1)
+    stage1(0)
     n_low = own[me_x, side, 0]
     for k in range(1, nx):
         x = along(k)
@@ -1211,7 +1236,6 @@
 
     grads[1][0:block, 0:half_w] = n_low.T * inv_temp
     grads[1][0:block, half_w:width] = n_high.T * inv_temp
-    stage1(0)
     embed_stage(1)
     stage1(1)
     second_stage(1, 2)
@@ -1224,36 +1248,37 @@
     stage0(3)
     stage3(0)
     stage1(3)
+    stage2(2)
     stage3(1)
-    stage2(2)
-    stage4(0)
     stage2(3)
-    stage4(1)
     stage3(2)
     stage3(3)
-    stage4(2)
-    stage4(3)
+    for g in range(4):
+        stage4(g)
     total_squares = squares[0] + squares[1] + squares[2] + squares[3]
-    lane = lax.broadcasted_iota(jnp.int32, (8, 128), 1)
-    stat_dp[...] = jnp.where(lane == 0, total_squares, loss_part)
-    stat_copies = share("dp", ndp, me_dp, lambda t: stat_dp, stat_dp_land, ss, sr2)
+    lane = lax.broadcasted_iota(jnp.int32, (1, 128), 1)
+    stat[...] = jnp.where(lane == 0, total_squares, loss_part)
+    for n in range(1, devices):
+        dp, neg = everyone(n)
+        copy = pltpu.make_async_remote_copy(
+            src_ref=stat, dst_ref=stat_land.at[me], send_sem=ss.at[n], recv_sem=sr2.at[me],
+            device_id={"dp": dp, "neg": neg}, device_id_type=pl.DeviceIdType.MESH,
+        )
+        queue(copy)
     for g in range(4):
         stage5(g)
-    finish(stat_copies)
-    total = stat_dp[...]
-    for k in range(1, ndp):
-        total = total + stat_dp_land[lax.rem(me_dp + k, ndp)]
-    stat_neg[...] = total
-    stat_copies = share("neg", nneg, me_neg, lambda t: stat_neg, stat_neg_land, ts, tr)
     for g in range(4):
         stage6(g)
-    finish(stat_copies)
-    total = stat_neg[...]
-    for k in range(1, nneg):
-        total = total + stat_neg_land[lax.rem(me_neg + k, nneg)]
-    stats_ref[...] = total
+    stat_land[me] = stat[...]
+    for n in range(1, devices):
+        source = lax.rem(me + n, devices)
+        arrived(stat_land.at[source], sr2, source)
+    stat_land[me] = jnp.sum(stat_land[...], axis=0)
+    leave(stat_land.at[me], stats_ref, 4)
     for copy in pending:
         copy.wait_send()
+    for copy in leaving:
+        copy.wait()
 
 
     for copy in sends:
@@ -1280,7 +1305,7 @@
     fin, h1 = named["item_first"].shape
     h2, width = named["item_third"].shape
     own_rows, block = named["query_features"].shape[0], named["negative_features"].shape[0]
-    blocks, cuts, lanes = 2 * nneg, 2, 128
+    blocks, cuts, lanes = 2 * nneg, 4, 128
     rows_half = (width // 2, block)
     sources = {"item_features": pltpu.VMEM((block + own_rows, fin), bf16)}
     for name, value in named.items():
@@ -1344,7 +1369,7 @@
         shapes = dict(
             packed=(2, ndp, nx, r, c), c_in=(ndp, nx, r, c), o1x=(nx, ndp, r1, c), l1x=(nx, ndp, r1, c),
             o1y=(line, nx, r2, c), l1y=(line, nx, r2, c), o2y=(line, r1, c), l2y=(line, r1, c),
-            o2x=(nx, line, r2, c), l2x=(nx, line, r2, c), zs=(line, r, c), l3=(line, r, c),
+            o2x=(nx, line, r2, c), l2x=(nx, line, r2, c), zs=(line, r, c), l3=(line, r, c), ag=(nneg, r, c),
         )
         buf = {name: pltpu.VMEM(shape, bf16) for name, shape in shapes.items()}
         buf.update(zip(sem_names, sems(1, 1, nx, nx, 1, 1, 1, 1, nx, nx, line, line, nx, nx, nx, nx)))
@@ -1353,20 +1378,35 @@
         sources, pltpu.VMEM((own_rows, width), bf16), pltpu.VMEM((2, block // 2, width), bf16),
         pltpu.VMEM((own_rows, width), bf16), towers, [pltpu.VMEM((count, width), f32) for count in counts], row, row,
         *score, scratch, bufs,
-        pltpu.VMEM((8, 128), f32), pltpu.VMEM((ndp, 8, 128), f32), pltpu.VMEM((8, 128), f32), pltpu.VMEM((nneg, 8, 128), f32),
-        *sems(ndp, ndp, nneg, nneg),
+        pltpu.VMEM((1, 128), f32), pltpu.VMEM((ndp * nneg, 1, 128), f32), *sems(ndp * nneg, ndp * nneg, 5),
     )
     leaves, names = jax.tree.flatten(tree)
+    space = sems(1)[0].memory_space
+    is_flag = [leaf.memory_space == space for leaf in leaves]
+    flags = [leaf for leaf, flag in zip(leaves, is_flag) if flag]
+    kept = [leaf for leaf, flag in zip(leaves, is_flag) if not flag]
+
+    def kernel(*refs):
+        fixed = refs[: len(refs) - len(kept)]
+        held = refs[len(refs) - len(kept) :]
+
+        def scoped(*flag_refs):
+            held_refs, flags_left = iter(held), iter(flag_refs)
+            merged = [next(flags_left) if flag else next(held_refs) for flag in is_flag]
+            step_kernel(ndp, nneg, names, tuple(groups), *fixed, *merged)
+
+        pl.run_scoped(scoped, *flags)
+
     any_space = pl.BlockSpec(memory_space=pl.ANY)
     stats, *gathered = pl.pallas_call(
-        functools.partial(step_kernel, ndp, nneg, names, tuple(groups)),
+        kernel,
         out_shape=(
-            jax.ShapeDtypeStruct((8, 128), f32),
+            jax.ShapeDtypeStruct((1, 128), f32),
             *[jax.ShapeDtypeStruct((nneg, r, pack_columns), bf16) for _, r in groups],
         ),
         in_specs=[any_space] * len(arguments),
-        out_specs=(vmem,) * 5,
-        scratch_shapes=leaves,
+        out_specs=(any_space,) * 5,
+        scratch_shapes=kept,
         compiler_params=pltpu.CompilerParams(
             collective_id=1, has_side_effects=True, vmem_limit_bytes=67043328
         ),
@@ -1374,15 +1414,27 @@
     mean_loss, *clipped = pl.pallas_call(
         functools.partial(finish_kernel, nneg, own_rows * ndp * nneg),
         out_shape=(jax.ShapeDtypeStruct((1,), f32), *outs),
-        in_specs=[vmem] * 5,
+        in_specs=[any_space] * 5,
         out_specs=(pl.BlockSpec(memory_space=pltpu.SMEM), *([any_space] * 6)),
-        scratch_shapes=[pltpu.VMEM(out.shape, f32) for out in outs] + sems(6),
+        scratch_shapes=[pltpu.VMEM((1, 128), f32)]
+        + [pltpu.VMEM((nneg, r, pack_columns), bf16) for _, r in groups]
+        + [pltpu.VMEM(out.shape, f32) for out in outs]
+        + sems(5, 6),
     )(stats, *gathered)
     return (mean_loss.reshape(()), *clipped)
 
 
-def finish_kernel(nneg, count, stats_ref, *refs):
-    gathered, loss_ref, outs, staged, done = refs[:4], refs[4], refs[5:11], refs[11:17], refs[17]
+def finish_kernel(nneg, count, *refs):
+    given, loss_ref, outs, stats_ref, gathered, staged = refs[:5], refs[5], refs[6:12], refs[12], refs[13:17], refs[17:23]
+    loaded, done = refs[23:]
+    loads = [
+        pltpu.make_async_copy(source, target, loaded.at[i])
+        for i, (source, target) in enumerate(zip(given, (stats_ref, *gathered)))
+    ]
+    for copy in loads:
+        copy.start()
+    for copy in loads:
+        copy.wait()
     clip = clip_norm / jnp.maximum(jnp.sqrt(stats_ref[0:1, 0:1]), clip_norm)
     copies = []
     for t in range(2):

time: 84.7 us -> 78.6 us (0.928)
  Pallas kernels: 83.8 us -> 77.6 us
    pallas_call x1, Pallas kernels: 81 us -> 74.8 us  [fused_step(): pl.pallas_call(kernel, out_shape=(jax.ShapeDtypeStruct((1, 128), f32), *[...]
where the time goes in v5:
time: 78.6 us; the launch traced here: 78.4 us
  Pallas kernels  77.6 us (99%)
  between operations  0.81 us (1%)
    pallas_call x1, Pallas kernels, fused_step(): pl.pallas_call(kernel, out_shape=(jax.ShapeDtypeStruct((1, 128), f32), *[...  74.8 us
    pallas_call x1, Pallas kernels, fused_step(): pl.pallas_call(functools.partial(finish_kernel, nneg, own_rows * ndp * nn...  2.85 us

profile of v5, /device:TPU:0, one launch (start us, length us, event | category | flops | bytes accessed | tf_op | source)
XLA Modules:
  0.0 78.4 jit_solution(11393694350487477864)
XLA Ops:
  0.6 74.8 %shard_map.180 = (f32[1,128]{1,0:T(1,128)}, bf16[4,80,256]{2,1,0:T(8,128)(2,1)}, bf16[4,64,256]{2,1,0:T(8,128)(2,1)}, bf16[4,80,256]{2,1,0:T(8,128)(2,1)}, bf16[4,64,256]{2,1,0:T(8,128)(2,1)}) custom-call(bf16[256,512]{1,0:T(8,128)(2,1)} %refs_0_.1, bf16[256,512]{1,0:T(8,128)(2,1)} %refs_1_.1, bf16[512,512]{1,0:T(8,128)(2,1)} %refs_2_.1, s32[1,1024]{1,0:T(1,128)} %bitcast.7, ...), custom_call_target="tpu_custom_call" | custom-call | tf_op jit(solution)/shard_map/pallas_call | solution.py:1401
  75.4 2.9 %shard_map.181 = (f32[1]{0:T(128)}, f32[64,1024]{1,0:T(8,128)}, f32[128,512]{1,0:T(8,128)}, f32[64,256]{1,0:T(8,128)}, f32[64,1024]{1,0:T(8,128)}, /*index=5*/f32[128,512]{1,0:T(8,128)}, f32[64,256]{1,0:T(8,128)}) custom-call(f32[1,128]{1,0:T(1,128)} %get-tuple-element.19.refs_0_, bf16[4,80,256]{2,1,0:T(8,128)(2,1)} %get-tuple-element.20.refs_1_, ...), custom_call_target="tpu_custom_call" | custom-call | tf_op jit(solution)/shard_map/pallas_call | solution.py:1414

commit v6 on v5

--- a/solution.py
+++ b/solution.py
@@ -634,6 +634,7 @@
     loads = {}
     for i, name in enumerate(order):
         loads[name] = pltpu.make_async_copy(inputs[name], places[name], loaded.at[i])
+    for name in order[:4]:
         loads[name].start()
 
     def along(k):
@@ -701,8 +702,8 @@
 
     goes_right, goes_left = place < line - 1, place > 0
 
-    def q_step(distance):
-        for j in range(cuts):
+    def q_step(distance, lo=0, hi=cuts):
+        for j in range(lo, hi):
 
             @pl.when(place >= distance)
             def _():
@@ -716,7 +717,7 @@
                 link(ref, ref, (sl, rq), (place + distance) * cuts + j, "dp", partner, 0).wait_recv()
                 pl.when(goes_left)(lambda: left(distance, j).start())
 
-    def forward(lo, count, features, first, second, third, saved, unit_ref, waits=((), (), ())):
+    def forward(lo, count, features, first, second, third, saved, unit_ref, waits=((), (), ()), starts=()):
         act1, slope1, act2, slope2, emb = saved
         span = slice(lo, lo + count)
 
@@ -730,6 +731,8 @@
                 slope[span, c : c + step] = sigma * (1.0 + pre * (1.0 - sigma))
 
         ready(waits[0])
+        for name in starts:
+            loads[name].start()
         layer(features, first, act1, slope1)
         ready(waits[1])
         layer(act1, second, act2, slope2)
@@ -751,6 +754,7 @@
     forward(
         0, rows_q, sources["query_features"], *query_weights, towers[0], q_unit,
         (("query_features", "query_first"), ("query_second",), ("query_third",)),
+        order[4:],
     )
     pl.semaphore_wait(barrier, devices - 1)
     for j in range(cuts):
@@ -847,11 +851,12 @@
         lax.fori_loop(jnp.maximum(lo, 0), jnp.minimum(hi, line), body, 0)
 
     relayed(me_x, side)
+    q_step(2, 0, cuts // 2)
     units(place - 1, place + 2, near_blocks)
     landed(me_x, far, 1)
     to_x(piece(me_x, far, 1), me_x, far, 1, 2)
     go(relay(piece(me_x, far, 1), me_x, far, 1))
-    q_step(2)
+    q_step(2, cuts // 2)
     units(place - 2, place - 1, near_blocks)
     units(place + 2, place + 3, near_blocks)
     for k in range(1, nx):
@@ -1107,8 +1112,14 @@
         lax.fori_loop(0, count, wrapped, 0)
 
     def stage1(g):
-        b, (r1, r) = bufs[g], groups[g]
+        b, (r1, r, full) = bufs[g], groups[g]
         arrived(b["c_in"], b["cr"], 0)
+        for k in range(1, line):
+            z = z_of(k)
+            for y in range(2):
+                for x in range(nx):
+                    b["o1z"][z, y, x] = base(b, 2 * z + y, x, r, full).astype(bf16)
+            queue(link(b["o1z"].at[z], b["l1z"].at[place], (b["s1z"], b["r1z"]), place, "dp", 2 * z + side, z))
         for k in range(1, nx):
             x = x_of(k)
 
@@ -1132,7 +1143,7 @@
         return value
 
     def stage2(g):
-        b, (r1, r) = bufs[g], groups[g]
+        b, (r1, r, full) = bufs[g], groups[g]
         for k in range(1, nx):
             x = x_of(k)
             arrived(b["l1x"].at[x], b["r1x"], x)
@@ -1154,7 +1165,7 @@
             queue(link(b["o2x"].at[x], b["l2x"].at[me_x], (b["s2x"], b["r2x"]), me_x, "neg", same_core(x), x))
 
     def stage3(g):
-        b, (r1, r) = bufs[g], groups[g]
+        b, (r1, r, full) = bufs[g], groups[g]
         arrived(b["l2y"], b["r2y"], 0)
         for k in range(1, nx):
             x = x_of(k)
@@ -1173,18 +1184,56 @@
             z = z_of(k)
             queue(link(b["zs"].at[z], b["l3"].at[place], (b["s3"], b["r3"]), place, "dp", 2 * z + side, z))
 
+    def z_sum(g, y, x):
+        b, (_, r, full) = bufs[g], groups[g]
+        value = base(b, 2 * place + y, x, r, full)
+        for k in range(1, line):
+            value = value + b["l1z"][z_of(k), y, x].astype(f32)
+        return value
+
+    def x_sum(g, y):
+        value = z_sum(g, y, me_x)
+        for k in range(1, nx):
+            value = value + bufs[g]["l2z"][x_of(k), y].astype(f32)
+        return value
+
+    def stage2z(g):
+        b = bufs[g]
+        for k in range(1, line):
+            z = z_of(k)
+            arrived(b["l1z"].at[z], b["r1z"], z)
+        for k in range(1, nx):
+            x = x_of(k)
+            for y in range(2):
+                b["o2z"][x, y] = z_sum(g, y, x).astype(bf16)
+            queue(link(b["o2z"].at[x], b["l2z"].at[me_x], (b["s2z"], b["r2z"]), me_x, "neg", same_core(x), x))
+
+    def stage3z(g):
+        b = bufs[g]
+        for k in range(1, nx):
+            x = x_of(k)
+            arrived(b["l2z"].at[x], b["r2z"], x)
+        b["o3z"][...] = x_sum(g, far).astype(bf16)
+        queue(link(b["o3z"], b["l3z"], (b["s3z"], b["r3z"]), 0, "dp", partner))
+
     squares = []
 
     def stage4(g):
-        b = bufs[g]
+        b, (_, r, full) = bufs[g], groups[g]
         for k in range(1, line):
             z = z_of(k)
             arrived(b["l3"].at[z], b["r3"], z)
         value = b["zs"][place].astype(f32)
         for k in range(1, line):
             value = value + b["l3"][z_of(k)].astype(f32)
-        squares.append(jnp.sum(value * value))
-        b["ag"][me_neg] = value.astype(bf16)
+        arrived(b["l3z"], b["r3z"], 0)
+        last = x_sum(g, side) + b["l3z"][...].astype(f32)
+        squares.append(jnp.sum(value * value) + jnp.sum(last * last))
+        b["ag"][me_neg, 0:r] = value.astype(bf16)
+        b["ag"][me_neg, r:full] = last.astype(bf16)
+
+    def spread(g):
+        b = bufs[g]
         mine = b["ag"].at[me_neg]
         for k in range(1, nx):
             x = x_of(k)
@@ -1236,24 +1285,35 @@
 
     grads[1][0:block, 0:half_w] = n_low.T * inv_temp
     grads[1][0:block, half_w:width] = n_high.T * inv_temp
+    stage1(1)
     embed_stage(1)
-    stage1(1)
     second_stage(1, 2)
     stage0(2)
+    slope_stage(1)
     stage2(0)
-    slope_stage(1)
     stage1(2)
-    stage2(1)
     first_stage(1, 3)
     stage0(3)
+    stage2(1)
+    stage1(3)
     stage3(0)
-    stage1(3)
+    stage2z(0)
     stage2(2)
+    stage2z(1)
     stage3(1)
+    stage2z(2)
     stage2(3)
+    stage2z(3)
+    stage3z(0)
+    stage3z(1)
     stage3(2)
+    stage3z(2)
     stage3(3)
-    for g in range(4):
+    stage3z(3)
+    for g in range(2):
+        stage4(g)
+        spread(g)
+    for g in range(2, 4):
         stage4(g)
     total_squares = squares[0] + squares[1] + squares[2] + squares[3]
     lane = lax.broadcasted_iota(jnp.int32, (1, 128), 1)
@@ -1265,6 +1325,8 @@
             device_id={"dp": dp, "neg": neg}, device_id_type=pl.DeviceIdType.MESH,
         )
         queue(copy)
+    for g in range(2, 4):
+        spread(g)
     for g in range(4):
         stage5(g)
     for g in range(4):
@@ -1361,18 +1423,22 @@
         both = h2 // (ndp * nneg) * (width // pack_columns) + h1 // (ndp * nneg) * (h2 // pack_columns)
         alone = fin // (ndp * nneg) * (h1 // pack_columns)
         for r in (both, alone):
-            groups.append((max((r * 4 + 72) // 144, 1) * 16, r))
+            spare = r // 16 - 1
+            low = spare // 2 + (spare % 2 if len(groups) == 3 else 0)
+            groups.append((low * 16, spare * 16, r))
     c = pack_columns
     sem_names = ["cs", "cr", "s1x", "r1x", "s1y", "r1y", "s2y", "r2y", "s2x", "r2x", "s3", "r3", "sg", "rg", "sh", "rh"]
-    for r1, r in groups:
-        r2 = r - r1
+    sem_names += ["s1z", "r1z", "s2z", "r2z", "s3z", "r3z"]
+    for r1, r, full in groups:
+        r2, r4 = r - r1, full - r
         shapes = dict(
-            packed=(2, ndp, nx, r, c), c_in=(ndp, nx, r, c), o1x=(nx, ndp, r1, c), l1x=(nx, ndp, r1, c),
+            packed=(2, ndp, nx, full, c), c_in=(ndp, nx, full, c), o1x=(nx, ndp, r1, c), l1x=(nx, ndp, r1, c),
             o1y=(line, nx, r2, c), l1y=(line, nx, r2, c), o2y=(line, r1, c), l2y=(line, r1, c),
-            o2x=(nx, line, r2, c), l2x=(nx, line, r2, c), zs=(line, r, c), l3=(line, r, c), ag=(nneg, r, c),
+            o2x=(nx, line, r2, c), l2x=(nx, line, r2, c), zs=(line, r, c), l3=(line, r, c), ag=(nneg, full, c),
+            o1z=(line, 2, nx, r4, c), l1z=(line, 2, nx, r4, c), o2z=(nx, 2, r4, c), l2z=(nx, 2, r4, c), o3z=(r4, c), l3z=(r4, c),
         )
         buf = {name: pltpu.VMEM(shape, bf16) for name, shape in shapes.items()}
-        buf.update(zip(sem_names, sems(1, 1, nx, nx, 1, 1, 1, 1, nx, nx, line, line, nx, nx, nx, nx)))
+        buf.update(zip(sem_names, sems(1, 1, nx, nx, 1, 1, 1, 1, nx, nx, line, line, nx, nx, nx, nx, line, line, nx, nx, 1, 1)))
         bufs.append(buf)
     tree = (
         sources, pltpu.VMEM((own_rows, width), bf16), pltpu.VMEM((2, block // 2, width), bf16),
@@ -1402,7 +1468,7 @@
         kernel,
         out_shape=(
             jax.ShapeDtypeStruct((1, 128), f32),
-            *[jax.ShapeDtypeStruct((nneg, r, pack_columns), bf16) for _, r in groups],
+            *[jax.ShapeDtypeStruct((nneg, group[-1], pack_columns), bf16) for group in groups],
         ),
         in_specs=[any_space] * len(arguments),
         out_specs=(any_space,) * 5,
@@ -1417,7 +1483,7 @@
         in_specs=[any_space] * 5,
         out_specs=(pl.BlockSpec(memory_space=pltpu.SMEM), *([any_space] * 6)),
         scratch_shapes=[pltpu.VMEM((1, 128), f32)]
-        + [pltpu.VMEM((nneg, r, pack_columns), bf16) for _, r in groups]
+        + [pltpu.VMEM((nneg, group[-1], pack_columns), bf16) for group in groups]
         + [pltpu.VMEM(out.shape, f32) for out in outs]
         + sems(5, 6),
     )(stats, *gathered)

time: 78.6 us -> 73.7 us (0.938)
  Pallas kernels: 77.6 us -> 72.7 us
    pallas_call x1, Pallas kernels: 74.8 us -> 69.9 us  [fused_step(): pl.pallas_call(kernel, out_shape=(jax.ShapeDtypeStruct((1, 128), f32), *[...]
where the time goes in v6:
time: 73.7 us; the launch traced here: 73.5 us
  Pallas kernels  72.7 us (99%)
  between operations  0.81 us (1%)
    pallas_call x1, Pallas kernels, fused_step(): pl.pallas_call(kernel, out_shape=(jax.ShapeDtypeStruct((1, 128), f32), *[...  69.9 us
    pallas_call x1, Pallas kernels, fused_step(): pl.pallas_call(functools.partial(finish_kernel, nneg, own_rows * ndp * nn...  2.85 us

profile of v6, /device:TPU:0, one launch (start us, length us, event | category | flops | bytes accessed | tf_op | source)
XLA Modules:
  0.0 73.5 jit_solution(118384074912622559)
XLA Ops:
  0.6 69.9 %shard_map.180 = (f32[1,128]{1,0:T(1,128)}, bf16[4,80,256]{2,1,0:T(8,128)(2,1)}, bf16[4,64,256]{2,1,0:T(8,128)(2,1)}, bf16[4,80,256]{2,1,0:T(8,128)(2,1)}, bf16[4,64,256]{2,1,0:T(8,128)(2,1)}) custom-call(bf16[256,512]{1,0:T(8,128)(2,1)} %refs_0_.1, bf16[256,512]{1,0:T(8,128)(2,1)} %refs_1_.1, bf16[512,512]{1,0:T(8,128)(2,1)} %refs_2_.1, s32[1,1024]{1,0:T(1,128)} %bitcast.7, ...), custom_call_target="tpu_custom_call" | custom-call | tf_op jit(solution)/shard_map/pallas_call | solution.py:1467
  70.5 2.9 %shard_map.181 = (f32[1]{0:T(128)}, f32[64,1024]{1,0:T(8,128)}, f32[128,512]{1,0:T(8,128)}, f32[64,256]{1,0:T(8,128)}, f32[64,1024]{1,0:T(8,128)}, /*index=5*/f32[128,512]{1,0:T(8,128)}, f32[64,256]{1,0:T(8,128)}) custom-call(f32[1,128]{1,0:T(1,128)} %get-tuple-element.19.refs_0_, bf16[4,80,256]{2,1,0:T(8,128)(2,1)} %get-tuple-element.20.refs_1_, ...), custom_call_target="tpu_custom_call" | custom-call | tf_op jit(solution)/shard_map/pallas_call | solution.py:1480

commit v7 on v6

--- a/solution.py
+++ b/solution.py
@@ -726,9 +726,10 @@
             step = 512 if columns % 512 == 0 else columns
             for c in range(0, columns, step):
                 pre = jnp.dot(source[span, :], weight[:, c : c + step], preferred_element_type=f32)
-                sigma = jax.nn.sigmoid(pre)
-                act[span, c : c + step] = (pre * sigma).astype(bf16)
-                slope[span, c : c + step] = sigma * (1.0 + pre * (1.0 - sigma))
+                sigma = 0.5 * jnp.tanh(0.5 * pre) + 0.5
+                value = pre * sigma
+                act[span, c : c + step] = value.astype(bf16)
+                slope[span, c : c + step] = sigma + value * (1.0 - sigma)
 
         ready(waits[0])
         for name in starts:
@@ -836,11 +837,11 @@
         return [(x * 2 + y) * 2 + core for core in range(2)]
 
     near_blocks = both_cores(me_x, side)
-    mid_blocks = both_cores(me_x, far)
-    far_blocks = []
+    side_blocks = both_cores(me_x, far)
+    along_blocks = []
     for k in range(1, nx):
-        mid_blocks = mid_blocks + both_cores(along(k), side)
-        far_blocks = far_blocks + both_cores(along(k), far)
+        along_blocks = along_blocks + both_cores(along(k), side)
+    mid_blocks = along_blocks + side_blocks
 
     def units(lo, hi, chosen):
         def body(z, carry):
@@ -863,24 +864,29 @@
         x = along(k)
         landed(x, side, 1)
         go(relay(piece(x, side, 1), x, side, 1))
+    landed(me_x, far, 0)
+    go(relay(piece(me_x, far, 0), me_x, far, 0))
     for k in range(1, nx):
         relayed(along(k), side)
-    landed(me_x, far, 0)
-    go(relay(piece(me_x, far, 0), me_x, far, 0))
+    units(place - 2, place + 3, along_blocks)
     relayed(me_x, far)
-    units(place - 2, place + 3, mid_blocks)
-    for distance in range(3, line):
-        q_step(distance)
+    units(place - 2, place, side_blocks)
     for half in range(2):
         for k in range(1, nx):
             x = along(k)
             landed(x, far, half)
             go(relay(piece(x, far, half), x, far, half))
+    units(place, place + 3, side_blocks)
+    for distance in range(3, line):
+        q_step(distance)
     units(0, place - 2, near_blocks + mid_blocks)
     units(place + 3, line, near_blocks + mid_blocks)
-    for k in range(1, nx):
-        relayed(along(k), far)
-    units(0, line, far_blocks)
+    for core in (me_core, other):
+        for k in range(1, nx):
+            if core is other:
+                relayed(along(k), far)
+            for z in range(line):
+                unit((along(k) * 2 + far) * 2 + core, z)
     for z in range(line):
         dpart[z] = jnp.sum(den[z].T, axis=0, keepdims=True)
     dpart[place] = dpart[place] + pexp[...]
@@ -1053,16 +1059,14 @@
         lax.fori_loop(0, rows // step, body, 0, unroll=True)
         return offset + hg // nneg * (columns // pack_columns)
 
-    def row_loop(count, body):
-        step = 256 if count % 256 == 0 else count
-
+    def row_loop(start, stop, body):
         def wrapped(i, carry):
-            body(pl.ds(pl.multiple_of(i * step, step), step))
+            body(pl.ds(pl.multiple_of(i * 256, 256), 256))
             return carry
 
-        lax.fori_loop(0, count // step, wrapped, 0)
-
-    def embed_stage(t):
+        lax.fori_loop(start // 256, stop // 256, wrapped, 0)
+
+    def embed_stage(t, start, stop):
         feat, act1, slope1, act2, slope2, emb_ref, grad_ref, second, third = steps[t]
         eg, s2, s1 = scratch[t]
 
@@ -1074,7 +1078,7 @@
             eg[rows, :] = value
             s2[rows, :] = (contract_cols(value, third[...]) * slope2[rows, :]).astype(bf16)
 
-        row_loop(feat.shape[0], body)
+        row_loop(start, stop, body)
 
     def second_stage(t, group):
         feat, act1, slope1, act2, slope2, emb_ref, grad_ref, second, third = steps[t]
@@ -1082,7 +1086,7 @@
         offset = weight_grad(group, 0, act2, eg)
         weight_grad(group, offset, act1, s2)
 
-    def slope_stage(t):
+    def slope_stage(t, start, stop):
         feat, act1, slope1, act2, slope2, emb_ref, grad_ref, second, third = steps[t]
         eg, s2, s1 = scratch[t]
         columns = second.shape[0]
@@ -1092,7 +1096,7 @@
                 value = contract_cols(s2[rows, :], second[c : c + 512, :]) * slope1[rows, c : c + 512]
                 s1[rows, c : c + 512] = value.astype(bf16)
 
-        row_loop(feat.shape[0], body)
+        row_loop(start, stop, body)
 
     def first_stage(t, group):
         weight_grad(group, 0, steps[t][0], scratch[t][2])
@@ -1261,13 +1265,16 @@
             arrived(b["ag"].at[2 * x + other], b["rh"], x)
         leave(b["ag"], gathered[g], g)
 
-    embed_stage(0)
+    embed_stage(0, 0, rows_q)
     second_stage(0, 0)
     stage0(0)
-    slope_stage(0)
+    slope_stage(0, 0, rows_q)
     first_stage(0, 1)
     stage0(1)
     stage1(0)
+    embed_stage(1, block, block + rows_q)
+    slope_stage(1, block, block + rows_q)
+    stage1(1)
     n_low = own[me_x, side, 0]
     for k in range(1, nx):
         x = along(k)
@@ -1285,11 +1292,10 @@
 
     grads[1][0:block, 0:half_w] = n_low.T * inv_temp
     grads[1][0:block, half_w:width] = n_high.T * inv_temp
-    stage1(1)
-    embed_stage(1)
+    embed_stage(1, 0, block)
     second_stage(1, 2)
     stage0(2)
-    slope_stage(1)
+    slope_stage(1, 0, block)
     stage2(0)
     stage1(2)
     first_stage(1, 3)
@@ -1303,18 +1309,17 @@
     stage3(1)
     stage2z(2)
     stage2(3)
+    stage3(2)
+    stage3z(0)
     stage2z(3)
-    stage3z(0)
     stage3z(1)
-    stage3(2)
+    stage3(3)
     stage3z(2)
-    stage3(3)
     stage3z(3)
-    for g in range(2):
+    for g in range(3):
         stage4(g)
         spread(g)
-    for g in range(2, 4):
-        stage4(g)
+    stage4(3)
     total_squares = squares[0] + squares[1] + squares[2] + squares[3]
     lane = lax.broadcasted_iota(jnp.int32, (1, 128), 1)
     stat[...] = jnp.where(lane == 0, total_squares, loss_part)
@@ -1325,8 +1330,7 @@
             device_id={"dp": dp, "neg": neg}, device_id_type=pl.DeviceIdType.MESH,
         )
         queue(copy)
-    for g in range(2, 4):
-        spread(g)
+    spread(3)
     for g in range(4):
         stage5(g)
     for g in range(4):
@@ -1499,12 +1503,13 @@
     ]
     for copy in loads:
         copy.start()
-    for copy in loads:
-        copy.wait()
+    loads[0].wait()
     clip = clip_norm / jnp.maximum(jnp.sqrt(stats_ref[0:1, 0:1]), clip_norm)
     copies = []
     for t in range(2):
         third_ref, second_ref, first_ref = staged[3 * t + 2], staged[3 * t + 1], staged[3 * t]
+        loads[2 * t + 1].wait()
+        loads[2 * t + 2].wait()
         for index, group, ref, offset in (
             (3 * t + 1, 2 * t, second_ref, third_ref.shape[0] // nneg),
             (3 * t, 2 * t + 1, first_ref, 0),

time: 73.7 us -> 71.8 us (0.974)
  Pallas kernels: 72.7 us -> 70.9 us
    pallas_call x1, Pallas kernels: 69.9 us -> 68.2 us  [fused_step(): pl.pallas_call(kernel, out_shape=(jax.ShapeDtypeStruct((1, 128), f32), *[...]
where the time goes in v7:
time: 71.8 us; the launch traced here: 71.7 us
  Pallas kernels  70.9 us (99%)
  between operations  0.81 us (1%)
    pallas_call x1, Pallas kernels, fused_step(): pl.pallas_call(kernel, out_shape=(jax.ShapeDtypeStruct((1, 128), f32), *[...  68.2 us
    pallas_call x1, Pallas kernels, fused_step(): pl.pallas_call(functools.partial(finish_kernel, nneg, own_rows * ndp * nn...  2.68 us

profile of v7, /device:TPU:0, one launch (start us, length us, event | category | flops | bytes accessed | tf_op | source)
XLA Modules:
  0.0 71.7 jit_solution(3635842668527672011)
XLA Ops:
  0.6 68.2 %shard_map.180 = (f32[1,128]{1,0:T(1,128)}, bf16[4,80,256]{2,1,0:T(8,128)(2,1)}, bf16[4,64,256]{2,1,0:T(8,128)(2,1)}, bf16[4,80,256]{2,1,0:T(8,128)(2,1)}, bf16[4,64,256]{2,1,0:T(8,128)(2,1)}) custom-call(bf16[256,512]{1,0:T(8,128)(2,1)} %refs_0_.1, bf16[256,512]{1,0:T(8,128)(2,1)} %refs_1_.1, bf16[512,512]{1,0:T(8,128)(2,1)} %refs_2_.1, s32[1,1024]{1,0:T(1,128)} %bitcast.7, ...), custom_call_target="tpu_custom_call" | custom-call | tf_op jit(solution)/shard_map/pallas_call | solution.py:1471
  68.8 2.7 %shard_map.181 = (f32[1]{0:T(128)}, f32[64,1024]{1,0:T(8,128)}, f32[128,512]{1,0:T(8,128)}, f32[64,256]{1,0:T(8,128)}, f32[64,1024]{1,0:T(8,128)}, /*index=5*/f32[128,512]{1,0:T(8,128)}, f32[64,256]{1,0:T(8,128)}) custom-call(f32[1,128]{1,0:T(1,128)} %get-tuple-element.19.refs_0_, bf16[4,80,256]{2,1,0:T(8,128)(2,1)} %get-tuple-element.20.refs_1_, ...), custom_call_target="tpu_custom_call" | custom-call | tf_op jit(solution)/shard_map/pallas_call | solution.py:1484

commit v8 on v7

--- a/solution.py
+++ b/solution.py
@@ -723,7 +723,7 @@
 
         def layer(source, weight, act, slope):
             columns = weight.shape[1]
-            step = 512 if columns % 512 == 0 else columns
+            step = 256 if columns % 256 == 0 else columns
             for c in range(0, columns, step):
                 pre = jnp.dot(source[span, :], weight[:, c : c + step], preferred_element_type=f32)
                 sigma = 0.5 * jnp.tanh(0.5 * pre) + 0.5
@@ -1113,7 +1113,7 @@
             body(i)
             return carry
 
-        lax.fori_loop(0, count, wrapped, 0)
+        lax.fori_loop(0, count, wrapped, 0, unroll=True)
 
     def stage1(g):
         b, (r1, r, full) = bufs[g], groups[g]

time: 71.8 us -> 71.6 us (level)
  no operation moved by 1% of the time
where the time goes in v8:
time: 71.6 us; the launch traced here: 71.5 us
  Pallas kernels  70.7 us (99%)
  between operations  0.81 us (1%)
    pallas_call x1, Pallas kernels, fused_step(): pl.pallas_call(kernel, out_shape=(jax.ShapeDtypeStruct((1, 128), f32), *[...  68 us
    pallas_call x1, Pallas kernels, fused_step(): pl.pallas_call(functools.partial(finish_kernel, nneg, own_rows * ndp * nn...  2.68 us

profile of v8, /device:TPU:0, one launch (start us, length us, event | category | flops | bytes accessed | tf_op | source)
XLA Modules:
  0.0 71.5 jit_solution(4538402816419478610)
XLA Ops:
  0.6 68.0 %shard_map.180 = (f32[1,128]{1,0:T(1,128)}, bf16[4,80,256]{2,1,0:T(8,128)(2,1)}, bf16[4,64,256]{2,1,0:T(8,128)(2,1)}, bf16[4,80,256]{2,1,0:T(8,128)(2,1)}, bf16[4,64,256]{2,1,0:T(8,128)(2,1)}) custom-call(bf16[256,512]{1,0:T(8,128)(2,1)} %refs_0_.1, bf16[256,512]{1,0:T(8,128)(2,1)} %refs_1_.1, bf16[512,512]{1,0:T(8,128)(2,1)} %refs_2_.1, s32[1,1024]{1,0:T(1,128)} %bitcast.7, ...), custom_call_target="tpu_custom_call" | custom-call | tf_op jit(solution)/shard_map/pallas_call | solution.py:1471
  68.6 2.7 %shard_map.181 = (f32[1]{0:T(128)}, f32[64,1024]{1,0:T(8,128)}, f32[128,512]{1,0:T(8,128)}, f32[64,256]{1,0:T(8,128)}, f32[64,1024]{1,0:T(8,128)}, /*index=5*/f32[128,512]{1,0:T(8,128)}, f32[64,256]{1,0:T(8,128)}) custom-call(f32[1,128]{1,0:T(1,128)} %get-tuple-element.19.refs_0_, bf16[4,80,256]{2,1,0:T(8,128)(2,1)} %get-tuple-element.20.refs_1_, ...), custom_call_target="tpu_custom_call" | custom-call | tf_op jit(solution)/shard_map/pallas_call | solution.py:1484
